TPU v7x, 32 devices: a whole 2x2x4 slice. The times are simulated.
32 devices in a mesh: blk: 8 (over y, x, core), rep: 4 (over z).
Axes of the slice: x: 2, y: 2, z: 4, core: 2. Of those that a mesh axis runs over, the one named last changes fastest.
Arguments:
- image: bfloat16 [4096, 1024], P(('blk', 'rep')), may hold values from -100 to 100
- text: bfloat16 [4096, 1024], P(('blk', 'rep')), may hold values from -100 to 100
- positive: int32 [8, 512], P('blk', 'rep'), may hold values from 0 to 511, each once within a row
- logit_scale: float32 [1], replicated, may hold values from 85 to 270
Outputs:
- row_loss: float32 [4096], P(('blk', 'rep'))
- col_loss: float32 [4096], P(('blk', 'rep'))
- img_grad: float32 [4096, 1024], P(('blk', 'rep'))
- txt_grad: float32 [4096, 1024], P(('blk', 'rep'))
Inputs may be any that keep to these rules, and one draw needn't show every extreme that they name: Each row of positive names every index of its block once.
All inputs are finite; a program needn't handle non-finite values.
Results may differ from a plain program's by a relative error of at most 0.0081.
The roundings to bfloat16 on the way count: a program that leaves them out, or rounds other values in their place, can miss the bound.
Values may be sent and summed in bfloat16 or wider, within the bound.
No kernel may reach another device: no remote copies, remote signals or barrier semaphores. Data moves between devices by JAX's collectives and lax.ppermute only.
A program may use at most 64 MiB of HBM per device.

v0:
```python
import jax
import jax.numpy as jnp
from jax import lax
from jax.sharding import PartitionSpec as P

STEPS = 4


def passed_along(array, axis, by):
    count = lax.axis_size(axis)
    return lax.ppermute(array, axis, [(i, (i + by) % count) for i in range(count)])


def combined_all(part, axis, combine):
    gathered = jax.tree.map(lambda a: lax.all_gather(a, axis), part)

    def take(source):
        return jax.tree.map(lambda a: lax.dynamic_index_in_dim(a, source, 0, False), gathered)

    return lax.fori_loop(
        1, lax.axis_size(axis), lambda source, state: combine(state, take(source)), take(0)
    )


def normalize(values):
    widened = values.astype(jnp.float32)
    inverse = lax.rsqrt(jnp.sum(widened * widened, axis=-1, keepdims=True) + 1e-06)
    return (widened * inverse, inverse)


def combine_stats(earlier, later):
    highest = jnp.maximum(earlier[0], later[0])
    summed = earlier[1] * jnp.exp(earlier[0] - highest) + later[1] * jnp.exp(later[0] - highest)
    return (highest, summed, earlier[2] + later[2])


def tile_scores(img_part, text_tile, factor):
    return factor * jnp.einsum("id,jd->ij", img_part, text_tile, preferred_element_type=jnp.float32)


def tile_weights(img_part, text_tile, factor, row_lse, col_lse, onehot):
    scores = tile_scores(img_part, text_tile, factor)
    weight = 0.5 * (jnp.exp(scores - row_lse[:, None]) + jnp.exp(scores - col_lse[None, :]))
    if onehot is not None:
        weight = weight - onehot
    return weight.astype(jnp.bfloat16)


def on_device(image, text, positive, logit_scale):
    factor = logit_scale[0]
    row_count = image.shape[0]
    width = image.shape[1]
    quarter = lax.axis_index("rep")
    img_unit, img_inverse = normalize(image)
    txt_unit, txt_inverse = normalize(text)
    img_tile = img_unit.astype(jnp.bfloat16)
    txt_own = txt_unit.astype(jnp.bfloat16)
    home_tile = lax.all_gather(txt_own, "rep", axis=0, tiled=True)
    block_rows = home_tile.shape[0]
    columns = lax.broadcasted_iota(jnp.int32, (row_count, block_rows), 1)
    onehot = (positive[0][:, None] == columns).astype(jnp.float32)
    kept = []
    moving = img_tile
    for loop_step in range(STEPS):
        if loop_step > 0:
            moving = passed_along(moving, "blk", -1)
            row_max, row_sum = passed_along((row_max, row_sum), "blk", -1)
        kept.append(moving)
        scores = tile_scores(moving, home_tile, factor)
        row_peak = jnp.max(scores, axis=1)
        col_peak = jnp.max(scores, axis=0)
        col_part = jnp.sum(jnp.exp(scores - col_peak[None, :]), axis=0)
        if loop_step == 0:
            row_max = row_peak
            row_sum = jnp.sum(jnp.exp(scores - row_peak[:, None]), axis=1)
            row_pos = jnp.sum(onehot * scores, axis=1)
            col_max, col_sum, col_pos = (col_peak, col_part, jnp.sum(onehot * scores, axis=0))
        else:
            highest = jnp.maximum(row_max, row_peak)
            row_sum = row_sum * jnp.exp(row_max - highest) + jnp.sum(
                jnp.exp(scores - highest[:, None]), axis=1
            )
            row_max = highest
            col_max, col_sum, col_pos = combine_stats(
                (col_max, col_sum, col_pos), (col_peak, col_part, jnp.zeros_like(col_peak))
            )
    col_max, col_sum, col_pos = combined_all((col_max, col_sum, col_pos), "rep", combine_stats)
    col_lse = col_max + jnp.log(col_sum)
    row_lse = row_max + jnp.log(row_sum)
    travel = (row_lse, jnp.zeros((row_count, width), jnp.float32))
    text_terms = jnp.zeros((block_rows, width), jnp.float32)
    for loop_step in range(STEPS - 1, -1, -1):
        if loop_step < STEPS - 1:
            travel = passed_along((travel[0], travel[1]), "blk", 1)
        tile = kept[loop_step]
        weight = tile_weights(
            tile, home_tile, factor, travel[0], col_lse, onehot if loop_step == 0 else None
        )
        travel = (
            travel[0],
            travel[1] + jnp.dot(weight, home_tile, preferred_element_type=jnp.float32),
        )
        text_terms = text_terms + jnp.einsum(
            "ij,id->jd", weight, tile, preferred_element_type=jnp.float32
        )
    row_lse, img_acc = travel
    col_lse_home, col_pos_home = (col_lse, col_pos)
    row_loss = row_lse - row_pos
    text_share = lax.psum_scatter(text_terms, "rep", scatter_dimension=0, tiled=True)
    img_sum = factor * img_acc
    txt_sum = factor * text_share
    img_grad = (
        img_sum - img_unit * jnp.sum(img_unit * img_sum, axis=-1, keepdims=True)
    ) * img_inverse
    txt_grad = (
        txt_sum - txt_unit * jnp.sum(txt_unit * txt_sum, axis=-1, keepdims=True)
    ) * txt_inverse
    col_whole = col_lse_home - col_pos_home
    col_loss = lax.dynamic_slice_in_dim(col_whole, quarter * row_count, row_count)
    return (row_loss, col_loss, img_grad, txt_grad)


def solution(mesh):
    placed = (P(("blk", "rep"), None), P(("blk", "rep"), None), P("blk", "rep"), P())
    return jax.shard_map(
        on_device,
        mesh=mesh,
        in_specs=placed,
        out_specs=(
            P(("blk", "rep")),
            P(("blk", "rep")),
            P(("blk", "rep"), None),
            P(("blk", "rep"), None),
        ),
        check_vma=False,
    )
```

profile of v0, /device:TPU:0, one launch (start us, length us, event | category | flops | bytes accessed | tf_op | source)
XLA Modules:
  0.0 154.7 jit_solution(10748212426085432188)
XLA Ops:
  7.2 1.1 fusion.13
  8.3 1.8 %fusion.2 = bf16[128,1024]{1,0:T(8,128)(2,1)} fusion(bf16[128,1024]{1,0:T(8,128)(2,1)} %param.7, f32[128]{0:T(128)S(1)} %add_rsqrt_fusion), kind=kLoop, calls=%fused_computation.14 | loop fusion | flops 393216 | bytes 524800 | tf_op jit(solution)/shard_map/convert_element_type | solution.py:57
  10.2 1.1 fusion.9
  11.2 1.1 fusion.5
  12.3 3.4 %collective-permute-start.1 = (bf16[128,1024]{1,0:T(8,128)(2,1)S(1)}, bf16[128,1024]{1,0:T(8,128)(2,1)S(1)}, u32[]{:S(2)}, u32[]{:S(2)}) collective-permute-start(bf16[128,1024]{1,0:T(8,128)(2,1)S(1)} %fusion.5), channel_id=1, source_target_pairs={{0,28},{4,0},{8,4},{12,8},{16,12},{20,16},{24,20},{28,24},{1,29},{... | collective-permute-start | bytes 786440 | tf_op jit(solution)/shard_map/ppermute | solution.py:11
  15.7 3.9 %collective-permute-done.1 = bf16[128,1024]{1,0:T(8,128)(2,1)S(1)} collective-permute-done((bf16[128,1024]{1,0:T(8,128)(2,1)S(1)}, bf16[128,1024]{1,0:T(8,128)(2,1)S(1)}, u32[]{:S(2)}, u32[]{:S(2)}) %collective-permute-start.1) | collective-permute-done | bytes 262176 | tf_op jit(solution)/shard_map/ppermute | solution.py:11
  19.6 2.8 %collective-permute-start.3 = (bf16[128,1024]{1,0:T(8,128)(2,1)S(1)}, bf16[128,1024]{1,0:T(8,128)(2,1)S(1)}, u32[]{:S(2)}, u32[]{:S(2)}) collective-permute-start(bf16[128,1024]{1,0:T(8,128)(2,1)S(1)} %collective-permute-done.1), channel_id=1, source_target_pairs={{0,28},{4,0},{8,4},{12,8},{16,12},{20,16},{24,20},{28,24},{1,29},{... | collective-permute-start | bytes 786440 | tf_op jit(solution)/shard_map/ppermute | solution.py:11
  23.1 3.2 %collective-permute-done.3 = bf16[128,1024]{1,0:T(8,128)(2,1)S(1)} collective-permute-done((bf16[128,1024]{1,0:T(8,128)(2,1)S(1)}, bf16[128,1024]{1,0:T(8,128)(2,1)S(1)}, u32[]{:S(2)}, u32[]{:S(2)}) %collective-permute-start.3) | collective-permute-done | bytes 262176 | tf_op jit(solution)/shard_map/ppermute | solution.py:11
  26.3 3.2 %collective-permute-start.5 = (bf16[128,1024]{1,0:T(8,128)(2,1)S(1)}, bf16[128,1024]{1,0:T(8,128)(2,1)S(1)}, u32[]{:S(2)}, u32[]{:S(2)}) collective-permute-start(bf16[128,1024]{1,0:T(8,128)(2,1)S(1)} %collective-permute-done.3), channel_id=1, source_target_pairs={{0,28},{4,0},{8,4},{12,8},{16,12},{20,16},{24,20},{28,24},{1,29},{... | collective-permute-start | bytes 786440 | tf_op jit(solution)/shard_map/ppermute | solution.py:11
  29.5 11.4 %all-gather.6.cloned.1.call-done = bf16[512,1024]{1,0:T(8,128)(2,1)} async-done(((bf16[128,1024]{1,0:T(8,128)(2,1)}), bf16[512,1024]{1,0:T(8,128)(2,1)}) %all-gather.6.cloned.1.call-update) | async-done | bytes 1048592 | tf_op jit(solution)/shard_map/all_gather | solution.py:58
  41.0 1.9 %fusion.25 = (f32[512]{0:T(512)S(1)}, f32[128]{0:T(128)S(1)}, f32[128,512]{1,0:T(8,128)S(1)}) fusion(bf16[128,1024]{1,0:T(8,128)(2,1)S(1)} %fusion.5, bf16[512,1024]{1,0:T(8,128)(2,1)} %all-gather.6.cloned.1.call-done, f32[]{:T(128)} %bitcast.52), kind=kOutput, calls=%fused_computation.64 | convolution fusion | flops 134413696 | bytes 1575428 | tf_op jit(solution)/shard_map/id,jd->ij/dot_general | solution.py:38
  43.1 11.9 %all-gather.3 = f32[4,1,512]{2,1,0:T(1,128)S(1)} all-gather(f32[1,1,512]{2,1,0:T(1,128)S(1)} %bitcast.77), channel_id=2, replica_groups=mesh['blk'=8,'rep'=4] {'rep'}, dimensions={0}, use_global_device_ids=true | all-gather | bytes 10240 | tf_op jit(solution)/shard_map/all_gather | solution.py:15
  55.1 2.5 %collective-permute-start.6 = (f32[128]{0:T(128)S(1)}, f32[128]{0:T(128)S(1)}, u32[]{:S(2)}, u32[]{:S(2)}) collective-permute-start(f32[128]{0:T(128)S(1)} %get-tuple-element.188), channel_id=1, source_target_pairs={{0,28},{4,0},{8,4},{12,8},{16,12},{20,16},{24,20},{28,24},{1,29},{... | collective-permute-start | bytes 1544 | tf_op jit(solution)/shard_map/ppermute | solution.py:11
  58.1 0.6 fusion.26
  59.6 1.8 %collective-permute-start.7 = (f32[128]{0:T(128)S(1)}, f32[128]{0:T(128)S(1)}, u32[]{:S(2)}, u32[]{:S(2)}) collective-permute-start(f32[128]{0:T(128)S(1)} %multiply_add_fusion.2), channel_id=1, source_target_pairs={{0,28},{4,0},{8,4},{12,8},{16,12},{20,16},{24,20},{28,24},{1,29},{... | collective-permute-start | bytes 1544 | tf_op jit(solution)/shard_map/ppermute | solution.py:11
  61.5 1.8 %collective-permute-start.4 = (f32[128]{0:T(128)S(1)}, f32[128]{0:T(128)S(1)}, u32[]{:S(2)}, u32[]{:S(2)}) collective-permute-start(f32[128]{0:T(128)S(1)} %max.62), channel_id=1, source_target_pairs={{0,28},{4,0},{8,4},{12,8},{16,12},{20,16},{24,20},{28,24},{1,29},{... | collective-permute-start | bytes 1544 | tf_op jit(solution)/shard_map/ppermute | solution.py:11
  63.5 1.8 %collective-permute-start.8 = (f32[128]{0:T(128)S(1)}, f32[128]{0:T(128)S(1)}, u32[]{:S(2)}, u32[]{:S(2)}) collective-permute-start(f32[128]{0:T(128)S(1)} %multiply_add_fusion.1), channel_id=1, source_target_pairs={{0,28},{4,0},{8,4},{12,8},{16,12},{20,16},{24,20},{28,24},{1,29},{... | collective-permute-start | bytes 1544 | tf_op jit(solution)/shard_map/ppermute | solution.py:11
  65.6 11.9 %all-gather.2 = f32[4,1,512]{2,1,0:T(1,128)S(1)} all-gather(f32[1,1,512]{2,1,0:T(1,128)S(1)} %get-tuple-element.223), channel_id=1, replica_groups=mesh['blk'=8,'rep'=4] {'rep'}, dimensions={0}, use_global_device_ids=true | all-gather | bytes 10240 | tf_op jit(solution)/shard_map/all_gather | solution.py:15
  77.6 11.9 %all-gather.1 = f32[4,1,512]{2,1,0:T(1,128)S(1)} all-gather(f32[1,1,512]{2,1,0:T(1,128)S(1)} %get-tuple-element.224), channel_id=1, replica_groups=mesh['blk'=8,'rep'=4] {'rep'}, dimensions={0}, use_global_device_ids=true | all-gather | bytes 10240 | tf_op jit(solution)/shard_map/all_gather | solution.py:15
  89.9 3.9 %collective-permute-done.9 = f32[128]{0:T(128)S(1)} collective-permute-done((f32[128]{0:T(128)S(1)}, f32[128]{0:T(128)S(1)}, u32[]{:S(2)}, u32[]{:S(2)}) %collective-permute-start.9) | collective-permute-done | bytes 544 | tf_op jit(solution)/shard_map/ppermute | solution.py:11
  94.3 3.4 %collective-permute-done.10 = f32[128]{0:T(128)S(1)} collective-permute-done((f32[128]{0:T(128)S(1)}, f32[128]{0:T(128)S(1)}, u32[]{:S(2)}, u32[]{:S(2)}) %collective-permute-start.10) | collective-permute-done | bytes 544 | tf_op jit(solution)/shard_map/ppermute | solution.py:11
  98.2 3.3 %collective-permute-done.11 = f32[128]{0:T(128)S(1)} collective-permute-done((f32[128]{0:T(128)S(1)}, f32[128]{0:T(128)S(1)}, u32[]{:S(2)}, u32[]{:S(2)}) %collective-permute-start.11) | collective-permute-done | bytes 544 | tf_op jit(solution)/shard_map/ppermute | solution.py:11
  101.5 0.6 fusion.22
  102.1 1.9 %add_add_fusion = f32[512,1024]{1,0:T(8,128)} fusion(f32[512,1024]{1,0:T(8,128)S(1)} %fusion.22, f32[512,1024]{1,0:T(8,128)S(1)} %fusion.19, f32[512,1024]{1,0:T(8,128)S(1)} %fusion.18, bf16[128,1024]{1,0:T(8,128)(2,1)S(1)} %collective-permute-done.5, f32[128,512]{1,0:T(8,128)S(1)} %get-tuple-element.228, f32[512]{0:T(512)S(1)} %get-tuple-element.220, ...), kind=kOutput, calls=%fused_computation.4 | convolution fusion | flops 136118272 | bytes 8915456 | tf_op jit(solution)/shard_map/ij,id->jd/dot_general | solution.py:103
  104.5 9.5 %collective-permute-done.12 = f32[128,1024]{1,0:T(8,128)S(1)} collective-permute-done((f32[128,1024]{1,0:T(8,128)S(1)}, f32[128,1024]{1,0:T(8,128)S(1)}, u32[]{:S(2)}, u32[]{:S(2)}) %collective-permute-start.12) | collective-permute-done | bytes 524320 | tf_op jit(solution)/shard_map/ppermute | solution.py:11
  114.4 9.5 %collective-permute-done.13 = f32[128,1024]{1,0:T(8,128)S(1)} collective-permute-done((f32[128,1024]{1,0:T(8,128)S(1)}, f32[128,1024]{1,0:T(8,128)S(1)}, u32[]{:S(2)}, u32[]{:S(2)}) %collective-permute-start.13) | collective-permute-done | bytes 524320 | tf_op jit(solution)/shard_map/ppermute | solution.py:11
  124.4 0.6 dynamic_slice.46
  125.5 8.4 %collective-permute-done.14 = f32[128,1024]{1,0:T(8,128)S(1)} collective-permute-done((f32[128,1024]{1,0:T(8,128)S(1)}, f32[128,1024]{1,0:T(8,128)S(1)}, u32[]{:S(2)}, u32[]{:S(2)}) %collective-permute-start.14) | collective-permute-done | bytes 524320 | tf_op jit(solution)/shard_map/ppermute | solution.py:11
  134.3 1.0 fusion.8
  135.4 9.2 %reduce-scatter.2.cloned.1.call-done = f32[128,1024]{1,0:T(8,128)} async-done(((f32[512,1024]{1,0:T(8,128)}), f32[128,1024]{1,0:T(8,128)}) %reduce-scatter.2.cloned.1.call-update) | async-done | bytes 524304 | tf_op jit(solution)/shard_map/reduce_scatter | solution.py:109
  144.5 1.3 fusion.10
  145.8 2.1 %fusion.12 = f32[128,1024]{1,0:T(8,128)} fusion(bf16[128,1024]{1,0:T(8,128)(2,1)S(1)} %copy-done.1, f32[128,1024]{1,0:T(8,128)} %reduce-scatter.2.cloned.1.call-done, f32[128]{0:T(128)S(1)} %fusion.10, f32[]{:T(128)} %bitcast.54, f32[128]{0:T(128)S(1)} %add_rsqrt_fusion), kind=kLoop, calls=%fused_computation.26 | loop fusion | flops 786432 | bytes 1311748 | tf_op jit(solution)/shard_map/mul | solution.py:115
  (69 shorter events, 6.2 us)
Async XLA Ops:
  7.2 35.7 %copy-start.3 = (s32[1,128]{1,0:T(1,128)S(1)}, s32[1,128]{1,0:T(1,128)}, u32[]{:S(2)}) copy-start(s32[1,128]{1,0:T(1,128)} %param.8) | copy-start | bytes 1540
  7.2 33.8 %all-gather.6.cloned.1.call-start = ((), (), s32[]{:S(2)}) async-start(), calls=%async_computation.1 | async-start | bytes 1310720 | tf_op jit(solution)/shard_map/all_gather | solution.py:58
  10.1 134.4 %reduce-scatter.2.cloned.1.call-start = ((), (), s32[]{:S(2)}) async-start(), calls=%async_computation.2 | async-start | bytes 2621440 | tf_op jit(solution)/shard_map/reduce_scatter | solution.py:109
  12.3 7.3 %collective-permute-start.1 = (bf16[128,1024]{1,0:T(8,128)(2,1)S(1)}, bf16[128,1024]{1,0:T(8,128)(2,1)S(1)}, u32[]{:S(2)}, u32[]{:S(2)}) collective-permute-start(bf16[128,1024]{1,0:T(8,128)(2,1)S(1)} %fusion.5), channel_id=1, source_target_pairs={{0,28},{4,0},{8,4},{12,8},{16,12},{20,16},{24,20},{28,24},{1,29},{... | collective-permute-start | bytes 786440 | tf_op jit(solution)/shard_map/ppermute | solution.py:11
  19.6 6.7 %collective-permute-start.3 = (bf16[128,1024]{1,0:T(8,128)(2,1)S(1)}, bf16[128,1024]{1,0:T(8,128)(2,1)S(1)}, u32[]{:S(2)}, u32[]{:S(2)}) collective-permute-start(bf16[128,1024]{1,0:T(8,128)(2,1)S(1)} %collective-permute-done.1), channel_id=1, source_target_pairs={{0,28},{4,0},{8,4},{12,8},{16,12},{20,16},{24,20},{28,24},{1,29},{... | collective-permute-start | bytes 786440 | tf_op jit(solution)/shard_map/ppermute | solution.py:11
  26.3 32.4 %collective-permute-start.5 = (bf16[128,1024]{1,0:T(8,128)(2,1)S(1)}, bf16[128,1024]{1,0:T(8,128)(2,1)S(1)}, u32[]{:S(2)}, u32[]{:S(2)}) collective-permute-start(bf16[128,1024]{1,0:T(8,128)(2,1)S(1)} %collective-permute-done.3), channel_id=1, source_target_pairs={{0,28},{4,0},{8,4},{12,8},{16,12},{20,16},{24,20},{28,24},{1,29},{... | collective-permute-start | bytes 786440 | tf_op jit(solution)/shard_map/ppermute | solution.py:11
  41.0 16.6 %copy-start = (bf16[512,1024]{1,0:T(8,128)(2,1)S(1)}, bf16[512,1024]{1,0:T(8,128)(2,1)}, u32[]{:S(2)}) copy-start(bf16[512,1024]{1,0:T(8,128)(2,1)} %all-gather.6.cloned.1.call-done) | copy-start | bytes 3145732
  55.0 4.3 %collective-permute-start = (f32[128]{0:T(128)S(1)}, f32[128]{0:T(128)S(1)}, u32[]{:S(2)}, u32[]{:S(2)}) collective-permute-start(f32[128]{0:T(128)S(1)} %get-tuple-element.198), channel_id=1, source_target_pairs={{0,28},{4,0},{8,4},{12,8},{16,12},{20,16},{24,20},{28,24},{1,29},{... | collective-permute-start | bytes 1544 | tf_op jit(solution)/shard_map/ppermute | solution.py:11
  55.1 4.5 %collective-permute-start.6 = (f32[128]{0:T(128)S(1)}, f32[128]{0:T(128)S(1)}, u32[]{:S(2)}, u32[]{:S(2)}) collective-permute-start(f32[128]{0:T(128)S(1)} %get-tuple-element.188), channel_id=1, source_target_pairs={{0,28},{4,0},{8,4},{12,8},{16,12},{20,16},{24,20},{28,24},{1,29},{... | collective-permute-start | bytes 1544 | tf_op jit(solution)/shard_map/ppermute | solution.py:11
  59.3 2.2 %collective-permute-start.2 = (f32[128]{0:T(128)S(1)}, f32[128]{0:T(128)S(1)}, u32[]{:S(2)}, u32[]{:S(2)}) collective-permute-start(f32[128]{0:T(128)S(1)} %max.61), channel_id=1, source_target_pairs={{0,28},{4,0},{8,4},{12,8},{16,12},{20,16},{24,20},{28,24},{1,29},{... | collective-permute-start | bytes 1544 | tf_op jit(solution)/shard_map/ppermute | solution.py:11
  59.6 3.9 %collective-permute-start.7 = (f32[128]{0:T(128)S(1)}, f32[128]{0:T(128)S(1)}, u32[]{:S(2)}, u32[]{:S(2)}) collective-permute-start(f32[128]{0:T(128)S(1)} %multiply_add_fusion.2), channel_id=1, source_target_pairs={{0,28},{4,0},{8,4},{12,8},{16,12},{20,16},{24,20},{28,24},{1,29},{... | collective-permute-start | bytes 1544 | tf_op jit(solution)/shard_map/ppermute | solution.py:11
  61.5 3.9 %collective-permute-start.4 = (f32[128]{0:T(128)S(1)}, f32[128]{0:T(128)S(1)}, u32[]{:S(2)}, u32[]{:S(2)}) collective-permute-start(f32[128]{0:T(128)S(1)} %max.62), channel_id=1, source_target_pairs={{0,28},{4,0},{8,4},{12,8},{16,12},{20,16},{24,20},{28,24},{1,29},{... | collective-permute-start | bytes 1544 | tf_op jit(solution)/shard_map/ppermute | solution.py:11
  63.5 26.2 %collective-permute-start.8 = (f32[128]{0:T(128)S(1)}, f32[128]{0:T(128)S(1)}, u32[]{:S(2)}, u32[]{:S(2)}) collective-permute-start(f32[128]{0:T(128)S(1)} %multiply_add_fusion.1), channel_id=1, source_target_pairs={{0,28},{4,0},{8,4},{12,8},{16,12},{20,16},{24,20},{28,24},{1,29},{... | collective-permute-start | bytes 1544 | tf_op jit(solution)/shard_map/ppermute | solution.py:11
  89.8 3.9 %collective-permute-start.9 = (f32[128]{0:T(128)S(1)}, f32[128]{0:T(128)S(1)}, u32[]{:S(2)}, u32[]{:S(2)}) collective-permute-start(f32[128]{0:T(128)S(1)} %log_add_fusion.1), channel_id=1, source_target_pairs={{0,4},{4,8},{8,12},{12,16},{16,20},{20,24},{24,28},{28,0},{1,5},{5... | collective-permute-start | bytes 1544 | tf_op jit(solution)/shard_map/ppermute | solution.py:11
  93.7 3.9 %collective-permute-start.10 = (f32[128]{0:T(128)S(1)}, f32[128]{0:T(128)S(1)}, u32[]{:S(2)}, u32[]{:S(2)}) collective-permute-start(f32[128]{0:T(128)S(1)} %collective-permute-done.9), channel_id=1, source_target_pairs={{0,4},{4,8},{8,12},{12,16},{16,20},{20,24},{24,28},{28,0},{1,5},{5... | collective-permute-start | bytes 1544 | tf_op jit(solution)/shard_map/ppermute | solution.py:11
  97.6 3.9 %collective-permute-start.11 = (f32[128]{0:T(128)S(1)}, f32[128]{0:T(128)S(1)}, u32[]{:S(2)}, u32[]{:S(2)}) collective-permute-start(f32[128]{0:T(128)S(1)} %collective-permute-done.10), channel_id=1, source_target_pairs={{0,4},{4,8},{8,12},{12,16},{16,20},{20,24},{24,28},{28,0},{1,5},{5... | collective-permute-start | bytes 1544 | tf_op jit(solution)/shard_map/ppermute | solution.py:11
  104.4 29.4 %copy-start.2 = (bf16[128,1024]{1,0:T(8,128)(2,1)S(1)}, bf16[128,1024]{1,0:T(8,128)(2,1)}, u32[]{:S(2)}) copy-start(bf16[128,1024]{1,0:T(8,128)(2,1)} %param.6) | copy-start | bytes 786436
  104.4 9.6 %collective-permute-start.12 = (f32[128,1024]{1,0:T(8,128)S(1)}, f32[128,1024]{1,0:T(8,128)S(1)}, u32[]{:S(2)}, u32[]{:S(2)}) collective-permute-start(f32[128,1024]{1,0:T(8,128)S(1)} %fusion.17), channel_id=1, source_target_pairs={{0,4},{4,8},{8,12},{12,16},{16,20},{20,24},{24,28},{28,0},{1,5},{5... | collective-permute-start | bytes 1572872 | tf_op jit(solution)/shard_map/ppermute | solution.py:11
  114.4 9.6 %collective-permute-start.13 = (f32[128,1024]{1,0:T(8,128)S(1)}, f32[128,1024]{1,0:T(8,128)S(1)}, u32[]{:S(2)}, u32[]{:S(2)}) collective-permute-start(f32[128,1024]{1,0:T(8,128)S(1)} %convolution_add_fusion), channel_id=1, source_target_pairs={{0,4},{4,8},{8,12},{12,16},{16,20},{20,24},{24,28},{28,0},{1,5},{5... | collective-permute-start | bytes 1572872 | tf_op jit(solution)/shard_map/ppermute | solution.py:11
  124.3 9.6 %collective-permute-start.14 = (f32[128,1024]{1,0:T(8,128)S(1)}, f32[128,1024]{1,0:T(8,128)S(1)}, u32[]{:S(2)}, u32[]{:S(2)}) collective-permute-start(f32[128,1024]{1,0:T(8,128)S(1)} %fusion.21), channel_id=1, source_target_pairs={{0,4},{4,8},{8,12},{12,16},{16,20},{20,24},{24,28},{28,0},{1,5},{5... | collective-permute-start | bytes 1572872 | tf_op jit(solution)/shard_map/ppermute | solution.py:11
  133.8 10.7 %copy-start.1 = (bf16[128,1024]{1,0:T(8,128)(2,1)S(1)}, bf16[128,1024]{1,0:T(8,128)(2,1)}, u32[]{:S(2)}) copy-start(bf16[128,1024]{1,0:T(8,128)(2,1)} %param.7) | copy-start | bytes 786436
Sparse Core Ops, SparseCore 0:
  10.2 30.6 all-gather.5
  104.1 40.3 reduce-scatter.1
where the time goes:
time: 155 us
  waiting for transfers between devices  65.7 us (42%)
  blocking collectives  35.8 us (23%)
  starting transfers between devices  17.9 us (12%)
  between operations  14.9 us (10%)
  other arithmetic  10.8 us (7%)
  matrix products  8.74 us (6%)
    ppermute x15, waiting for transfers between devices, passed_along(): lax.ppermute(array, axis, [(i, (i + by) % count) for i in range(count)])  45.1 us
    all_gather x3, blocking collectives, combined_all(): gathered = jax.tree.map(lambda a: lax.all_gather(a, axis), part)  35.8 us
    ppermute x15, starting transfers between devices, passed_along(): lax.ppermute(array, axis, [(i, (i + by) % count) for i in range(count)])  17.8 us
    all_gather x1, waiting for transfers between devices, on_device(): home_tile = lax.all_gather(txt_own, 'rep', axis=0, tiled=True)  11.4 us
    reduce_scatter x1, waiting for transfers between devices, on_device(): lax.psum_scatter(text_terms, 'rep', scatter_dimension=0, tiled=True)  9.15 us
    dot_general x4, matrix products, tile_scores(): jnp.einsum('id,jd->ij', img_part, text_tile, preferred_element_type=jnp.f...  3.59 us
    dot_general x4, matrix products, on_device(): jnp.einsum('ij,id->jd', weight, tile, preferred_element_type=jnp.float32)  3.56 us
  transfers between devices with their start and end apart: 17, of which 10 were waited for; matrix products, arithmetic and copies ran while one was open for 7% of the time, Pallas kernels for 0%

commit v1 on v0

v1 whole, which is shorter than its diff:
```python
import functools

import jax
import jax.numpy as jnp
from jax import lax
from jax.experimental import pallas as pl
from jax.experimental.pallas import tpu as pltpu
from jax.sharding import PartitionSpec as P

STEPS = 4
F32 = jnp.float32
BF16 = jnp.bfloat16
VMEM = pltpu.VMEM
SMEM = pltpu.SMEM


def passed_along(array, axis, by):
    count = lax.axis_size(axis)
    return lax.ppermute(array, axis, [(i, (i + by) % count) for i in range(count)])


def inverse_norm(wide):
    return lax.rsqrt(jnp.sum(wide * wide, axis=-1, keepdims=True) + 1e-06)


def unit_tile(raw):
    wide = raw.astype(F32)
    return (wide * inverse_norm(wide)).astype(BF16)


def diagonal(rows):
    return lax.broadcasted_iota(jnp.int32, (rows, rows), 0) == lax.broadcasted_iota(
        jnp.int32, (rows, rows), 1
    )


def to_lanes(column, eye):
    return jnp.sum(jnp.where(eye, column, 0.0), axis=0, keepdims=True)


def to_column(lanes, eye):
    return jnp.sum(jnp.where(eye, lanes, 0.0), axis=1, keepdims=True)


def onehot_of(positive, eye, parts, rows):
    wanted = to_column(positive.astype(F32), eye)
    lane = lax.broadcasted_iota(jnp.int32, (rows, rows), 1)
    quarter = lax.axis_index("rep")
    return [
        wanted == (lane + lax.rem(quarter - s + parts, parts) * rows).astype(F32)
        for s in range(parts)
    ]


def scores_kernel(parts, scale, positive, *refs):
    images, texts = refs[:STEPS], refs[STEPS : STEPS + parts]
    scores, img_out, txt_out, row_stats, col_stats, row_pos = refs[STEPS + parts :]
    rows = images[0].shape[0]
    factor = scale[0]
    eye = diagonal(rows)
    onehot = onehot_of(positive[...], eye, parts, rows)
    for s in range(parts):
        txt_out[s * rows : (s + 1) * rows, :] = unit_tile(texts[s][...])
    for k in range(STEPS):
        img_out[k * rows : (k + 1) * rows, :] = unit_tile(images[k][...])
    scores[...] = factor * lax.dot_general(
        img_out[...], txt_out[...], (((1,), (1,)), ((), ())), preferred_element_type=F32
    )
    peaks, sums = [], []
    for k in range(STEPS):
        tile = scores[k * rows : (k + 1) * rows, :]
        peak = jnp.max(tile, axis=1, keepdims=True)
        peaks.append(to_lanes(peak, eye))
        sums.append(to_lanes(jnp.sum(jnp.exp(tile - peak), axis=1, keepdims=True), eye))
    row_stats[...] = jnp.concatenate(peaks + sums, axis=0)
    peaks, sums, picked = [], [], []
    found = jnp.zeros((rows, 1), F32)
    for s in range(parts):
        tile = scores[:, s * rows : (s + 1) * rows]
        peak = jnp.max(tile, axis=0, keepdims=True)
        peaks.append(peak)
        sums.append(jnp.sum(jnp.exp(tile - peak), axis=0, keepdims=True))
        chosen = jnp.where(onehot[s], tile[:rows, :], 0.0)
        picked.append(jnp.sum(chosen, axis=0, keepdims=True))
        found = found + jnp.sum(chosen, axis=1, keepdims=True)
    row_pos[...] = to_lanes(found, eye)
    col_stats[...] = jnp.concatenate(peaks + sums + picked, axis=0)


def merged(parts):
    peak = functools.reduce(jnp.maximum, [p for p, _ in parts])
    total = sum(s * jnp.exp(p - peak) for p, s in parts)
    return peak + jnp.log(total)


def grads_kernel(parts, positive, scores, images, texts, row_pos, *refs):
    row_stats, col_stats = refs[: 2 * STEPS - 1], refs[2 * STEPS - 1 : 2 * STEPS - 1 + parts]
    outs = refs[2 * STEPS - 1 + parts : -1]
    weights = refs[-1]
    row_loss, col_loss = outs[:2]
    img_parts, txt_parts = outs[2 : 2 + STEPS], outs[2 + STEPS :]
    rows = row_pos.shape[1]
    eye = diagonal(rows)
    onehot = onehot_of(positive[...], eye, parts, rows)

    def row_pair(shift, k):
        table = row_stats[shift + STEPS - 1]
        return table[k + shift : k + shift + 1, :], table[
            STEPS + k + shift : STEPS + k + shift + 1, :
        ]

    row_lse = []
    for k in range(STEPS):
        lse = merged(
            [row_pair(t, k) for t in range(1 - STEPS, STEPS) if 0 <= k + t < STEPS]
        )
        if k == 0:
            row_loss[...] = lse - row_pos[...]
        row_lse.append(to_column(lse, eye))
    col_lse = []
    for s in range(parts):
        at = [(t, (s - t) % parts) for t in range(parts)]
        lse = merged(
            [(col_stats[t][q : q + 1, :], col_stats[t][parts + q : parts + q + 1, :]) for t, q in at]
        )
        if s == 0:
            picked = sum(col_stats[t][2 * parts + q : 2 * parts + q + 1, :] for t, q in at)
            col_loss[...] = lse - picked
        col_lse.append(lse)
    for k in range(STEPS):
        for s in range(parts):
            tile = scores[k * rows : (k + 1) * rows, s * rows : (s + 1) * rows]
            weight = 0.5 * (jnp.exp(tile - row_lse[k]) + jnp.exp(tile - col_lse[s]))
            if k == 0:
                weight = weight - onehot[s].astype(F32)
            weights[k * rows : (k + 1) * rows, s * rows : (s + 1) * rows] = weight.astype(BF16)
    for s in range(parts - 1, -1, -1):
        part = lax.dot_general(
            weights[:, s * rows : (s + 1) * rows],
            images[...],
            (((0,), (0,)), ((), ())),
            preferred_element_type=F32,
        )
        txt_parts[s][...] = part.astype(txt_parts[s].dtype)
    for k in range(STEPS):
        part = jnp.dot(
            weights[k * rows : (k + 1) * rows, :], texts[...], preferred_element_type=F32
        )
        img_parts[k][...] = part.astype(img_parts[k].dtype)


def final_kernel(scale, raw, *refs):
    grad = refs[-1]
    wide = raw[...].astype(F32)
    inverse = inverse_norm(wide)
    unit = wide * inverse
    total = scale[0] * sum(part[...].astype(F32) for part in refs[:-1])
    grad[...] = (total - unit * jnp.sum(unit * total, axis=-1, keepdims=True)) * inverse


def call(kernel, outs, specs, args, scratch=(), name=None):
    return pl.pallas_call(
        kernel,
        out_shape=outs,
        in_specs=[pl.BlockSpec(memory_space=space) for space in specs],
        out_specs=jax.tree.map(lambda _: pl.BlockSpec(memory_space=VMEM), outs),
        scratch_shapes=list(scratch),
        name=name,
    )(*args)


def on_device(image, text, positive, logit_scale):
    rows, width = image.shape
    parts = lax.axis_size("rep")
    shape = jax.ShapeDtypeStruct
    texts = [text] + [passed_along(text, "rep", t) for t in range(1, parts)]
    images = [image] + [passed_along(image, "blk", -k) for k in range(1, STEPS)]
    scores, img_tiles, txt_tiles, row_stats, col_stats, row_pos = call(
        functools.partial(scores_kernel, parts),
        (
            shape((STEPS * rows, parts * rows), F32),
            shape((STEPS * rows, width), BF16),
            shape((parts * rows, width), BF16),
            shape((2 * STEPS, rows), F32),
            shape((3 * parts, rows), F32),
            shape((1, rows), F32),
        ),
        [SMEM] + [VMEM] * (1 + STEPS + parts),
        (logit_scale, positive, *images, *texts),
        name="scores",
    )
    col_tables = [col_stats] + [passed_along(col_stats, "rep", t) for t in range(1, parts)]
    row_tables = [
        row_stats if t == 0 else passed_along(row_stats, "blk", t)
        for t in range(1 - STEPS, STEPS)
    ]
    row_loss, col_loss, *partials = call(
        functools.partial(grads_kernel, parts),
        (
            shape((1, rows), F32),
            shape((1, rows), F32),
            *[shape((rows, width), BF16 if k else F32) for k in range(STEPS)],
            *[shape((rows, width), BF16 if s else F32) for s in range(parts)],
        ),
        [VMEM] * (5 + 2 * STEPS - 1 + parts),
        (positive, scores, img_tiles, txt_tiles, row_pos, *row_tables, *col_tables),
        scratch=[pltpu.VMEM((STEPS * rows, parts * rows), BF16)],
        name="grads",
    )
    img_parts, txt_parts = partials[:STEPS], partials[STEPS:]
    txt_sums = [txt_parts[0]] + [
        passed_along(txt_parts[s], "rep", -s) for s in range(1, parts)
    ]
    img_sums = [img_parts[0]] + [passed_along(img_parts[k], "blk", k) for k in range(1, STEPS)]
    grads = [
        call(
            final_kernel,
            shape((rows, width), F32),
            [SMEM] + [VMEM] * (1 + len(sums)),
            (logit_scale, raw, *sums),
            name=name,
        )
        for raw, sums, name in ((image, img_sums, "img_final"), (text, txt_sums, "txt_final"))
    ]
    return (row_loss[0], col_loss[0], *grads)


def solution(mesh):
    placed = (P(("blk", "rep"), None), P(("blk", "rep"), None), P("blk", "rep"), P())
    return jax.shard_map(
        on_device,
        mesh=mesh,
        in_specs=placed,
        out_specs=(
            P(("blk", "rep")),
            P(("blk", "rep")),
            P(("blk", "rep"), None),
            P(("blk", "rep"), None),
        ),
        check_vma=False,
    )
```

time: 155 us -> 88.3 us (0.57)
  blocking collectives: 35.8 us -> 0 us
  waiting for transfers between devices: 65.7 us -> 39.8 us
  Pallas kernels: 0 us -> 13.8 us
  between operations: 14.9 us -> 1.42 us
  starting transfers between devices: 17.9 us -> 29.5 us
  other arithmetic: 10.8 us -> 0 us
  matrix products: 8.74 us -> 0 us
  local copies, waits for them, and re-layouts: 0.68 us -> 3.47 us
    all_gather x3 -> x0, blocking collectives: 35.8 us -> none  [combined_all(): gathered = jax.tree.map(lambda a: lax.all_gather(a, axis), part)]
    pallas_call x0 -> x4, Pallas kernels: none -> 13.8 us  [call(): pl.pallas_call(kernel, out_shape=outs, in_specs=[pl.BlockSpec(memory_spac...]
    ppermute x15 -> x21, starting transfers between devices: 17.8 us -> 29.5 us  [passed_along(): lax.ppermute(array, axis, [(i, (i + by) % count) for i in range(count)])]
    all_gather x1 -> x0, waiting for transfers between devices: 11.4 us -> none  [on_device(): home_tile = lax.all_gather(txt_own, 'rep', axis=0, tiled=True)]
    reduce_scatter x1 -> x0, waiting for transfers between devices: 9.15 us -> none  [on_device(): lax.psum_scatter(text_terms, 'rep', scatter_dimension=0, tiled=True)]
    dot_general x12 -> x0, matrix products: 8.74 us -> none  [the longest x4 3.59 us: tile_scores(): jnp.einsum('id,jd->ij', img_part, text_tile, preferred_element_type=jnp.f...]
    ppermute x15 -> x21, waiting for transfers between devices: 45.1 us -> 39.8 us  [passed_along(): lax.ppermute(array, axis, [(i, (i + by) % count) for i in range(count)])]
    reduce_sum x7 -> x0, other arithmetic: 4.23 us -> none  [the longest x2 2.17 us: normalize(): jnp.sum(widened * widened, axis=-1, keepdims=True) + 1e-06]
  transfers between devices with their start and end apart: 17 -> 21, of which waited for: 10 -> 9; matrix products, arithmetic and copies ran while one was open for 7% -> 0% of each run, Pallas kernels for 0% -> 3%
where the time goes in v1:
time: 88.3 us; the launch traced here: 88.1 us
  waiting for transfers between devices  39.8 us (45%)
  starting transfers between devices  29.5 us (33%)
  Pallas kernels  13.8 us (16%)
  local copies, waits for them, and re-layouts  3.47 us (4%)
  between operations  1.42 us (2%)
    ppermute x21, waiting for transfers between devices, passed_along(): lax.ppermute(array, axis, [(i, (i + by) % count) for i in range(count)])  39.8 us
    ppermute x21, starting transfers between devices, passed_along(): lax.ppermute(array, axis, [(i, (i + by) % count) for i in range(count)])  29.5 us
    pallas_call x4, Pallas kernels, call(): pl.pallas_call(kernel, out_shape=outs, in_specs=[pl.BlockSpec(memory_spac...  13.8 us
    unnamed x42, local copies, waits for them, and re-layouts  3.47 us
  transfers between devices with their start and end apart: 21, of which 9 were waited for; matrix products, arithmetic and copies ran while one was open for 0% of the time, Pallas kernels for 3%

profile of v1, /device:TPU:0, one launch (start us, length us, event | category | flops | bytes accessed | tf_op | source)
XLA Modules:
  0.0 88.1 jit_solution(2934129503982647698)
XLA Ops:
  0.6 2.5 %collective-permute-start.2 = (bf16[128,1024]{1,0:T(8,128)(2,1)}, bf16[128,1024]{1,0:T(8,128)(2,1)S(1)}, u32[]{:S(2)}, u32[]{:S(2)}) collective-permute-start(bf16[128,1024]{1,0:T(8,128)(2,1)} %raw.2), channel_id=1, source_target_pairs={{0,20},{4,24},{8,28},{12,0},{16,4},{20,8},{24,12},{28,16},{1,21},{... | collective-permute-start | bytes 786440 | tf_op jit(solution)/shard_map/ppermute | solution.py:19
  3.1 1.6 %collective-permute-start.1 = (bf16[128,1024]{1,0:T(8,128)(2,1)}, bf16[128,1024]{1,0:T(8,128)(2,1)S(1)}, u32[]{:S(2)}, u32[]{:S(2)}) collective-permute-start(bf16[128,1024]{1,0:T(8,128)(2,1)} %raw.2), channel_id=1, source_target_pairs={{0,24},{4,28},{8,0},{12,4},{16,8},{20,12},{24,16},{28,20},{1,25},{... | collective-permute-start | bytes 786440 | tf_op jit(solution)/shard_map/ppermute | solution.py:19
  4.7 1.3 %collective-permute-start = (bf16[128,1024]{1,0:T(8,128)(2,1)}, bf16[128,1024]{1,0:T(8,128)(2,1)S(1)}, u32[]{:S(2)}, u32[]{:S(2)}) collective-permute-start(bf16[128,1024]{1,0:T(8,128)(2,1)} %raw.2), channel_id=1, source_target_pairs={{0,28},{4,0},{8,4},{12,8},{16,12},{20,16},{24,20},{28,24},{1,29},{... | collective-permute-start | bytes 786440 | tf_op jit(solution)/shard_map/ppermute | solution.py:19
  6.0 3.6 %collective-permute-start.5 = (bf16[128,1024]{1,0:T(8,128)(2,1)}, bf16[128,1024]{1,0:T(8,128)(2,1)S(1)}, u32[]{:S(2)}, u32[]{:S(2)}) collective-permute-start(bf16[128,1024]{1,0:T(8,128)(2,1)} %raw.3), channel_id=1, source_target_pairs={{0,3},{1,0},{2,1},{3,2},{4,7},{5,4},{6,5},{7,6},{8,11},{9,8},{10,9... | collective-permute-start | bytes 786440 | tf_op jit(solution)/shard_map/ppermute | solution.py:19
  9.6 1.4 %collective-permute-start.3 = (bf16[128,1024]{1,0:T(8,128)(2,1)}, bf16[128,1024]{1,0:T(8,128)(2,1)S(1)}, u32[]{:S(2)}, u32[]{:S(2)}) collective-permute-start(bf16[128,1024]{1,0:T(8,128)(2,1)} %raw.3), channel_id=1, source_target_pairs={{0,1},{1,2},{2,3},{3,0},{4,5},{5,6},{6,7},{7,4},{8,9},{9,10},{10,1... | collective-permute-start | bytes 786440 | tf_op jit(solution)/shard_map/ppermute | solution.py:19
  11.7 0.8 collective-permute-done.1.refs_2_
  12.5 4.2 %collective-permute-done.refs_1_ = bf16[128,1024]{1,0:T(8,128)(2,1)S(1)} collective-permute-done((bf16[128,1024]{1,0:T(8,128)(2,1)}, bf16[128,1024]{1,0:T(8,128)(2,1)S(1)}, u32[]{:S(2)}, u32[]{:S(2)}) %collective-permute-start) | collective-permute-done | bytes 262176 | tf_op jit(solution)/shard_map/ppermute | solution.py:19
  16.7 14.8 %collective-permute-done.4.refs_6_ = bf16[128,1024]{1,0:T(8,128)(2,1)S(1)} collective-permute-done((bf16[128,1024]{1,0:T(8,128)(2,1)}, bf16[128,1024]{1,0:T(8,128)(2,1)S(1)}, u32[]{:S(2)}, u32[]{:S(2)}) %collective-permute-start.4) | collective-permute-done | bytes 262176 | tf_op jit(solution)/shard_map/ppermute | solution.py:19
  31.5 0.7 copy-done.10
  32.2 0.7 copy-done.11
  32.9 4.1 %scores.1 = (f32[512,512]{1,0:T(8,128)}, bf16[512,1024]{1,0:T(8,128)(2,1)}, bf16[512,1024]{1,0:T(8,128)(2,1)}, f32[8,128]{1,0:T(8,128)}, f32[12,128]{1,0:T(8,128)}, /*index=5*/f32[1,128]{1,0:T(1,128)}) custom-call(f32[1]{0:T(128)S(6)} %copy.8.scale, s32[1,128]{1,0:T(1,128)} %positive.3, bf16[128,1024]{1,0:T(8,128)(2,1)} %raw.2, bf16[128,1024]{1,0:T(8,128)(2,1)} %copy-done.8, ...), custom_call_target="tpu_custom_call" | custom-call | tf_op jit(solution)/shard_map/scores/pallas_call | solution.py:162
  37.0 1.3 %collective-permute-start.10 = (f32[8,128]{1,0:T(8,128)}, f32[8,128]{1,0:T(8,128)S(1)}, u32[]{:S(2)}, u32[]{:S(2)}) collective-permute-start(f32[8,128]{1,0:T(8,128)} %get-tuple-element.24.refs_3_), channel_id=1, source_target_pairs={{0,8},{4,12},{8,16},{12,20},{16,24},{20,28},{24,0},{28,4},{1,9},{5... | collective-permute-start | bytes 12296 | tf_op jit(solution)/shard_map/ppermute | solution.py:19
  38.4 0.3 collective-permute-start.9
  38.6 2.4 %collective-permute-start.8 = (f32[8,128]{1,0:T(8,128)}, f32[8,128]{1,0:T(8,128)S(1)}, u32[]{:S(2)}, u32[]{:S(2)}) collective-permute-start(f32[8,128]{1,0:T(8,128)} %get-tuple-element.24.refs_3_), channel_id=1, source_target_pairs={{0,28},{4,0},{8,4},{12,8},{16,12},{20,16},{24,20},{28,24},{1,29},{... | collective-permute-start | bytes 12296 | tf_op jit(solution)/shard_map/ppermute | solution.py:19
  41.0 3.0 %collective-permute-start.14 = (f32[12,128]{1,0:T(8,128)}, f32[12,128]{1,0:T(8,128)S(1)}, u32[]{:S(2)}, u32[]{:S(2)}) collective-permute-start(f32[12,128]{1,0:T(8,128)} %get-tuple-element.25.refs_7_), channel_id=1, source_target_pairs={{0,3},{1,0},{2,1},{3,2},{4,7},{5,4},{6,5},{7,6},{8,11},{9,8},{10,9... | collective-permute-start | bytes 18440 | tf_op jit(solution)/shard_map/ppermute | solution.py:19
  44.0 1.6 %collective-permute-start.12 = (f32[12,128]{1,0:T(8,128)}, f32[12,128]{1,0:T(8,128)S(1)}, u32[]{:S(2)}, u32[]{:S(2)}) collective-permute-start(f32[12,128]{1,0:T(8,128)} %get-tuple-element.25.refs_7_), channel_id=1, source_target_pairs={{0,1},{1,2},{2,3},{3,0},{4,5},{5,6},{6,7},{7,4},{8,9},{9,10},{10,1... | collective-permute-start | bytes 18440 | tf_op jit(solution)/shard_map/ppermute | solution.py:19
  45.6 0.7 collective-permute-start.7
  46.3 3.1 %collective-permute-done.7.refs_1_ = f32[8,128]{1,0:T(8,128)S(1)} collective-permute-done((f32[8,128]{1,0:T(8,128)}, f32[8,128]{1,0:T(8,128)S(1)}, u32[]{:S(2)}, u32[]{:S(2)}) %collective-permute-start.7) | collective-permute-done | bytes 4128 | tf_op jit(solution)/shard_map/ppermute | solution.py:19
  49.7 0.2 copy-done.19
  50.3 4.8 %grads.1 = (f32[1,128]{1,0:T(1,128)}, f32[1,128]{1,0:T(1,128)}, f32[128,1024]{1,0:T(8,128)}, bf16[128,1024]{1,0:T(8,128)(2,1)}, bf16[128,1024]{1,0:T(8,128)(2,1)...) custom-call(s32[1,128]{1,0:T(1,128)} %positive.3, ...), custom_call_target="tpu_custom_call" | custom-call | tf_op jit(solution)/shard_map/grads/pallas_call | solution.py:162
  55.1 2.1 %collective-permute-start.16 = (bf16[128,1024]{1,0:T(8,128)(2,1)}, bf16[128,1024]{1,0:T(8,128)(2,1)S(1)}, u32[]{:S(2)}, u32[]{:S(2)}) collective-permute-start(bf16[128,1024]{1,0:T(8,128)(2,1)} %get-tuple-element.30), channel_id=1, source_target_pairs={{0,8},{4,12},{8,16},{12,20},{16,24},{20,28},{24,0},{28,4},{1,9},{5... | collective-permute-start | bytes 786440 | tf_op jit(solution)/shard_map/ppermute | solution.py:19
  57.3 1.4 %collective-permute-start.17 = (bf16[128,1024]{1,0:T(8,128)(2,1)}, bf16[128,1024]{1,0:T(8,128)(2,1)S(1)}, u32[]{:S(2)}, u32[]{:S(2)}) collective-permute-start(bf16[128,1024]{1,0:T(8,128)(2,1)} %get-tuple-element.31), channel_id=1, source_target_pairs={{0,12},{4,16},{8,20},{12,24},{16,28},{20,0},{24,4},{28,8},{1,13},{... | collective-permute-start | bytes 786440 | tf_op jit(solution)/shard_map/ppermute | solution.py:19
  58.7 2.5 %collective-permute-start.18 = (bf16[128,1024]{1,0:T(8,128)(2,1)}, bf16[128,1024]{1,0:T(8,128)(2,1)S(1)}, u32[]{:S(2)}, u32[]{:S(2)}) collective-permute-start(bf16[128,1024]{1,0:T(8,128)(2,1)} %get-tuple-element.33), channel_id=1, source_target_pairs={{0,3},{1,0},{2,1},{3,2},{4,7},{5,4},{6,5},{7,6},{8,11},{9,8},{10,9... | collective-permute-start | bytes 786440 | tf_op jit(solution)/shard_map/ppermute | solution.py:19
  61.2 1.1 %collective-permute-start.19 = (bf16[128,1024]{1,0:T(8,128)(2,1)}, bf16[128,1024]{1,0:T(8,128)(2,1)S(1)}, u32[]{:S(2)}, u32[]{:S(2)}) collective-permute-start(bf16[128,1024]{1,0:T(8,128)(2,1)} %get-tuple-element.34), channel_id=1, source_target_pairs={{0,2},{1,3},{2,0},{3,1},{4,6},{5,7},{6,4},{7,5},{8,10},{9,11},{10,... | collective-permute-start | bytes 786440 | tf_op jit(solution)/shard_map/ppermute | solution.py:19
  62.3 2.0 %collective-permute-done.15.refs_1_ = bf16[128,1024]{1,0:T(8,128)(2,1)S(1)} collective-permute-done((bf16[128,1024]{1,0:T(8,128)(2,1)}, bf16[128,1024]{1,0:T(8,128)(2,1)S(1)}, u32[]{:S(2)}, u32[]{:S(2)}) %collective-permute-start.15) | collective-permute-done | bytes 262176 | tf_op jit(solution)/shard_map/ppermute | solution.py:19
  64.3 2.7 %collective-permute-start.20 = (bf16[128,1024]{1,0:T(8,128)(2,1)}, bf16[128,1024]{1,0:T(8,128)(2,1)S(1)}, u32[]{:S(2)}, u32[]{:S(2)}) collective-permute-start(bf16[128,1024]{1,0:T(8,128)(2,1)} %get-tuple-element.35), channel_id=1, source_target_pairs={{0,1},{1,2},{2,3},{3,0},{4,5},{5,6},{6,7},{7,4},{8,9},{9,10},{10,1... | collective-permute-start | bytes 786440 | tf_op jit(solution)/shard_map/ppermute | solution.py:19
  67.0 6.2 %collective-permute-done.17.refs_3_ = bf16[128,1024]{1,0:T(8,128)(2,1)S(1)} collective-permute-done((bf16[128,1024]{1,0:T(8,128)(2,1)}, bf16[128,1024]{1,0:T(8,128)(2,1)S(1)}, u32[]{:S(2)}, u32[]{:S(2)}) %collective-permute-start.17) | collective-permute-done | bytes 262176 | tf_op jit(solution)/shard_map/ppermute | solution.py:19
  73.3 0.7 copy-done.5
  74.0 2.4 %img_final.1 = f32[128,1024]{1,0:T(8,128)} custom-call(f32[1]{0:T(128)S(6)} %copy.8.scale, bf16[128,1024]{1,0:T(8,128)(2,1)} %raw.2, f32[128,1024]{1,0:T(8,128)} %get-tuple-element.28.refs_0_, bf16[128,1024]{1,0:T(8,128)(2,1)} %copy-done.2, bf16[128,1024]{1,0:T(8,128)(2,1)} %copy-done.3, bf16[128,1024]{1,0:T(8,128)(2,1)} %copy-done.5), custom_call_target="tpu_custom_call" | custom-call | tf_op jit(solution)/shard_map/img_final/pallas_call | solution.py:162
  76.4 8.4 %collective-permute-done.19.refs_2_ = bf16[128,1024]{1,0:T(8,128)(2,1)S(1)} collective-permute-done((bf16[128,1024]{1,0:T(8,128)(2,1)}, bf16[128,1024]{1,0:T(8,128)(2,1)S(1)}, u32[]{:S(2)}, u32[]{:S(2)}) %collective-permute-start.19) | collective-permute-done | bytes 262176 | tf_op jit(solution)/shard_map/ppermute | solution.py:19
  84.8 0.7 copy-done.1
  85.6 2.4 %txt_final.1 = f32[128,1024]{1,0:T(8,128)} custom-call(f32[1]{0:T(128)S(6)} %copy.8.scale, bf16[128,1024]{1,0:T(8,128)(2,1)} %raw.3, f32[128,1024]{1,0:T(8,128)} %get-tuple-element.32.refs_0_, bf16[128,1024]{1,0:T(8,128)(2,1)} %copy-done, bf16[128,1024]{1,0:T(8,128)(2,1)} %copy-done.1, bf16[128,1024]{1,0:T(8,128)(2,1)} %copy-done.4), custom_call_target="tpu_custom_call" | custom-call | tf_op jit(solution)/shard_map/txt_final/pallas_call | solution.py:162
  (56 shorter events, 0.9 us)
Async XLA Ops:
  0.6 9.0 %collective-permute-start.2 = (bf16[128,1024]{1,0:T(8,128)(2,1)}, bf16[128,1024]{1,0:T(8,128)(2,1)S(1)}, u32[]{:S(2)}, u32[]{:S(2)}) collective-permute-start(bf16[128,1024]{1,0:T(8,128)(2,1)} %raw.2), channel_id=1, source_target_pairs={{0,20},{4,24},{8,28},{12,0},{16,4},{20,8},{24,12},{28,16},{1,21},{... | collective-permute-start | bytes 786440 | tf_op jit(solution)/shard_map/ppermute | solution.py:19
  3.1 9.4 %collective-permute-start.1 = (bf16[128,1024]{1,0:T(8,128)(2,1)}, bf16[128,1024]{1,0:T(8,128)(2,1)S(1)}, u32[]{:S(2)}, u32[]{:S(2)}) collective-permute-start(bf16[128,1024]{1,0:T(8,128)(2,1)} %raw.2), channel_id=1, source_target_pairs={{0,24},{4,28},{8,0},{12,4},{16,8},{20,12},{24,16},{28,20},{1,25},{... | collective-permute-start | bytes 786440 | tf_op jit(solution)/shard_map/ppermute | solution.py:19
  4.7 12.0 %collective-permute-start = (bf16[128,1024]{1,0:T(8,128)(2,1)}, bf16[128,1024]{1,0:T(8,128)(2,1)S(1)}, u32[]{:S(2)}, u32[]{:S(2)}) collective-permute-start(bf16[128,1024]{1,0:T(8,128)(2,1)} %raw.2), channel_id=1, source_target_pairs={{0,28},{4,0},{8,4},{12,8},{16,12},{20,16},{24,20},{28,24},{1,29},{... | collective-permute-start | bytes 786440 | tf_op jit(solution)/shard_map/ppermute | solution.py:19
  6.0 10.7 %collective-permute-start.5 = (bf16[128,1024]{1,0:T(8,128)(2,1)}, bf16[128,1024]{1,0:T(8,128)(2,1)S(1)}, u32[]{:S(2)}, u32[]{:S(2)}) collective-permute-start(bf16[128,1024]{1,0:T(8,128)(2,1)} %raw.3), channel_id=1, source_target_pairs={{0,3},{1,0},{2,1},{3,2},{4,7},{5,4},{6,5},{7,6},{8,11},{9,8},{10,9... | collective-permute-start | bytes 786440 | tf_op jit(solution)/shard_map/ppermute | solution.py:19
  9.6 21.9 %collective-permute-start.4 = (bf16[128,1024]{1,0:T(8,128)(2,1)}, bf16[128,1024]{1,0:T(8,128)(2,1)S(1)}, u32[]{:S(2)}, u32[]{:S(2)}) collective-permute-start(bf16[128,1024]{1,0:T(8,128)(2,1)} %raw.3), channel_id=1, source_target_pairs={{0,2},{1,3},{2,0},{3,1},{4,6},{5,7},{6,4},{7,5},{8,10},{9,11},{10,... | collective-permute-start | bytes 786440 | tf_op jit(solution)/shard_map/ppermute | solution.py:19
  9.6 21.9 %copy-start.6 = (bf16[128,1024]{1,0:T(8,128)(2,1)}, bf16[128,1024]{1,0:T(8,128)(2,1)S(1)}, u32[]{:S(2)}) copy-start(bf16[128,1024]{1,0:T(8,128)(2,1)S(1)} %collective-permute-done.2.refs_3_) | copy-start | bytes 786436
  9.6 21.8 %collective-permute-start.3 = (bf16[128,1024]{1,0:T(8,128)(2,1)}, bf16[128,1024]{1,0:T(8,128)(2,1)S(1)}, u32[]{:S(2)}, u32[]{:S(2)}) collective-permute-start(bf16[128,1024]{1,0:T(8,128)(2,1)} %raw.3), channel_id=1, source_target_pairs={{0,1},{1,2},{2,3},{3,0},{4,5},{5,6},{6,7},{7,4},{8,9},{9,10},{10,1... | collective-permute-start | bytes 786440 | tf_op jit(solution)/shard_map/ppermute | solution.py:19
  12.5 19.0 %copy-start.7 = (bf16[128,1024]{1,0:T(8,128)(2,1)}, bf16[128,1024]{1,0:T(8,128)(2,1)S(1)}, u32[]{:S(2)}) copy-start(bf16[128,1024]{1,0:T(8,128)(2,1)S(1)} %collective-permute-done.1.refs_2_) | copy-start | bytes 786436
  16.7 14.8 %copy-start.8 = (bf16[128,1024]{1,0:T(8,128)(2,1)}, bf16[128,1024]{1,0:T(8,128)(2,1)S(1)}, u32[]{:S(2)}) copy-start(bf16[128,1024]{1,0:T(8,128)(2,1)S(1)} %collective-permute-done.refs_1_) | copy-start | bytes 786436
  16.7 14.8 %copy-start.9 = (bf16[128,1024]{1,0:T(8,128)(2,1)}, bf16[128,1024]{1,0:T(8,128)(2,1)S(1)}, u32[]{:S(2)}) copy-start(bf16[128,1024]{1,0:T(8,128)(2,1)S(1)} %collective-permute-done.5.refs_7_) | copy-start | bytes 786436
  37.0 7.0 %collective-permute-start.11 = (f32[8,128]{1,0:T(8,128)}, f32[8,128]{1,0:T(8,128)S(1)}, u32[]{:S(2)}, u32[]{:S(2)}) collective-permute-start(f32[8,128]{1,0:T(8,128)} %get-tuple-element.24.refs_3_), channel_id=1, source_target_pairs={{0,12},{4,16},{8,20},{12,24},{16,28},{20,0},{24,4},{28,8},{1,13},{... | collective-permute-start | bytes 12296 | tf_op jit(solution)/shard_map/ppermute | solution.py:19
  37.0 7.0 %collective-permute-start.10 = (f32[8,128]{1,0:T(8,128)}, f32[8,128]{1,0:T(8,128)S(1)}, u32[]{:S(2)}, u32[]{:S(2)}) collective-permute-start(f32[8,128]{1,0:T(8,128)} %get-tuple-element.24.refs_3_), channel_id=1, source_target_pairs={{0,8},{4,12},{8,16},{12,20},{16,24},{20,28},{24,0},{28,4},{1,9},{5... | collective-permute-start | bytes 12296 | tf_op jit(solution)/shard_map/ppermute | solution.py:19
  38.4 7.2 %collective-permute-start.9 = (f32[8,128]{1,0:T(8,128)}, f32[8,128]{1,0:T(8,128)S(1)}, u32[]{:S(2)}, u32[]{:S(2)}) collective-permute-start(f32[8,128]{1,0:T(8,128)} %get-tuple-element.24.refs_3_), channel_id=1, source_target_pairs={{0,4},{4,8},{8,12},{12,16},{16,20},{20,24},{24,28},{28,0},{1,5},{5... | collective-permute-start | bytes 12296 | tf_op jit(solution)/shard_map/ppermute | solution.py:19
  38.6 7.7 %collective-permute-start.8 = (f32[8,128]{1,0:T(8,128)}, f32[8,128]{1,0:T(8,128)S(1)}, u32[]{:S(2)}, u32[]{:S(2)}) collective-permute-start(f32[8,128]{1,0:T(8,128)} %get-tuple-element.24.refs_3_), channel_id=1, source_target_pairs={{0,28},{4,0},{8,4},{12,8},{16,12},{20,16},{24,20},{28,24},{1,29},{... | collective-permute-start | bytes 12296 | tf_op jit(solution)/shard_map/ppermute | solution.py:19
  41.0 8.6 %collective-permute-start.14 = (f32[12,128]{1,0:T(8,128)}, f32[12,128]{1,0:T(8,128)S(1)}, u32[]{:S(2)}, u32[]{:S(2)}) collective-permute-start(f32[12,128]{1,0:T(8,128)} %get-tuple-element.25.refs_7_), channel_id=1, source_target_pairs={{0,3},{1,0},{2,1},{3,2},{4,7},{5,4},{6,5},{7,6},{8,11},{9,8},{10,9... | collective-permute-start | bytes 18440 | tf_op jit(solution)/shard_map/ppermute | solution.py:19
  44.0 5.7 %copy-start.15 = (f32[8,128]{1,0:T(8,128)}, f32[8,128]{1,0:T(8,128)S(1)}, u32[]{:S(2)}) copy-start(f32[8,128]{1,0:T(8,128)S(1)} %collective-permute-done.11.refs_6_) | copy-start | bytes 12292
  44.0 5.6 %collective-permute-start.13 = (f32[12,128]{1,0:T(8,128)}, f32[12,128]{1,0:T(8,128)S(1)}, u32[]{:S(2)}, u32[]{:S(2)}) collective-permute-start(f32[12,128]{1,0:T(8,128)} %get-tuple-element.25.refs_7_), channel_id=1, source_target_pairs={{0,2},{1,3},{2,0},{3,1},{4,6},{5,7},{6,4},{7,5},{8,10},{9,11},{10,... | collective-permute-start | bytes 18440 | tf_op jit(solution)/shard_map/ppermute | solution.py:19
  44.0 5.7 %copy-start.16 = (f32[8,128]{1,0:T(8,128)}, f32[8,128]{1,0:T(8,128)S(1)}, u32[]{:S(2)}) copy-start(f32[8,128]{1,0:T(8,128)S(1)} %collective-permute-done.10.refs_5_) | copy-start | bytes 12292
  44.0 5.7 %collective-permute-start.12 = (f32[12,128]{1,0:T(8,128)}, f32[12,128]{1,0:T(8,128)S(1)}, u32[]{:S(2)}, u32[]{:S(2)}) collective-permute-start(f32[12,128]{1,0:T(8,128)} %get-tuple-element.25.refs_7_), channel_id=1, source_target_pairs={{0,1},{1,2},{2,3},{3,0},{4,5},{5,6},{6,7},{7,4},{8,9},{9,10},{10,1... | collective-permute-start | bytes 18440 | tf_op jit(solution)/shard_map/ppermute | solution.py:19
  45.6 4.2 %copy-start.17 = (f32[8,128]{1,0:T(8,128)}, f32[8,128]{1,0:T(8,128)S(1)}, u32[]{:S(2)}) copy-start(f32[8,128]{1,0:T(8,128)S(1)} %collective-permute-done.9.refs_4_) | copy-start | bytes 12292
  45.6 3.8 %collective-permute-start.7 = (f32[8,128]{1,0:T(8,128)}, f32[8,128]{1,0:T(8,128)S(1)}, u32[]{:S(2)}, u32[]{:S(2)}) collective-permute-start(f32[8,128]{1,0:T(8,128)} %get-tuple-element.24.refs_3_), channel_id=1, source_target_pairs={{0,24},{4,28},{8,0},{12,4},{16,8},{20,12},{24,16},{28,20},{1,25},{... | collective-permute-start | bytes 12296 | tf_op jit(solution)/shard_map/ppermute | solution.py:19
  46.3 3.4 %copy-start.18 = (f32[8,128]{1,0:T(8,128)}, f32[8,128]{1,0:T(8,128)S(1)}, u32[]{:S(2)}) copy-start(f32[8,128]{1,0:T(8,128)S(1)} %collective-permute-done.8.refs_2_) | copy-start | bytes 12292
  46.3 3.2 %collective-permute-start.6 = (f32[8,128]{1,0:T(8,128)}, f32[8,128]{1,0:T(8,128)S(1)}, u32[]{:S(2)}, u32[]{:S(2)}) collective-permute-start(f32[8,128]{1,0:T(8,128)} %get-tuple-element.24.refs_3_), channel_id=1, source_target_pairs={{0,20},{4,24},{8,28},{12,0},{16,4},{20,8},{24,12},{28,16},{1,21},{... | collective-permute-start | bytes 12296 | tf_op jit(solution)/shard_map/ppermute | solution.py:19
  55.1 9.2 %collective-permute-start.15 = (bf16[128,1024]{1,0:T(8,128)(2,1)}, bf16[128,1024]{1,0:T(8,128)(2,1)S(1)}, u32[]{:S(2)}, u32[]{:S(2)}) collective-permute-start(bf16[128,1024]{1,0:T(8,128)(2,1)} %get-tuple-element.29), channel_id=1, source_target_pairs={{0,4},{4,8},{8,12},{12,16},{16,20},{20,24},{24,28},{28,0},{1,5},{5... | collective-permute-start | bytes 786440 | tf_op jit(solution)/shard_map/ppermute | solution.py:19
  55.1 11.9 %collective-permute-start.16 = (bf16[128,1024]{1,0:T(8,128)(2,1)}, bf16[128,1024]{1,0:T(8,128)(2,1)S(1)}, u32[]{:S(2)}, u32[]{:S(2)}) collective-permute-start(bf16[128,1024]{1,0:T(8,128)(2,1)} %get-tuple-element.30), channel_id=1, source_target_pairs={{0,8},{4,12},{8,16},{12,20},{16,24},{20,28},{24,0},{28,4},{1,9},{5... | collective-permute-start | bytes 786440 | tf_op jit(solution)/shard_map/ppermute | solution.py:19
  57.3 16.0 %collective-permute-start.17 = (bf16[128,1024]{1,0:T(8,128)(2,1)}, bf16[128,1024]{1,0:T(8,128)(2,1)S(1)}, u32[]{:S(2)}, u32[]{:S(2)}) collective-permute-start(bf16[128,1024]{1,0:T(8,128)(2,1)} %get-tuple-element.31), channel_id=1, source_target_pairs={{0,12},{4,16},{8,20},{12,24},{16,28},{20,0},{24,4},{28,8},{1,13},{... | collective-permute-start | bytes 786440 | tf_op jit(solution)/shard_map/ppermute | solution.py:19
  58.7 17.7 %collective-permute-start.18 = (bf16[128,1024]{1,0:T(8,128)(2,1)}, bf16[128,1024]{1,0:T(8,128)(2,1)S(1)}, u32[]{:S(2)}, u32[]{:S(2)}) collective-permute-start(bf16[128,1024]{1,0:T(8,128)(2,1)} %get-tuple-element.33), channel_id=1, source_target_pairs={{0,3},{1,0},{2,1},{3,2},{4,7},{5,4},{6,5},{7,6},{8,11},{9,8},{10,9... | collective-permute-start | bytes 786440 | tf_op jit(solution)/shard_map/ppermute | solution.py:19
  61.2 23.6 %collective-permute-start.19 = (bf16[128,1024]{1,0:T(8,128)(2,1)}, bf16[128,1024]{1,0:T(8,128)(2,1)S(1)}, u32[]{:S(2)}, u32[]{:S(2)}) collective-permute-start(bf16[128,1024]{1,0:T(8,128)(2,1)} %get-tuple-element.34), channel_id=1, source_target_pairs={{0,2},{1,3},{2,0},{3,1},{4,6},{5,7},{6,4},{7,5},{8,10},{9,11},{10,... | collective-permute-start | bytes 786440 | tf_op jit(solution)/shard_map/ppermute | solution.py:19
  64.3 9.0 %copy-start.2 = (bf16[128,1024]{1,0:T(8,128)(2,1)}, bf16[128,1024]{1,0:T(8,128)(2,1)S(1)}, u32[]{:S(2)}) copy-start(bf16[128,1024]{1,0:T(8,128)(2,1)S(1)} %collective-permute-done.15.refs_1_) | copy-start | bytes 786436
  64.3 20.5 %collective-permute-start.20 = (bf16[128,1024]{1,0:T(8,128)(2,1)}, bf16[128,1024]{1,0:T(8,128)(2,1)S(1)}, u32[]{:S(2)}, u32[]{:S(2)}) collective-permute-start(bf16[128,1024]{1,0:T(8,128)(2,1)} %get-tuple-element.35), channel_id=1, source_target_pairs={{0,1},{1,2},{2,3},{3,0},{4,5},{5,6},{6,7},{7,4},{8,9},{9,10},{10,1... | collective-permute-start | bytes 786440 | tf_op jit(solution)/shard_map/ppermute | solution.py:19
  67.0 6.2 %copy-start.3 = (bf16[128,1024]{1,0:T(8,128)(2,1)}, bf16[128,1024]{1,0:T(8,128)(2,1)S(1)}, u32[]{:S(2)}) copy-start(bf16[128,1024]{1,0:T(8,128)(2,1)S(1)} %collective-permute-done.16.refs_2_) | copy-start | bytes 786436
  76.4 8.4 %copy-start = (bf16[128,1024]{1,0:T(8,128)(2,1)}, bf16[128,1024]{1,0:T(8,128)(2,1)S(1)}, u32[]{:S(2)}) copy-start(bf16[128,1024]{1,0:T(8,128)(2,1)S(1)} %collective-permute-done.18.refs_1_) | copy-start | bytes 786436
  (10 other events, 6.6 us)

commit v2 on v1

v2 whole, which is shorter than its diff:
```python
import functools

import jax
import jax.numpy as jnp
from jax import lax
from jax.experimental import pallas as pl
from jax.experimental.pallas import tpu as pltpu
from jax.sharding import PartitionSpec as P

STEPS = 4
CHUNK = 16
F32 = jnp.float32
BF16 = jnp.bfloat16
VMEM = pltpu.VMEM
SMEM = pltpu.SMEM


def power_of_two(count):
    return count & (count - 1) == 0


def place(own, slot, count):
    return own ^ slot if power_of_two(count) else (own + slot) % count


def slot_at(slot, partner, count):
    return slot ^ partner if power_of_two(count) else (slot - partner) % count


def fetched(array, axis, slot):
    count = lax.axis_size(axis)
    return lax.ppermute(array, axis, [(place(i, slot, count), i) for i in range(count)])


def returned(array, axis, slot):
    count = lax.axis_size(axis)
    return lax.ppermute(array, axis, [(i, place(i, slot, count)) for i in range(count)])


def passed_along(array, axis, by):
    count = lax.axis_size(axis)
    return lax.ppermute(array, axis, [(i, (i + by) % count) for i in range(count)])


def inverse_norm(wide):
    return lax.rsqrt(jnp.sum(wide * wide, axis=-1, keepdims=True) + 1e-06)


def store_units(raw, out, base):
    for at in range(0, raw.shape[0], CHUNK):
        wide = raw[at : at + CHUNK, :].astype(F32)
        out[base + at : base + at + CHUNK, :] = (wide * inverse_norm(wide)).astype(BF16)


def diagonal(rows):
    return lax.broadcasted_iota(jnp.int32, (rows, rows), 0) == lax.broadcasted_iota(
        jnp.int32, (rows, rows), 1
    )


def to_lanes(column, eye):
    return jnp.sum(jnp.where(eye, column, 0.0), axis=0, keepdims=True)


def to_column(lanes, eye):
    return jnp.sum(jnp.where(eye, lanes, 0.0), axis=1, keepdims=True)


def onehot_of(positive, eye, parts, rows):
    wanted = to_column(positive.astype(F32), eye)
    lane = lax.broadcasted_iota(jnp.int32, (rows, rows), 1)
    quarter = lax.axis_index("rep")
    return [wanted == (lane + place(quarter, s, parts) * rows).astype(F32) for s in range(parts)]


def scores_kernel(parts, scale, positive, *refs):
    images, texts = refs[:STEPS], refs[STEPS : STEPS + parts]
    scores, img_out, txt_out, row_stats, col_stats, row_pos = refs[STEPS + parts :]
    rows = images[0].shape[0]
    factor = scale[0]
    eye = diagonal(rows)
    onehot = onehot_of(positive[...], eye, parts, rows)
    for s in range(parts):
        store_units(texts[s], txt_out, s * rows)
    for k in range(STEPS):
        store_units(images[k], img_out, k * rows)
    scores[...] = factor * lax.dot_general(
        img_out[...], txt_out[...], (((1,), (1,)), ((), ())), preferred_element_type=F32
    )
    peaks, sums = [], []
    for k in range(STEPS):
        tile = scores[k * rows : (k + 1) * rows, :]
        peak = jnp.max(tile, axis=1, keepdims=True)
        peaks.append(to_lanes(peak, eye))
        sums.append(to_lanes(jnp.sum(jnp.exp(tile - peak), axis=1, keepdims=True), eye))
    row_stats[...] = jnp.concatenate(peaks + sums, axis=0)
    peaks, sums, picked = [], [], []
    found = jnp.zeros((rows, 1), F32)
    for s in range(parts):
        tile = scores[:, s * rows : (s + 1) * rows]
        peak = jnp.max(tile, axis=0, keepdims=True)
        peaks.append(peak)
        sums.append(jnp.sum(jnp.exp(tile - peak), axis=0, keepdims=True))
        chosen = jnp.where(onehot[s], tile[:rows, :], 0.0)
        picked.append(jnp.sum(chosen, axis=0, keepdims=True))
        found = found + jnp.sum(chosen, axis=1, keepdims=True)
    row_pos[...] = to_lanes(found, eye)
    col_stats[...] = jnp.concatenate(peaks + sums + picked, axis=0)


def merged(pairs):
    peak = functools.reduce(jnp.maximum, [p for p, _ in pairs])
    return peak + jnp.log(sum(s * jnp.exp(p - peak) for p, s in pairs))


def weights_kernel(parts, positive, scores, images, row_pos, *refs):
    row_stats, col_stats = refs[: 2 * STEPS - 1], refs[2 * STEPS - 1 : 2 * STEPS - 1 + parts]
    row_loss, col_loss, weights, *txt_parts = refs[2 * STEPS - 1 + parts :]
    rows = row_pos.shape[1]
    eye = diagonal(rows)
    onehot = onehot_of(positive[...], eye, parts, rows)

    def row_pair(shift, k):
        table = row_stats[shift + STEPS - 1]
        at = k + shift
        return table[at : at + 1, :], table[STEPS + at : STEPS + at + 1, :]

    row_lse = []
    for k in range(STEPS):
        lse = merged([row_pair(t, k) for t in range(1 - STEPS, STEPS) if 0 <= k + t < STEPS])
        if k == 0:
            row_loss[...] = lse - row_pos[...]
        row_lse.append(to_column(lse, eye))
    col_lse = []
    for s in range(parts):
        at = [(t, slot_at(s, t, parts)) for t in range(parts)]
        lse = merged(
            [(col_stats[t][q : q + 1, :], col_stats[t][parts + q : parts + q + 1, :]) for t, q in at]
        )
        if s == 0:
            picked = sum(col_stats[t][2 * parts + q : 2 * parts + q + 1, :] for t, q in at)
            col_loss[...] = lse - picked
        col_lse.append(lse)
    for s in range(parts):
        for k in range(STEPS):
            tile = scores[k * rows : (k + 1) * rows, s * rows : (s + 1) * rows]
            weight = 0.5 * (jnp.exp(tile - row_lse[k]) + jnp.exp(tile - col_lse[s]))
            if k == 0:
                weight = weight - onehot[s].astype(F32)
            weights[k * rows : (k + 1) * rows, s * rows : (s + 1) * rows] = weight.astype(BF16)
    for s in range(parts):
        part = lax.dot_general(
            weights[:, s * rows : (s + 1) * rows],
            images[...],
            (((0,), (0,)), ((), ())),
            preferred_element_type=F32,
        )
        txt_parts[s][...] = part.astype(txt_parts[s].dtype)


def images_kernel(weights, texts, *img_parts):
    rows = img_parts[0].shape[0]
    for k in range(STEPS):
        part = jnp.dot(
            weights[k * rows : (k + 1) * rows, :], texts[...], preferred_element_type=F32
        )
        img_parts[k][...] = part.astype(img_parts[k].dtype)


def final_kernel(scale, raw, *refs):
    grad = refs[-1]
    factor = scale[0]
    for at in range(0, raw.shape[0], CHUNK):
        chunk = slice(at, at + CHUNK)
        wide = raw[chunk, :].astype(F32)
        inverse = inverse_norm(wide)
        unit = wide * inverse
        total = factor * sum(part[chunk, :].astype(F32) for part in refs[:-1])
        along = jnp.sum(unit * total, axis=-1, keepdims=True)
        grad[chunk, :] = (total - unit * along) * inverse


def call(kernel, outs, specs, args):
    return pl.pallas_call(
        kernel,
        out_shape=outs,
        in_specs=[pl.BlockSpec(memory_space=space) for space in specs],
        out_specs=jax.tree.map(lambda _: pl.BlockSpec(memory_space=VMEM), outs),
        compiler_params=pltpu.CompilerParams(vmem_limit_bytes=16 << 20),
    )(*args)


def on_device(image, text, positive, logit_scale):
    rows, width = image.shape
    parts = lax.axis_size("rep")
    shape = jax.ShapeDtypeStruct
    texts = [text] + [fetched(text, "rep", s) for s in range(1, parts)]
    images = [image] + [passed_along(image, "blk", -k) for k in range(1, STEPS)]
    scores, img_tiles, txt_tiles, row_stats, col_stats, row_pos = call(
        functools.partial(scores_kernel, parts),
        (
            shape((STEPS * rows, parts * rows), F32),
            shape((STEPS * rows, width), BF16),
            shape((parts * rows, width), BF16),
            shape((2 * STEPS, rows), F32),
            shape((3 * parts, rows), F32),
            shape((1, rows), F32),
        ),
        [SMEM] + [VMEM] * (1 + STEPS + parts),
        (logit_scale, positive, *images, *texts),
    )
    col_tables = [col_stats] + [fetched(col_stats, "rep", t) for t in range(1, parts)]
    row_tables = [
        row_stats if t == 0 else passed_along(row_stats, "blk", t)
        for t in range(1 - STEPS, STEPS)
    ]
    row_loss, col_loss, weights, *txt_parts = call(
        functools.partial(weights_kernel, parts),
        (
            shape((1, rows), F32),
            shape((1, rows), F32),
            shape((STEPS * rows, parts * rows), BF16),
            *[shape((rows, width), BF16 if s else F32) for s in range(parts)],
        ),
        [VMEM] * (4 + 2 * STEPS - 1 + parts),
        (positive, scores, img_tiles, row_pos, *row_tables, *col_tables),
    )
    txt_sums = [txt_parts[0]] + [returned(txt_parts[s], "rep", s) for s in range(1, parts)]
    img_parts = call(
        images_kernel,
        [shape((rows, width), BF16 if k else F32) for k in range(STEPS)],
        [VMEM] * 2,
        (weights, txt_tiles),
    )
    img_sums = [img_parts[0]] + [passed_along(img_parts[k], "blk", k) for k in range(1, STEPS)]
    grads = [
        call(
            final_kernel,
            shape((rows, width), F32),
            [SMEM] + [VMEM] * (1 + len(sums)),
            (logit_scale, raw, *sums),
        )
        for raw, sums in ((image, img_sums), (text, txt_sums))
    ]
    return (row_loss[0], col_loss[0], *grads)


def solution(mesh):
    placed = (P(("blk", "rep"), None), P(("blk", "rep"), None), P("blk", "rep"), P())

    return jax.shard_map(
        on_device,
        mesh=mesh,
        in_specs=placed,
        out_specs=(
            P(("blk", "rep")),
            P(("blk", "rep")),
            P(("blk", "rep"), None),
            P(("blk", "rep"), None),
        ),
        check_vma=False,
    )
```

time: 88.3 us -> 80.8 us (0.915); the launches traced: 88.1 us -> 79.1 us
  Pallas kernels: 13.8 us -> 6.21 us
  starting transfers between devices: 29.5 us -> 32.8 us
  waiting for transfers between devices: 39.8 us -> 36.9 us
  local copies, waits for them, and re-layouts: 3.47 us -> 1.91 us
    ppermute x21 -> x12, waiting for transfers between devices: 39.8 us -> 15.8 us  [passed_along(): lax.ppermute(array, axis, [(i, (i + by) % count) for i in range(count)])]
    ppermute x0 -> x9, waiting for transfers between devices: none -> 21 us  [the longest x6 14.8 us: fetched(): lax.ppermute(array, axis, [(place(i, slot, count), i) for i in range(coun...]
    ppermute x0 -> x9, starting transfers between devices: none -> 16.6 us  [the longest x6 9.38 us: fetched(): lax.ppermute(array, axis, [(place(i, slot, count), i) for i in range(coun...]
    ppermute x21 -> x12, starting transfers between devices: 29.5 us -> 16.2 us  [passed_along(): lax.ppermute(array, axis, [(i, (i + by) % count) for i in range(count)])]
    pallas_call x4 -> x5, Pallas kernels: 13.8 us -> 6.21 us  [call(): pl.pallas_call(kernel, out_shape=outs, in_specs=[pl.BlockSpec(memory_spac...]
    unnamed x42 -> x10, local copies, waits for them, and re-layouts: 3.47 us -> 1.91 us
  transfers between devices with their start and end apart: 21 -> 21, of which waited for: 9 -> 9; matrix products, arithmetic and copies ran while one was open for 0% -> 0% of each run, Pallas kernels for 3% -> 1%
where the time goes in v2:
time: 80.8 us; the launch traced here: 79.1 us
  waiting for transfers between devices  36.9 us (46%)
  starting transfers between devices  32.8 us (41%)
  Pallas kernels  6.21 us (8%)
  local copies, waits for them, and re-layouts  1.91 us (2%)
  between operations  1.35 us (2%)
    ppermute x12, starting transfers between devices, passed_along(): lax.ppermute(array, axis, [(i, (i + by) % count) for i in range(count)])  16.2 us
    ppermute x12, waiting for transfers between devices, passed_along(): lax.ppermute(array, axis, [(i, (i + by) % count) for i in range(count)])  15.8 us
    ppermute x6, waiting for transfers between devices, fetched(): lax.ppermute(array, axis, [(place(i, slot, count), i) for i in range(coun...  14.8 us
    ppermute x6, starting transfers between devices, fetched(): lax.ppermute(array, axis, [(place(i, slot, count), i) for i in range(coun...  9.38 us
    ppermute x3, starting transfers between devices, returned(): lax.ppermute(array, axis, [(i, place(i, slot, count)) for i in range(coun...  7.24 us
    ppermute x3, waiting for transfers between devices, returned(): lax.ppermute(array, axis, [(i, place(i, slot, count)) for i in range(coun...  6.26 us
    pallas_call x5, Pallas kernels, call(): pl.pallas_call(kernel, out_shape=outs, in_specs=[pl.BlockSpec(memory_spac...  6.21 us
    unnamed x10, local copies, waits for them, and re-layouts  1.91 us
  transfers between devices with their start and end apart: 21, of which 9 were waited for; matrix products, arithmetic and copies ran while one was open for 0% of the time, Pallas kernels for 1%

profile of v2, /device:TPU:0, one launch (start us, length us, event | category | flops | bytes accessed | tf_op | source)
XLA Modules:
  0.0 79.1 jit_solution(15884006194474078152)
XLA Ops:
  0.6 2.5 %collective-permute-start.2 = (bf16[128,1024]{1,0:T(8,128)(2,1)}, bf16[128,1024]{1,0:T(8,128)(2,1)S(1)}, u32[]{:S(2)}, u32[]{:S(2)}) collective-permute-start(bf16[128,1024]{1,0:T(8,128)(2,1)} %raw.2), channel_id=1, source_target_pairs={{0,20},{4,24},{8,28},{12,0},{16,4},{20,8},{24,12},{28,16},{1,21},{... | collective-permute-start | bytes 786440 | tf_op jit(solution)/shard_map/ppermute | solution.py:42
  3.1 1.6 %collective-permute-start.1 = (bf16[128,1024]{1,0:T(8,128)(2,1)}, bf16[128,1024]{1,0:T(8,128)(2,1)S(1)}, u32[]{:S(2)}, u32[]{:S(2)}) collective-permute-start(bf16[128,1024]{1,0:T(8,128)(2,1)} %raw.2), channel_id=1, source_target_pairs={{0,24},{4,28},{8,0},{12,4},{16,8},{20,12},{24,16},{28,20},{1,25},{... | collective-permute-start | bytes 786440 | tf_op jit(solution)/shard_map/ppermute | solution.py:42
  4.7 1.3 %collective-permute-start = (bf16[128,1024]{1,0:T(8,128)(2,1)}, bf16[128,1024]{1,0:T(8,128)(2,1)S(1)}, u32[]{:S(2)}, u32[]{:S(2)}) collective-permute-start(bf16[128,1024]{1,0:T(8,128)(2,1)} %raw.2), channel_id=1, source_target_pairs={{0,28},{4,0},{8,4},{12,8},{16,12},{20,16},{24,20},{28,24},{1,29},{... | collective-permute-start | bytes 786440 | tf_op jit(solution)/shard_map/ppermute | solution.py:42
  6.0 3.6 %collective-permute-start.5 = (bf16[128,1024]{1,0:T(8,128)(2,1)}, bf16[128,1024]{1,0:T(8,128)(2,1)S(1)}, u32[]{:S(2)}, u32[]{:S(2)}) collective-permute-start(bf16[128,1024]{1,0:T(8,128)(2,1)} %raw.3), channel_id=1, source_target_pairs={{3,0},{2,1},{1,2},{0,3},{7,4},{6,5},{5,6},{4,7},{11,8},{10,9},{9,1... | collective-permute-start | bytes 786440 | tf_op jit(solution)/shard_map/ppermute | solution.py:32
  9.6 1.4 %collective-permute-start.3 = (bf16[128,1024]{1,0:T(8,128)(2,1)}, bf16[128,1024]{1,0:T(8,128)(2,1)S(1)}, u32[]{:S(2)}, u32[]{:S(2)}) collective-permute-start(bf16[128,1024]{1,0:T(8,128)(2,1)} %raw.3), channel_id=1, source_target_pairs={{1,0},{0,1},{3,2},{2,3},{5,4},{4,5},{7,6},{6,7},{9,8},{8,9},{11,10... | collective-permute-start | bytes 786440 | tf_op jit(solution)/shard_map/ppermute | solution.py:32
  11.7 0.8 %collective-permute-done.1.refs_2_ = bf16[128,1024]{1,0:T(8,128)(2,1)S(1)} collective-permute-done((bf16[128,1024]{1,0:T(8,128)(2,1)}, bf16[128,1024]{1,0:T(8,128)(2,1)S(1)}, u32[]{:S(2)}, u32[]{:S(2)}) %collective-permute-start.1) | collective-permute-done | bytes 262176 | tf_op jit(solution)/shard_map/ppermute | solution.py:42
  12.5 4.2 %collective-permute-done.refs_1_ = bf16[128,1024]{1,0:T(8,128)(2,1)S(1)} collective-permute-done((bf16[128,1024]{1,0:T(8,128)(2,1)}, bf16[128,1024]{1,0:T(8,128)(2,1)S(1)}, u32[]{:S(2)}, u32[]{:S(2)}) %collective-permute-start) | collective-permute-done | bytes 262176 | tf_op jit(solution)/shard_map/ppermute | solution.py:42
  16.7 0.5 collective-permute-done.5.refs_7_
  17.3 14.2 %collective-permute-done.4.refs_6_ = bf16[128,1024]{1,0:T(8,128)(2,1)S(1)} collective-permute-done((bf16[128,1024]{1,0:T(8,128)(2,1)}, bf16[128,1024]{1,0:T(8,128)(2,1)S(1)}, u32[]{:S(2)}, u32[]{:S(2)}) %collective-permute-start.4) | collective-permute-done | bytes 262176 | tf_op jit(solution)/shard_map/ppermute | solution.py:32
  31.5 0.9 %copy-done = bf16[128,1024]{1,0:T(8,128)(2,1)S(1)} copy-done((bf16[128,1024]{1,0:T(8,128)(2,1)S(1)}, bf16[128,1024]{1,0:T(8,128)(2,1)}, u32[]{:S(2)}) %copy-start) | copy-done | bytes 262168
  32.4 0.9 %copy-done.2 = bf16[128,1024]{1,0:T(8,128)(2,1)S(1)} copy-done((bf16[128,1024]{1,0:T(8,128)(2,1)S(1)}, bf16[128,1024]{1,0:T(8,128)(2,1)}, u32[]{:S(2)}) %copy-start.2) | copy-done | bytes 262168
  33.4 1.6 %shard_map.75 = (f32[512,512]{1,0:T(8,128)S(1)}, bf16[512,1024]{1,0:T(8,128)(2,1)S(1)}, bf16[512,1024]{1,0:T(8,128)(2,1)S(1)}, f32[8,128]{1,0:T(8,128)S(1)}, f32...) custom-call(f32[1]{0:T(128)S(6)} %copy.8.scale, s32[1,128]{1,0:T(1,128)S(1)} %copy-done.4, bf16[128,1024]{1,0:T(8,128)(2,1)S(1)} %copy-done, ...), custom_call_target="tpu_custom_call" | custom-call | tf_op jit(solution)/shard_map/pallas_call | solution.py:184
  35.0 3.2 %collective-permute-start.11 = (f32[8,128]{1,0:T(8,128)S(1)}, f32[8,128]{1,0:T(8,128)S(1)}, u32[]{:S(2)}, u32[]{:S(2)}) collective-permute-start(f32[8,128]{1,0:T(8,128)S(1)} %get-tuple-element.24.refs_3_), channel_id=1, source_target_pairs={{0,12},{4,16},{8,20},{12,24},{16,28},{20,0},{24,4},{28,8},{1,13},{... | collective-permute-start | bytes 12296 | tf_op jit(solution)/shard_map/ppermute | solution.py:42
  38.2 0.5 collective-permute-start.10
  38.6 2.6 %collective-permute-start.8 = (f32[8,128]{1,0:T(8,128)S(1)}, f32[8,128]{1,0:T(8,128)S(1)}, u32[]{:S(2)}, u32[]{:S(2)}) collective-permute-start(f32[8,128]{1,0:T(8,128)S(1)} %get-tuple-element.24.refs_3_), channel_id=1, source_target_pairs={{0,28},{4,0},{8,4},{12,8},{16,12},{20,16},{24,20},{28,24},{1,29},{... | collective-permute-start | bytes 12296 | tf_op jit(solution)/shard_map/ppermute | solution.py:42
  41.3 3.5 %collective-permute-start.14 = (f32[12,128]{1,0:T(8,128)S(1)}, f32[12,128]{1,0:T(8,128)S(1)}, u32[]{:S(2)}, u32[]{:S(2)}) collective-permute-start(f32[12,128]{1,0:T(8,128)S(1)} %get-tuple-element.25.refs_7_), channel_id=1, source_target_pairs={{3,0},{2,1},{1,2},{0,3},{7,4},{6,5},{5,6},{4,7},{11,8},{10,9},{9,1... | collective-permute-start | bytes 18440 | tf_op jit(solution)/shard_map/ppermute | solution.py:32
  44.8 0.9 %collective-permute-start.12 = (f32[12,128]{1,0:T(8,128)S(1)}, f32[12,128]{1,0:T(8,128)S(1)}, u32[]{:S(2)}, u32[]{:S(2)}) collective-permute-start(f32[12,128]{1,0:T(8,128)S(1)} %get-tuple-element.25.refs_7_), channel_id=1, source_target_pairs={{1,0},{0,1},{3,2},{2,3},{5,4},{4,5},{7,6},{6,7},{9,8},{8,9},{11,10... | collective-permute-start | bytes 18440 | tf_op jit(solution)/shard_map/ppermute | solution.py:32
  45.7 1.6 %collective-permute-start.7 = (f32[8,128]{1,0:T(8,128)S(1)}, f32[8,128]{1,0:T(8,128)S(1)}, u32[]{:S(2)}, u32[]{:S(2)}) collective-permute-start(f32[8,128]{1,0:T(8,128)S(1)} %get-tuple-element.24.refs_3_), channel_id=1, source_target_pairs={{0,24},{4,28},{8,0},{12,4},{16,8},{20,12},{24,16},{28,20},{1,25},{... | collective-permute-start | bytes 12296 | tf_op jit(solution)/shard_map/ppermute | solution.py:42
  47.2 2.0 %collective-permute-done.7.refs_1_ = f32[8,128]{1,0:T(8,128)S(1)} collective-permute-done((f32[8,128]{1,0:T(8,128)S(1)}, f32[8,128]{1,0:T(8,128)S(1)}, u32[]{:S(2)}, u32[]{:S(2)}) %collective-permute-start.7) | collective-permute-done | bytes 4128 | tf_op jit(solution)/shard_map/ppermute | solution.py:42
  49.3 1.0 %collective-permute-done.6.refs_0_ = f32[8,128]{1,0:T(8,128)S(1)} collective-permute-done((f32[8,128]{1,0:T(8,128)S(1)}, f32[8,128]{1,0:T(8,128)S(1)}, u32[]{:S(2)}, u32[]{:S(2)}) %collective-permute-start.6) | collective-permute-done | bytes 4128 | tf_op jit(solution)/shard_map/ppermute | solution.py:42
  50.3 1.6 %shard_map.76 = (f32[1,128]{1,0:T(1,128)}, f32[1,128]{1,0:T(1,128)}, bf16[512,512]{1,0:T(8,128)(2,1)S(1)}, f32[128,1024]{1,0:T(8,128)S(1)}, bf16[128,1024]{1,0:T...) custom-call(s32[1,128]{1,0:T(1,128)S(1)} %copy-done.4, ...), custom_call_target="tpu_custom_call" | custom-call | tf_op jit(solution)/shard_map/pallas_call | solution.py:184
  51.9 0.8 shard_map.77
  52.7 1.4 %collective-permute-start.16 = (bf16[128,1024]{1,0:T(8,128)(2,1)S(1)}, bf16[128,1024]{1,0:T(8,128)(2,1)S(1)}, u32[]{:S(2)}, u32[]{:S(2)}) collective-permute-start(bf16[128,1024]{1,0:T(8,128)(2,1)S(1)} %get-tuple-element.32), channel_id=1, source_target_pairs={{0,8},{4,12},{8,16},{12,20},{16,24},{20,28},{24,0},{28,4},{1,9},{5... | collective-permute-start | bytes 786440 | tf_op jit(solution)/shard_map/ppermute | solution.py:42
  54.1 1.5 %collective-permute-start.17 = (bf16[128,1024]{1,0:T(8,128)(2,1)S(1)}, bf16[128,1024]{1,0:T(8,128)(2,1)S(1)}, u32[]{:S(2)}, u32[]{:S(2)}) collective-permute-start(bf16[128,1024]{1,0:T(8,128)(2,1)S(1)} %get-tuple-element.33), channel_id=1, source_target_pairs={{0,12},{4,16},{8,20},{12,24},{16,28},{20,0},{24,4},{28,8},{1,13},{... | collective-permute-start | bytes 786440 | tf_op jit(solution)/shard_map/ppermute | solution.py:42
  55.7 1.0 %collective-permute-start.18 = (bf16[128,1024]{1,0:T(8,128)(2,1)S(1)}, bf16[128,1024]{1,0:T(8,128)(2,1)S(1)}, u32[]{:S(2)}, u32[]{:S(2)}) collective-permute-start(bf16[128,1024]{1,0:T(8,128)(2,1)S(1)} %get-tuple-element.35), channel_id=1, source_target_pairs={{0,1},{1,0},{2,3},{3,2},{4,5},{5,4},{6,7},{7,6},{8,9},{9,8},{10,11... | collective-permute-start | bytes 786440 | tf_op jit(solution)/shard_map/ppermute | solution.py:37
  56.7 2.9 %collective-permute-start.19 = (bf16[128,1024]{1,0:T(8,128)(2,1)S(1)}, bf16[128,1024]{1,0:T(8,128)(2,1)S(1)}, u32[]{:S(2)}, u32[]{:S(2)}) collective-permute-start(bf16[128,1024]{1,0:T(8,128)(2,1)S(1)} %get-tuple-element.36), channel_id=1, source_target_pairs={{0,2},{1,3},{2,0},{3,1},{4,6},{5,7},{6,4},{7,5},{8,10},{9,11},{10,... | collective-permute-start | bytes 786440 | tf_op jit(solution)/shard_map/ppermute | solution.py:37
  59.6 2.1 %collective-permute-done.15.refs_1_ = bf16[128,1024]{1,0:T(8,128)(2,1)S(1)} collective-permute-done((bf16[128,1024]{1,0:T(8,128)(2,1)S(1)}, bf16[128,1024]{1,0:T(8,128)(2,1)S(1)}, u32[]{:S(2)}, u32[]{:S(2)}) %collective-permute-start.15) | collective-permute-done | bytes 262176 | tf_op jit(solution)/shard_map/ppermute | solution.py:42
  61.7 3.3 %collective-permute-start.20 = (bf16[128,1024]{1,0:T(8,128)(2,1)S(1)}, bf16[128,1024]{1,0:T(8,128)(2,1)S(1)}, u32[]{:S(2)}, u32[]{:S(2)}) collective-permute-start(bf16[128,1024]{1,0:T(8,128)(2,1)S(1)} %get-tuple-element.37), channel_id=1, source_target_pairs={{0,3},{1,2},{2,1},{3,0},{4,7},{5,6},{6,5},{7,4},{8,11},{9,10},{10,... | collective-permute-start | bytes 786440 | tf_op jit(solution)/shard_map/ppermute | solution.py:37
  65.0 5.6 %collective-permute-done.17.refs_3_ = bf16[128,1024]{1,0:T(8,128)(2,1)S(1)} collective-permute-done((bf16[128,1024]{1,0:T(8,128)(2,1)S(1)}, bf16[128,1024]{1,0:T(8,128)(2,1)S(1)}, u32[]{:S(2)}, u32[]{:S(2)}) %collective-permute-start.17) | collective-permute-done | bytes 262176 | tf_op jit(solution)/shard_map/ppermute | solution.py:42
  70.7 1.1 %shard_map.78 = f32[128,1024]{1,0:T(8,128)} custom-call(f32[1]{0:T(128)S(6)} %copy.8.scale, bf16[128,1024]{1,0:T(8,128)(2,1)S(1)} %copy-done.1, f32[128,1024]{1,0:T(8,128)S(1)} %get-tuple-element.30.refs_0_, bf16[128,1024]{1,0:T(8,128)(2,1)S(1)} %collective-permute-done.15.refs_1_, bf16[128,1024]{1,0:T(8,128)(2,1)S(1)} %collective-permute-done.16.refs_2_, ...), custom_call_target="tpu_custom_call" | custom-call | tf_op jit(solution)/shard_map/pallas_call | solution.py:184
  71.8 6.3 %collective-permute-done.19.refs_2_ = bf16[128,1024]{1,0:T(8,128)(2,1)S(1)} collective-permute-done((bf16[128,1024]{1,0:T(8,128)(2,1)S(1)}, bf16[128,1024]{1,0:T(8,128)(2,1)S(1)}, u32[]{:S(2)}, u32[]{:S(2)}) %collective-permute-start.19) | collective-permute-done | bytes 262176 | tf_op jit(solution)/shard_map/ppermute | solution.py:37
  78.0 1.1 %shard_map.79 = f32[128,1024]{1,0:T(8,128)} custom-call(f32[1]{0:T(128)S(6)} %copy.8.scale, bf16[128,1024]{1,0:T(8,128)(2,1)S(1)} %copy-done.3, f32[128,1024]{1,0:T(8,128)S(1)} %get-tuple-element.34.refs_0_, bf16[128,1024]{1,0:T(8,128)(2,1)S(1)} %collective-permute-done.18.refs_1_, bf16[128,1024]{1,0:T(8,128)(2,1)S(1)} %collective-permute-done.19.refs_2_, ...), custom_call_target="tpu_custom_call" | custom-call | tf_op jit(solution)/shard_map/pallas_call | solution.py:184
  (25 shorter events, 0.1 us)
Async XLA Ops:
  0.6 30.9 %copy-start.4 = (s32[1,128]{1,0:T(1,128)S(1)}, s32[1,128]{1,0:T(1,128)}, u32[]{:S(2)}) copy-start(s32[1,128]{1,0:T(1,128)} %positive.3) | copy-start | bytes 1540
  0.6 9.0 %collective-permute-start.2 = (bf16[128,1024]{1,0:T(8,128)(2,1)}, bf16[128,1024]{1,0:T(8,128)(2,1)S(1)}, u32[]{:S(2)}, u32[]{:S(2)}) collective-permute-start(bf16[128,1024]{1,0:T(8,128)(2,1)} %raw.2), channel_id=1, source_target_pairs={{0,20},{4,24},{8,28},{12,0},{16,4},{20,8},{24,12},{28,16},{1,21},{... | collective-permute-start | bytes 786440 | tf_op jit(solution)/shard_map/ppermute | solution.py:42
  3.1 9.4 %collective-permute-start.1 = (bf16[128,1024]{1,0:T(8,128)(2,1)}, bf16[128,1024]{1,0:T(8,128)(2,1)S(1)}, u32[]{:S(2)}, u32[]{:S(2)}) collective-permute-start(bf16[128,1024]{1,0:T(8,128)(2,1)} %raw.2), channel_id=1, source_target_pairs={{0,24},{4,28},{8,0},{12,4},{16,8},{20,12},{24,16},{28,20},{1,25},{... | collective-permute-start | bytes 786440 | tf_op jit(solution)/shard_map/ppermute | solution.py:42
  4.7 12.0 %collective-permute-start = (bf16[128,1024]{1,0:T(8,128)(2,1)}, bf16[128,1024]{1,0:T(8,128)(2,1)S(1)}, u32[]{:S(2)}, u32[]{:S(2)}) collective-permute-start(bf16[128,1024]{1,0:T(8,128)(2,1)} %raw.2), channel_id=1, source_target_pairs={{0,28},{4,0},{8,4},{12,8},{16,12},{20,16},{24,20},{28,24},{1,29},{... | collective-permute-start | bytes 786440 | tf_op jit(solution)/shard_map/ppermute | solution.py:42
  6.0 11.2 %collective-permute-start.5 = (bf16[128,1024]{1,0:T(8,128)(2,1)}, bf16[128,1024]{1,0:T(8,128)(2,1)S(1)}, u32[]{:S(2)}, u32[]{:S(2)}) collective-permute-start(bf16[128,1024]{1,0:T(8,128)(2,1)} %raw.3), channel_id=1, source_target_pairs={{3,0},{2,1},{1,2},{0,3},{7,4},{6,5},{5,6},{4,7},{11,8},{10,9},{9,1... | collective-permute-start | bytes 786440 | tf_op jit(solution)/shard_map/ppermute | solution.py:32
  9.6 21.9 %collective-permute-start.4 = (bf16[128,1024]{1,0:T(8,128)(2,1)}, bf16[128,1024]{1,0:T(8,128)(2,1)S(1)}, u32[]{:S(2)}, u32[]{:S(2)}) collective-permute-start(bf16[128,1024]{1,0:T(8,128)(2,1)} %raw.3), channel_id=1, source_target_pairs={{2,0},{3,1},{0,2},{1,3},{6,4},{7,5},{4,6},{5,7},{10,8},{11,9},{8,1... | collective-permute-start | bytes 786440 | tf_op jit(solution)/shard_map/ppermute | solution.py:32
  9.6 21.9 %collective-permute-start.3 = (bf16[128,1024]{1,0:T(8,128)(2,1)}, bf16[128,1024]{1,0:T(8,128)(2,1)S(1)}, u32[]{:S(2)}, u32[]{:S(2)}) collective-permute-start(bf16[128,1024]{1,0:T(8,128)(2,1)} %raw.3), channel_id=1, source_target_pairs={{1,0},{0,1},{3,2},{2,3},{5,4},{4,5},{7,6},{6,7},{9,8},{8,9},{11,10... | collective-permute-start | bytes 786440 | tf_op jit(solution)/shard_map/ppermute | solution.py:32
  31.5 1.0 %copy-start = (bf16[128,1024]{1,0:T(8,128)(2,1)S(1)}, bf16[128,1024]{1,0:T(8,128)(2,1)}, u32[]{:S(2)}) copy-start(bf16[128,1024]{1,0:T(8,128)(2,1)} %raw.2) | copy-start | bytes 786436
  32.4 0.9 %copy-start.2 = (bf16[128,1024]{1,0:T(8,128)(2,1)S(1)}, bf16[128,1024]{1,0:T(8,128)(2,1)}, u32[]{:S(2)}) copy-start(bf16[128,1024]{1,0:T(8,128)(2,1)} %raw.3) | copy-start | bytes 786436
  35.0 9.7 %collective-permute-start.11 = (f32[8,128]{1,0:T(8,128)S(1)}, f32[8,128]{1,0:T(8,128)S(1)}, u32[]{:S(2)}, u32[]{:S(2)}) collective-permute-start(f32[8,128]{1,0:T(8,128)S(1)} %get-tuple-element.24.refs_3_), channel_id=1, source_target_pairs={{0,12},{4,16},{8,20},{12,24},{16,28},{20,0},{24,4},{28,8},{1,13},{... | collective-permute-start | bytes 12296 | tf_op jit(solution)/shard_map/ppermute | solution.py:42
  38.2 6.6 %collective-permute-start.10 = (f32[8,128]{1,0:T(8,128)S(1)}, f32[8,128]{1,0:T(8,128)S(1)}, u32[]{:S(2)}, u32[]{:S(2)}) collective-permute-start(f32[8,128]{1,0:T(8,128)S(1)} %get-tuple-element.24.refs_3_), channel_id=1, source_target_pairs={{0,8},{4,12},{8,16},{12,20},{16,24},{20,28},{24,0},{28,4},{1,9},{5... | collective-permute-start | bytes 12296 | tf_op jit(solution)/shard_map/ppermute | solution.py:42
  38.6 7.0 %collective-permute-start.9 = (f32[8,128]{1,0:T(8,128)S(1)}, f32[8,128]{1,0:T(8,128)S(1)}, u32[]{:S(2)}, u32[]{:S(2)}) collective-permute-start(f32[8,128]{1,0:T(8,128)S(1)} %get-tuple-element.24.refs_3_), channel_id=1, source_target_pairs={{0,4},{4,8},{8,12},{12,16},{16,20},{20,24},{24,28},{28,0},{1,5},{5... | collective-permute-start | bytes 12296 | tf_op jit(solution)/shard_map/ppermute | solution.py:42
  38.6 8.6 %collective-permute-start.8 = (f32[8,128]{1,0:T(8,128)S(1)}, f32[8,128]{1,0:T(8,128)S(1)}, u32[]{:S(2)}, u32[]{:S(2)}) collective-permute-start(f32[8,128]{1,0:T(8,128)S(1)} %get-tuple-element.24.refs_3_), channel_id=1, source_target_pairs={{0,28},{4,0},{8,4},{12,8},{16,12},{20,16},{24,20},{28,24},{1,29},{... | collective-permute-start | bytes 12296 | tf_op jit(solution)/shard_map/ppermute | solution.py:42
  41.3 9.0 %collective-permute-start.14 = (f32[12,128]{1,0:T(8,128)S(1)}, f32[12,128]{1,0:T(8,128)S(1)}, u32[]{:S(2)}, u32[]{:S(2)}) collective-permute-start(f32[12,128]{1,0:T(8,128)S(1)} %get-tuple-element.25.refs_7_), channel_id=1, source_target_pairs={{3,0},{2,1},{1,2},{0,3},{7,4},{6,5},{5,6},{4,7},{11,8},{10,9},{9,1... | collective-permute-start | bytes 18440 | tf_op jit(solution)/shard_map/ppermute | solution.py:32
  44.7 5.5 %collective-permute-start.13 = (f32[12,128]{1,0:T(8,128)S(1)}, f32[12,128]{1,0:T(8,128)S(1)}, u32[]{:S(2)}, u32[]{:S(2)}) collective-permute-start(f32[12,128]{1,0:T(8,128)S(1)} %get-tuple-element.25.refs_7_), channel_id=1, source_target_pairs={{2,0},{3,1},{0,2},{1,3},{6,4},{7,5},{4,6},{5,7},{10,8},{11,9},{8,1... | collective-permute-start | bytes 18440 | tf_op jit(solution)/shard_map/ppermute | solution.py:32
  44.8 5.5 %collective-permute-start.12 = (f32[12,128]{1,0:T(8,128)S(1)}, f32[12,128]{1,0:T(8,128)S(1)}, u32[]{:S(2)}, u32[]{:S(2)}) collective-permute-start(f32[12,128]{1,0:T(8,128)S(1)} %get-tuple-element.25.refs_7_), channel_id=1, source_target_pairs={{1,0},{0,1},{3,2},{2,3},{5,4},{4,5},{7,6},{6,7},{9,8},{8,9},{11,10... | collective-permute-start | bytes 18440 | tf_op jit(solution)/shard_map/ppermute | solution.py:32
  45.7 3.6 %collective-permute-start.7 = (f32[8,128]{1,0:T(8,128)S(1)}, f32[8,128]{1,0:T(8,128)S(1)}, u32[]{:S(2)}, u32[]{:S(2)}) collective-permute-start(f32[8,128]{1,0:T(8,128)S(1)} %get-tuple-element.24.refs_3_), channel_id=1, source_target_pairs={{0,24},{4,28},{8,0},{12,4},{16,8},{20,12},{24,16},{28,20},{1,25},{... | collective-permute-start | bytes 12296 | tf_op jit(solution)/shard_map/ppermute | solution.py:42
  47.2 3.0 %collective-permute-start.6 = (f32[8,128]{1,0:T(8,128)S(1)}, f32[8,128]{1,0:T(8,128)S(1)}, u32[]{:S(2)}, u32[]{:S(2)}) collective-permute-start(f32[8,128]{1,0:T(8,128)S(1)} %get-tuple-element.24.refs_3_), channel_id=1, source_target_pairs={{0,20},{4,24},{8,28},{12,0},{16,4},{20,8},{24,12},{28,16},{1,21},{... | collective-permute-start | bytes 12296 | tf_op jit(solution)/shard_map/ppermute | solution.py:42
  51.9 18.8 %copy-start.1 = (bf16[128,1024]{1,0:T(8,128)(2,1)S(1)}, bf16[128,1024]{1,0:T(8,128)(2,1)}, u32[]{:S(2)}) copy-start(bf16[128,1024]{1,0:T(8,128)(2,1)} %raw.2) | copy-start | bytes 786436
  52.7 9.0 %collective-permute-start.15 = (bf16[128,1024]{1,0:T(8,128)(2,1)S(1)}, bf16[128,1024]{1,0:T(8,128)(2,1)S(1)}, u32[]{:S(2)}, u32[]{:S(2)}) collective-permute-start(bf16[128,1024]{1,0:T(8,128)(2,1)S(1)} %get-tuple-element.31), channel_id=1, source_target_pairs={{0,4},{4,8},{8,12},{12,16},{16,20},{20,24},{24,28},{28,0},{1,5},{5... | collective-permute-start | bytes 786440 | tf_op jit(solution)/shard_map/ppermute | solution.py:42
  52.7 12.3 %collective-permute-start.16 = (bf16[128,1024]{1,0:T(8,128)(2,1)S(1)}, bf16[128,1024]{1,0:T(8,128)(2,1)S(1)}, u32[]{:S(2)}, u32[]{:S(2)}) collective-permute-start(bf16[128,1024]{1,0:T(8,128)(2,1)S(1)} %get-tuple-element.32), channel_id=1, source_target_pairs={{0,8},{4,12},{8,16},{12,20},{16,24},{20,28},{24,0},{28,4},{1,9},{5... | collective-permute-start | bytes 786440 | tf_op jit(solution)/shard_map/ppermute | solution.py:42
  54.1 16.5 %collective-permute-start.17 = (bf16[128,1024]{1,0:T(8,128)(2,1)S(1)}, bf16[128,1024]{1,0:T(8,128)(2,1)S(1)}, u32[]{:S(2)}, u32[]{:S(2)}) collective-permute-start(bf16[128,1024]{1,0:T(8,128)(2,1)S(1)} %get-tuple-element.33), channel_id=1, source_target_pairs={{0,12},{4,16},{8,20},{12,24},{16,28},{20,0},{24,4},{28,8},{1,13},{... | collective-permute-start | bytes 786440 | tf_op jit(solution)/shard_map/ppermute | solution.py:42
  55.7 16.1 %collective-permute-start.18 = (bf16[128,1024]{1,0:T(8,128)(2,1)S(1)}, bf16[128,1024]{1,0:T(8,128)(2,1)S(1)}, u32[]{:S(2)}, u32[]{:S(2)}) collective-permute-start(bf16[128,1024]{1,0:T(8,128)(2,1)S(1)} %get-tuple-element.35), channel_id=1, source_target_pairs={{0,1},{1,0},{2,3},{3,2},{4,5},{5,4},{6,7},{7,6},{8,9},{9,8},{10,11... | collective-permute-start | bytes 786440 | tf_op jit(solution)/shard_map/ppermute | solution.py:37
  56.7 21.3 %collective-permute-start.19 = (bf16[128,1024]{1,0:T(8,128)(2,1)S(1)}, bf16[128,1024]{1,0:T(8,128)(2,1)S(1)}, u32[]{:S(2)}, u32[]{:S(2)}) collective-permute-start(bf16[128,1024]{1,0:T(8,128)(2,1)S(1)} %get-tuple-element.36), channel_id=1, source_target_pairs={{0,2},{1,3},{2,0},{3,1},{4,6},{5,7},{6,4},{7,5},{8,10},{9,11},{10,... | collective-permute-start | bytes 786440 | tf_op jit(solution)/shard_map/ppermute | solution.py:37
  61.7 16.3 %collective-permute-start.20 = (bf16[128,1024]{1,0:T(8,128)(2,1)S(1)}, bf16[128,1024]{1,0:T(8,128)(2,1)S(1)}, u32[]{:S(2)}, u32[]{:S(2)}) collective-permute-start(bf16[128,1024]{1,0:T(8,128)(2,1)S(1)} %get-tuple-element.37), channel_id=1, source_target_pairs={{0,3},{1,2},{2,1},{3,0},{4,7},{5,6},{6,5},{7,4},{8,11},{9,10},{10,... | collective-permute-start | bytes 786440 | tf_op jit(solution)/shard_map/ppermute | solution.py:37
  70.7 7.4 %copy-start.3 = (bf16[128,1024]{1,0:T(8,128)(2,1)S(1)}, bf16[128,1024]{1,0:T(8,128)(2,1)}, u32[]{:S(2)}) copy-start(bf16[128,1024]{1,0:T(8,128)(2,1)} %raw.3) | copy-start | bytes 786436

commit v3 on v2

--- a/solution.py
+++ b/solution.py
@@ -42,6 +42,34 @@
     return lax.ppermute(array, axis, [(i, (i + by) % count) for i in range(count)])
 
 
+def table_rows(parts):
+    return -(-3 * parts // 8) * 8
+
+
+def doublings(reach):
+    known, rounds = 0, []
+    while known < reach:
+        shift = min(2 * known + 1, reach - known)
+        rounds.append((shift, known))
+        known += shift
+    return rounds
+
+
+def known_places(reach):
+    held = [[0]]
+    for shift, known in doublings(reach):
+        for centre in (shift, -shift):
+            held.append(list(range(centre - known, centre + known + 1)))
+    return held
+
+
+def slot_counts(parts):
+    counts = [1]
+    while sum(counts) < parts:
+        counts.append(min(sum(counts), parts - sum(counts)))
+    return counts
+
+
 def inverse_norm(wide):
     return lax.rsqrt(jnp.sum(wide * wide, axis=-1, keepdims=True) + 1e-06)
 
@@ -73,19 +101,16 @@
     return [wanted == (lane + place(quarter, s, parts) * rows).astype(F32) for s in range(parts)]
 
 
-def scores_kernel(parts, scale, positive, *refs):
-    images, texts = refs[:STEPS], refs[STEPS : STEPS + parts]
-    scores, img_out, txt_out, row_stats, col_stats, row_pos = refs[STEPS + parts :]
-    rows = images[0].shape[0]
-    factor = scale[0]
+def scores_kernel(parts, slots, factor, positive, images, texts, scores, txt_out, row_out, col_out):
+    rows = texts[0].shape[0]
     eye = diagonal(rows)
-    onehot = onehot_of(positive[...], eye, parts, rows)
-    for s in range(parts):
-        store_units(texts[s], txt_out, s * rows)
-    for k in range(STEPS):
-        store_units(images[k], img_out, k * rows)
+    wanted = to_column(positive.astype(F32), eye)
+    lane = lax.broadcasted_iota(jnp.int32, (rows, rows), 1)
+    quarter = lax.axis_index("rep")
+    for n, text in enumerate(texts):
+        store_units(text, txt_out, n * rows)
     scores[...] = factor * lax.dot_general(
-        img_out[...], txt_out[...], (((1,), (1,)), ((), ())), preferred_element_type=F32
+        images[...], txt_out[...], (((1,), (1,)), ((), ())), preferred_element_type=F32
     )
     peaks, sums = [], []
     for k in range(STEPS):
@@ -93,19 +118,49 @@
         peak = jnp.max(tile, axis=1, keepdims=True)
         peaks.append(to_lanes(peak, eye))
         sums.append(to_lanes(jnp.sum(jnp.exp(tile - peak), axis=1, keepdims=True), eye))
-    row_stats[...] = jnp.concatenate(peaks + sums, axis=0)
-    peaks, sums, picked = [], [], []
     found = jnp.zeros((rows, 1), F32)
-    for s in range(parts):
-        tile = scores[:, s * rows : (s + 1) * rows]
+    col_peaks, col_sums, picked = [], [], []
+    for n, s in enumerate(slots):
+        tile = scores[:, n * rows : (n + 1) * rows]
         peak = jnp.max(tile, axis=0, keepdims=True)
-        peaks.append(peak)
-        sums.append(jnp.sum(jnp.exp(tile - peak), axis=0, keepdims=True))
-        chosen = jnp.where(onehot[s], tile[:rows, :], 0.0)
+        col_peaks.append(peak)
+        col_sums.append(jnp.sum(jnp.exp(tile - peak), axis=0, keepdims=True))
+        match = wanted == (lane + place(quarter, s, parts) * rows).astype(F32)
+        chosen = jnp.where(match, tile[:rows, :], 0.0)
         picked.append(jnp.sum(chosen, axis=0, keepdims=True))
         found = found + jnp.sum(chosen, axis=1, keepdims=True)
-    row_pos[...] = to_lanes(found, eye)
-    col_stats[...] = jnp.concatenate(peaks + sums + picked, axis=0)
+    row_out[...] = jnp.concatenate(peaks + sums + [to_lanes(found, eye)], axis=0)
+    col_out[...] = jnp.concatenate(col_peaks + col_sums + picked, axis=0)
+
+
+def first_kernel(parts, scale, positive, *refs):
+    images, texts = refs[:STEPS], refs[STEPS : STEPS + parts - 1]
+    img_out, *outs = refs[STEPS + parts - 1 :]
+    rows = images[0].shape[0]
+    for k in range(STEPS):
+        store_units(images[k], img_out, k * rows)
+    slots = range(parts - 1)
+    scores_kernel(parts, slots, scale[0], positive[...], img_out, texts, *outs)
+
+
+def last_kernel(parts, scale, positive, images, text, row_first, col_first, *outs):
+    *outs, row_stats, col_stats, row_pos, row_last, col_last = outs
+    slots = [parts - 1]
+    scores_kernel(
+        parts, slots, scale[0], positive[...], images, [text], *outs, row_last, col_last
+    )
+    peaks = jnp.maximum(row_first[:STEPS, :], row_last[:STEPS, :])
+    sums = sum(
+        t[STEPS : 2 * STEPS, :] * jnp.exp(t[:STEPS, :] - peaks) for t in (row_first, row_last)
+    )
+    row_stats[...] = jnp.concatenate([peaks, sums], axis=0)
+    row_pos[...] = row_first[2 * STEPS :, :] + row_last[2 * STEPS :, :]
+    tables = []
+    for which in range(3):
+        tables += [col_first[which * (parts - 1) : (which + 1) * (parts - 1), :]]
+        tables += [col_last[which : which + 1, :]]
+    blank = jnp.zeros((col_stats.shape[0] - 3 * parts, col_last.shape[1]), F32)
+    col_stats[...] = jnp.concatenate(tables + [blank] * (blank.shape[0] > 0), axis=0)
 
 
 def merged(pairs):
@@ -113,37 +168,45 @@
     return peak + jnp.log(sum(s * jnp.exp(p - peak) for p, s in pairs))
 
 
-def weights_kernel(parts, positive, scores, images, row_pos, *refs):
-    row_stats, col_stats = refs[: 2 * STEPS - 1], refs[2 * STEPS - 1 : 2 * STEPS - 1 + parts]
-    row_loss, col_loss, weights, *txt_parts = refs[2 * STEPS - 1 + parts :]
+def weights_kernel(parts, positive, first, last, images, row_pos, *refs):
+    places = known_places(STEPS - 1)
+    row_refs, refs = refs[: len(places)], refs[len(places) :]
+    held = slot_counts(parts)
+    col_refs, refs = refs[: len(held)], refs[len(held) :]
+    row_loss, col_loss, weights, *txt_parts = refs
     rows = row_pos.shape[1]
     eye = diagonal(rows)
     onehot = onehot_of(positive[...], eye, parts, rows)
+    row_tables = {}
+    for ref, shifts in zip(row_refs, places):
+        for n, shift in enumerate(shifts):
+            row_tables[shift] = ref[n * 2 * STEPS : (n + 1) * 2 * STEPS, :]
+    height = table_rows(parts)
+    col_tables = []
+    for ref, count in zip(col_refs, held):
+        col_tables += [ref[n * height : (n + 1) * height, :] for n in range(count)]
 
     def row_pair(shift, k):
-        table = row_stats[shift + STEPS - 1]
-        at = k + shift
+        table, at = row_tables[shift], k - shift
         return table[at : at + 1, :], table[STEPS + at : STEPS + at + 1, :]
 
     row_lse = []
     for k in range(STEPS):
-        lse = merged([row_pair(t, k) for t in range(1 - STEPS, STEPS) if 0 <= k + t < STEPS])
+        lse = merged([row_pair(t, k) for t in range(1 - STEPS, STEPS) if 0 <= k - t < STEPS])
         if k == 0:
             row_loss[...] = lse - row_pos[...]
         row_lse.append(to_column(lse, eye))
     col_lse = []
     for s in range(parts):
-        at = [(t, slot_at(s, t, parts)) for t in range(parts)]
-        lse = merged(
-            [(col_stats[t][q : q + 1, :], col_stats[t][parts + q : parts + q + 1, :]) for t, q in at]
-        )
+        at = [(col_tables[t], slot_at(s, t, parts)) for t in range(parts)]
+        lse = merged([(c[q : q + 1, :], c[parts + q : parts + q + 1, :]) for c, q in at])
         if s == 0:
-            picked = sum(col_stats[t][2 * parts + q : 2 * parts + q + 1, :] for t, q in at)
-            col_loss[...] = lse - picked
+            col_loss[...] = lse - sum(c[2 * parts + q : 2 * parts + q + 1, :] for c, q in at)
         col_lse.append(lse)
     for s in range(parts):
+        source, base = (first, s * rows) if s < parts - 1 else (last, 0)
         for k in range(STEPS):
-            tile = scores[k * rows : (k + 1) * rows, s * rows : (s + 1) * rows]
+            tile = source[k * rows : (k + 1) * rows, base : base + rows]
             weight = 0.5 * (jnp.exp(tile - row_lse[k]) + jnp.exp(tile - col_lse[s]))
             if k == 0:
                 weight = weight - onehot[s].astype(F32)
@@ -158,12 +221,13 @@
         txt_parts[s][...] = part.astype(txt_parts[s].dtype)
 
 
-def images_kernel(weights, texts, *img_parts):
+def images_kernel(weights, first, last, *img_parts):
     rows = img_parts[0].shape[0]
+    split = first.shape[0]
     for k in range(STEPS):
-        part = jnp.dot(
-            weights[k * rows : (k + 1) * rows, :], texts[...], preferred_element_type=F32
-        )
+        strip = slice(k * rows, (k + 1) * rows)
+        part = jnp.dot(weights[strip, :split], first[...], preferred_element_type=F32)
+        part = part + jnp.dot(weights[strip, split:], last[...], preferred_element_type=F32)
         img_parts[k][...] = part.astype(img_parts[k].dtype)
 
 
@@ -180,12 +244,13 @@
         grad[chunk, :] = (total - unit * along) * inverse
 
 
-def call(kernel, outs, specs, args):
+def call(kernel, outs, specs, args, scratch=()):
     return pl.pallas_call(
         kernel,
         out_shape=outs,
         in_specs=[pl.BlockSpec(memory_space=space) for space in specs],
         out_specs=jax.tree.map(lambda _: pl.BlockSpec(memory_space=VMEM), outs),
+        scratch_shapes=list(scratch),
         compiler_params=pltpu.CompilerParams(vmem_limit_bytes=16 << 20),
     )(*args)
 
@@ -193,27 +258,49 @@
 def on_device(image, text, positive, logit_scale):
     rows, width = image.shape
     parts = lax.axis_size("rep")
+    height = table_rows(parts)
     shape = jax.ShapeDtypeStruct
     texts = [text] + [fetched(text, "rep", s) for s in range(1, parts)]
     images = [image] + [passed_along(image, "blk", -k) for k in range(1, STEPS)]
-    scores, img_tiles, txt_tiles, row_stats, col_stats, row_pos = call(
-        functools.partial(scores_kernel, parts),
+    split = (parts - 1) * rows
+    img_tiles, first, txt_first, row_first, col_first = call(
+        functools.partial(first_kernel, parts),
         (
-            shape((STEPS * rows, parts * rows), F32),
             shape((STEPS * rows, width), BF16),
-            shape((parts * rows, width), BF16),
+            shape((STEPS * rows, split), F32),
+            shape((split, width), BF16),
+            shape((2 * STEPS + 1, rows), F32),
+            shape((3 * (parts - 1), rows), F32),
+        ),
+        [SMEM] + [VMEM] * (STEPS + parts),
+        (logit_scale, positive, *images, *texts[:-1]),
+    )
+    last, txt_last, row_stats, col_stats, row_pos = call(
+        functools.partial(last_kernel, parts),
+        (
+            shape((STEPS * rows, rows), F32),
+            shape((rows, width), BF16),
             shape((2 * STEPS, rows), F32),
-            shape((3 * parts, rows), F32),
+            shape((height, rows), F32),
             shape((1, rows), F32),
         ),
-        [SMEM] + [VMEM] * (1 + STEPS + parts),
-        (logit_scale, positive, *images, *texts),
-    )
-    col_tables = [col_stats] + [fetched(col_stats, "rep", t) for t in range(1, parts)]
-    row_tables = [
-        row_stats if t == 0 else passed_along(row_stats, "blk", t)
-        for t in range(1 - STEPS, STEPS)
-    ]
+        [SMEM] + [VMEM] * 5,
+        (logit_scale, positive, img_tiles, texts[-1], row_first, col_first),
+        [pltpu.VMEM((2 * STEPS + 1, rows), F32), pltpu.VMEM((3, rows), F32)],
+    )
+    col_tables = [col_stats]
+    for n, count in enumerate(slot_counts(parts)[1:]):
+        sent = jnp.concatenate(col_tables, axis=0)[: count * height]
+        col_tables.append(fetched(sent, "rep", 2**n))
+    row_tables = [row_stats]
+    for shift, known in doublings(STEPS - 1):
+        by_shift = {}
+        for array, shifts in zip(row_tables, known_places(STEPS - 1)):
+            for at, place_ in enumerate(shifts):
+                by_shift[place_] = array[at * 2 * STEPS : (at + 1) * 2 * STEPS]
+        sent = jnp.concatenate([by_shift[t] for t in range(-known, known + 1)], axis=0)
+        for sign in (1, -1):
+            row_tables.append(passed_along(sent, "blk", -sign * shift))
     row_loss, col_loss, weights, *txt_parts = call(
         functools.partial(weights_kernel, parts),
         (
@@ -222,15 +309,15 @@
             shape((STEPS * rows, parts * rows), BF16),
             *[shape((rows, width), BF16 if s else F32) for s in range(parts)],
         ),
-        [VMEM] * (4 + 2 * STEPS - 1 + parts),
-        (positive, scores, img_tiles, row_pos, *row_tables, *col_tables),
+        [VMEM] * (5 + len(row_tables) + len(col_tables)),
+        (positive, first, last, img_tiles, row_pos, *row_tables, *col_tables),
     )
     txt_sums = [txt_parts[0]] + [returned(txt_parts[s], "rep", s) for s in range(1, parts)]
     img_parts = call(
         images_kernel,
         [shape((rows, width), BF16 if k else F32) for k in range(STEPS)],
-        [VMEM] * 2,
-        (weights, txt_tiles),
+        [VMEM] * 3,
+        (weights, txt_first, txt_last),
     )
     img_sums = [img_parts[0]] + [passed_along(img_parts[k], "blk", k) for k in range(1, STEPS)]
     grads = [

time: 80.8 us -> 77.4 us (0.958)
  the two profiles are of different devices: /device:TPU:0 before, /device:TPU:8 now
where the time goes in v3:
time: 77.4 us; the launch traced here: 77.2 us
  waiting for transfers between devices  44.4 us (57%)
  starting transfers between devices  22.5 us (29%)
  Pallas kernels  6.99 us (9%)
  local copies, waits for them, and re-layouts  1.92 us (2%)
  between operations  1.34 us (2%)
    ppermute x10, waiting for transfers between devices, passed_along(): lax.ppermute(array, axis, [(i, (i + by) % count) for i in range(count)])  21.4 us
    ppermute x10, starting transfers between devices, passed_along(): lax.ppermute(array, axis, [(i, (i + by) % count) for i in range(count)])  14.2 us
    ppermute x5, waiting for transfers between devices, fetched(): lax.ppermute(array, axis, [(place(i, slot, count), i) for i in range(coun...  12.9 us
    ppermute x3, waiting for transfers between devices, returned(): lax.ppermute(array, axis, [(i, place(i, slot, count)) for i in range(coun...  10.1 us
    pallas_call x6, Pallas kernels, call(): pl.pallas_call(kernel, out_shape=outs, in_specs=[pl.BlockSpec(memory_spac...  6.99 us
    ppermute x5, starting transfers between devices, fetched(): lax.ppermute(array, axis, [(place(i, slot, count), i) for i in range(coun...  5.64 us
    ppermute x3, starting transfers between devices, returned(): lax.ppermute(array, axis, [(i, place(i, slot, count)) for i in range(coun...  2.73 us
    unnamed x12, local copies, waits for them, and re-layouts  1.91 us
  transfers between devices with their start and end apart: 18, of which 15 were waited for; matrix products, arithmetic and copies ran while one was open for 0% of the time, Pallas kernels for 3%

profile of v3, /device:TPU:8, one launch (start us, length us, event | category | flops | bytes accessed | tf_op | source)
XLA Modules:
  0.0 77.2 jit_solution(6630348865379179776)
XLA Ops:
  0.6 1.0 %collective-permute-start.2 = (bf16[128,1024]{1,0:T(8,128)(2,1)}, bf16[128,1024]{1,0:T(8,128)(2,1)S(1)}, u32[]{:S(2)}, u32[]{:S(2)}) collective-permute-start(bf16[128,1024]{1,0:T(8,128)(2,1)} %raw.2), channel_id=1, source_target_pairs={{0,20},{4,24},{8,28},{12,0},{16,4},{20,8},{24,12},{28,16},{1,21},{... | collective-permute-start | bytes 786440 | tf_op jit(solution)/shard_map/ppermute | solution.py:42
  1.7 1.6 %collective-permute-start.1 = (bf16[128,1024]{1,0:T(8,128)(2,1)}, bf16[128,1024]{1,0:T(8,128)(2,1)S(1)}, u32[]{:S(2)}, u32[]{:S(2)}) collective-permute-start(bf16[128,1024]{1,0:T(8,128)(2,1)} %raw.2), channel_id=1, source_target_pairs={{0,24},{4,28},{8,0},{12,4},{16,8},{20,12},{24,16},{28,20},{1,25},{... | collective-permute-start | bytes 786440 | tf_op jit(solution)/shard_map/ppermute | solution.py:42
  3.2 1.3 %collective-permute-start = (bf16[128,1024]{1,0:T(8,128)(2,1)}, bf16[128,1024]{1,0:T(8,128)(2,1)S(1)}, u32[]{:S(2)}, u32[]{:S(2)}) collective-permute-start(bf16[128,1024]{1,0:T(8,128)(2,1)} %raw.2), channel_id=1, source_target_pairs={{0,28},{4,0},{8,4},{12,8},{16,12},{20,16},{24,20},{28,24},{1,29},{... | collective-permute-start | bytes 786440 | tf_op jit(solution)/shard_map/ppermute | solution.py:42
  4.5 2.6 %collective-permute-start.4 = (bf16[128,1024]{1,0:T(8,128)(2,1)}, bf16[128,1024]{1,0:T(8,128)(2,1)S(1)}, u32[]{:S(2)}, u32[]{:S(2)}) collective-permute-start(bf16[128,1024]{1,0:T(8,128)(2,1)} %raw.3), channel_id=1, source_target_pairs={{2,0},{3,1},{0,2},{1,3},{6,4},{7,5},{4,6},{5,7},{10,8},{11,9},{8,1... | collective-permute-start | bytes 786440 | tf_op jit(solution)/shard_map/ppermute | solution.py:32
  8.0 1.6 %collective-permute-start.5 = (bf16[128,1024]{1,0:T(8,128)(2,1)}, bf16[128,1024]{1,0:T(8,128)(2,1)S(1)}, u32[]{:S(2)}, u32[]{:S(2)}) collective-permute-start(bf16[128,1024]{1,0:T(8,128)(2,1)} %raw.3), channel_id=1, source_target_pairs={{3,0},{2,1},{1,2},{0,3},{7,4},{6,5},{5,6},{4,7},{11,8},{10,9},{9,1... | collective-permute-start | bytes 786440 | tf_op jit(solution)/shard_map/ppermute | solution.py:32
  10.2 0.8 %collective-permute-done.1.refs_2_ = bf16[128,1024]{1,0:T(8,128)(2,1)S(1)} collective-permute-done((bf16[128,1024]{1,0:T(8,128)(2,1)}, bf16[128,1024]{1,0:T(8,128)(2,1)S(1)}, u32[]{:S(2)}, u32[]{:S(2)}) %collective-permute-start.1) | collective-permute-done | bytes 262176 | tf_op jit(solution)/shard_map/ppermute | solution.py:42
  11.0 4.2 %collective-permute-done.refs_1_ = bf16[128,1024]{1,0:T(8,128)(2,1)S(1)} collective-permute-done((bf16[128,1024]{1,0:T(8,128)(2,1)}, bf16[128,1024]{1,0:T(8,128)(2,1)S(1)}, u32[]{:S(2)}, u32[]{:S(2)}) %collective-permute-start) | collective-permute-done | bytes 262176 | tf_op jit(solution)/shard_map/ppermute | solution.py:42
  15.2 4.2 %collective-permute-done.4.refs_6_ = bf16[128,1024]{1,0:T(8,128)(2,1)S(1)} collective-permute-done((bf16[128,1024]{1,0:T(8,128)(2,1)}, bf16[128,1024]{1,0:T(8,128)(2,1)S(1)}, u32[]{:S(2)}, u32[]{:S(2)}) %collective-permute-start.4) | collective-permute-done | bytes 262176 | tf_op jit(solution)/shard_map/ppermute | solution.py:32
  19.4 1.1 %collective-permute-done.3.refs_5_ = bf16[128,1024]{1,0:T(8,128)(2,1)S(1)} collective-permute-done((bf16[128,1024]{1,0:T(8,128)(2,1)}, bf16[128,1024]{1,0:T(8,128)(2,1)S(1)}, u32[]{:S(2)}, u32[]{:S(2)}) %collective-permute-start.3) | collective-permute-done | bytes 262176 | tf_op jit(solution)/shard_map/ppermute | solution.py:32
  20.6 0.9 %copy-done = bf16[128,1024]{1,0:T(8,128)(2,1)S(1)} copy-done((bf16[128,1024]{1,0:T(8,128)(2,1)S(1)}, bf16[128,1024]{1,0:T(8,128)(2,1)}, u32[]{:S(2)}) %copy-start) | copy-done | bytes 262168
  21.5 0.9 %copy-done.2 = bf16[128,1024]{1,0:T(8,128)(2,1)S(1)} copy-done((bf16[128,1024]{1,0:T(8,128)(2,1)S(1)}, bf16[128,1024]{1,0:T(8,128)(2,1)}, u32[]{:S(2)}) %copy-start.2) | copy-done | bytes 262168
  22.5 1.4 %shard_map.75 = (bf16[512,1024]{1,0:T(8,128)(2,1)S(1)}, f32[512,384]{1,0:T(8,128)S(1)}, bf16[384,1024]{1,0:T(8,128)(2,1)S(1)}, f32[9,128]{1,0:T(8,128)S(1)}, f32[9,128]{1,0:T(8,128)S(1)}) custom-call(f32[1]{0:T(128)S(6)} %copy.10.scale, s32[1,128]{1,0:T(1,128)S(1)} %copy-done.4, bf16[128,1024]{1,0:T(8,128)(2,1)S(1)} %copy-done, ...), custom_call_target="tpu_custom_call" | custom-call | tf_op jit(solution)/shard_map/pallas_call | solution.py:248
  23.9 5.2 %collective-permute-done.5.text = bf16[128,1024]{1,0:T(8,128)(2,1)S(1)} collective-permute-done((bf16[128,1024]{1,0:T(8,128)(2,1)}, bf16[128,1024]{1,0:T(8,128)(2,1)S(1)}, u32[]{:S(2)}, u32[]{:S(2)}) %collective-permute-start.5) | collective-permute-done | bytes 262176 | tf_op jit(solution)/shard_map/ppermute | solution.py:32
  29.9 4.0 %collective-permute-start.6 = (f32[8,128]{1,0:T(8,128)S(1)}, f32[8,128]{1,0:T(8,128)S(1)}, u32[]{:S(2)}, u32[]{:S(2)}) collective-permute-start(f32[8,128]{1,0:T(8,128)S(1)} %get-tuple-element.31.refs_0_), channel_id=1, source_target_pairs={{0,28},{4,0},{8,4},{12,8},{16,12},{20,16},{24,20},{28,24},{1,29},{... | collective-permute-start | bytes 12296 | tf_op jit(solution)/shard_map/ppermute | solution.py:42
  33.9 1.2 %collective-permute-done.7.refs_2_ = f32[8,128]{1,0:T(8,128)S(1)} collective-permute-done((f32[8,128]{1,0:T(8,128)S(1)}, f32[8,128]{1,0:T(8,128)S(1)}, u32[]{:S(2)}, u32[]{:S(2)}) %collective-permute-start.7) | collective-permute-done | bytes 4128 | tf_op jit(solution)/shard_map/ppermute | solution.py:42
  35.1 2.4 %collective-permute-done.10.refs_6_ = f32[16,128]{1,0:T(8,128)S(1)} collective-permute-done((f32[16,128]{1,0:T(8,128)S(1)}, f32[16,128]{1,0:T(8,128)S(1)}, u32[]{:S(2)}, u32[]{:S(2)}) %collective-permute-start.10) | collective-permute-done | bytes 8224 | tf_op jit(solution)/shard_map/ppermute | solution.py:32
  37.5 1.0 %collective-permute-start.11 = (f32[32,128]{1,0:T(8,128)S(1)}, f32[32,128]{1,0:T(8,128)S(1)}, u32[]{:S(2)}, u32[]{:S(2)}) collective-permute-start(f32[32,128]{1,0:T(8,128)S(1)} %pad_maximum_fusion), channel_id=1, source_target_pairs={{2,0},{3,1},{0,2},{1,3},{6,4},{7,5},{4,6},{5,7},{10,8},{11,9},{8,1... | collective-permute-start | bytes 49160 | tf_op jit(solution)/shard_map/ppermute | solution.py:32
  38.6 2.0 %collective-permute-start.9 = (f32[24,128]{1,0:T(8,128)S(1)}, f32[24,128]{1,0:T(8,128)S(1)}, u32[]{:S(2)}, u32[]{:S(2)}) collective-permute-start(f32[24,128]{1,0:T(8,128)S(1)} %constant_dynamic-update-slice_fusion), channel_id=1, source_target_pairs={{0,8},{4,12},{8,16},{12,20},{16,24},{20,28},{24,0},{28,4},{1,9},{5... | collective-permute-start | bytes 36872 | tf_op jit(solution)/shard_map/ppermute | solution.py:42
  40.6 0.9 %collective-permute-start.8 = (f32[24,128]{1,0:T(8,128)S(1)}, f32[24,128]{1,0:T(8,128)S(1)}, u32[]{:S(2)}, u32[]{:S(2)}) collective-permute-start(f32[24,128]{1,0:T(8,128)S(1)} %constant_dynamic-update-slice_fusion), channel_id=1, source_target_pairs={{0,24},{4,28},{8,0},{12,4},{16,8},{20,12},{24,16},{28,20},{1,25},{... | collective-permute-start | bytes 36872 | tf_op jit(solution)/shard_map/ppermute | solution.py:42
  41.5 1.7 %collective-permute-done.9.refs_4_ = f32[24,128]{1,0:T(8,128)S(1)} collective-permute-done((f32[24,128]{1,0:T(8,128)S(1)}, f32[24,128]{1,0:T(8,128)S(1)}, u32[]{:S(2)}, u32[]{:S(2)}) %collective-permute-start.9) | collective-permute-done | bytes 12320 | tf_op jit(solution)/shard_map/ppermute | solution.py:42
  43.2 1.1 %collective-permute-done.8.refs_3_ = f32[24,128]{1,0:T(8,128)S(1)} collective-permute-done((f32[24,128]{1,0:T(8,128)S(1)}, f32[24,128]{1,0:T(8,128)S(1)}, u32[]{:S(2)}, u32[]{:S(2)}) %collective-permute-start.8) | collective-permute-done | bytes 12320 | tf_op jit(solution)/shard_map/ppermute | solution.py:42
  44.3 1.6 %shard_map.77 = (f32[1,128]{1,0:T(1,128)}, f32[1,128]{1,0:T(1,128)}, bf16[512,512]{1,0:T(8,128)(2,1)S(1)}, f32[128,1024]{1,0:T(8,128)S(1)}, bf16[128,1024]{1,0:T...) custom-call(s32[1,128]{1,0:T(1,128)S(1)} %copy-done.4, ...), custom_call_target="tpu_custom_call" | custom-call | tf_op jit(solution)/shard_map/pallas_call | solution.py:248
  45.9 1.0 %shard_map.78 = (f32[128,1024]{1,0:T(8,128)S(1)}, bf16[128,1024]{1,0:T(8,128)(2,1)S(1)}, bf16[128,1024]{1,0:T(8,128)(2,1)S(1)}, bf16[128,1024]{1,0:T(8,128)(2,1)S(1)}) custom-call(bf16[512,512]{1,0:T(8,128)(2,1)S(1)} %get-tuple-element.35.weights, bf16[384,1024]{1,0:T(8,128)(2,1)S(1)} %get-tuple-element.36.first, bf16[128,1024]{1,0:T(8,128)(2,1)S(1)} %get-tuple-element.37.last), custom_call_target="tpu_custom_call" | custom-call | tf_op jit(solution)/shard_map/pallas_call | solution.py:248
  46.9 1.7 %collective-permute-start.13 = (bf16[128,1024]{1,0:T(8,128)(2,1)S(1)}, bf16[128,1024]{1,0:T(8,128)(2,1)S(1)}, u32[]{:S(2)}, u32[]{:S(2)}) collective-permute-start(bf16[128,1024]{1,0:T(8,128)(2,1)S(1)} %get-tuple-element.40), channel_id=1, source_target_pairs={{0,8},{4,12},{8,16},{12,20},{16,24},{20,28},{24,0},{28,4},{1,9},{5... | collective-permute-start | bytes 786440 | tf_op jit(solution)/shard_map/ppermute | solution.py:42
  48.6 1.6 %collective-permute-start.14 = (bf16[128,1024]{1,0:T(8,128)(2,1)S(1)}, bf16[128,1024]{1,0:T(8,128)(2,1)S(1)}, u32[]{:S(2)}, u32[]{:S(2)}) collective-permute-start(bf16[128,1024]{1,0:T(8,128)(2,1)S(1)} %get-tuple-element.41), channel_id=1, source_target_pairs={{0,12},{4,16},{8,20},{12,24},{16,28},{20,0},{24,4},{28,8},{1,13},{... | collective-permute-start | bytes 786440 | tf_op jit(solution)/shard_map/ppermute | solution.py:42
  50.2 2.0 %collective-permute-start.15 = (bf16[128,1024]{1,0:T(8,128)(2,1)S(1)}, bf16[128,1024]{1,0:T(8,128)(2,1)S(1)}, u32[]{:S(2)}, u32[]{:S(2)}) collective-permute-start(bf16[128,1024]{1,0:T(8,128)(2,1)S(1)} %get-tuple-element.43), channel_id=1, source_target_pairs={{0,1},{1,0},{2,3},{3,2},{4,5},{5,4},{6,7},{7,6},{8,9},{9,8},{10,11... | collective-permute-start | bytes 786440 | tf_op jit(solution)/shard_map/ppermute | solution.py:37
  52.3 3.6 %collective-permute-done.12.refs_1_ = bf16[128,1024]{1,0:T(8,128)(2,1)S(1)} collective-permute-done((bf16[128,1024]{1,0:T(8,128)(2,1)S(1)}, bf16[128,1024]{1,0:T(8,128)(2,1)S(1)}, u32[]{:S(2)}, u32[]{:S(2)}) %collective-permute-start.12) | collective-permute-done | bytes 262176 | tf_op jit(solution)/shard_map/ppermute | solution.py:42
  57.2 7.7 %collective-permute-done.14.refs_3_ = bf16[128,1024]{1,0:T(8,128)(2,1)S(1)} collective-permute-done((bf16[128,1024]{1,0:T(8,128)(2,1)S(1)}, bf16[128,1024]{1,0:T(8,128)(2,1)S(1)}, u32[]{:S(2)}, u32[]{:S(2)}) %collective-permute-start.14) | collective-permute-done | bytes 262176 | tf_op jit(solution)/shard_map/ppermute | solution.py:42
  64.9 1.1 %shard_map.79 = f32[128,1024]{1,0:T(8,128)} custom-call(f32[1]{0:T(128)S(6)} %copy.10.scale, bf16[128,1024]{1,0:T(8,128)(2,1)S(1)} %copy-done.1, f32[128,1024]{1,0:T(8,128)S(1)} %get-tuple-element.38.refs_0_, bf16[128,1024]{1,0:T(8,128)(2,1)S(1)} %collective-permute-done.12.refs_1_, bf16[128,1024]{1,0:T(8,128)(2,1)S(1)} %collective-permute-done.13.refs_2_, ...), custom_call_target="tpu_custom_call" | custom-call | tf_op jit(solution)/shard_map/pallas_call | solution.py:248
  66.0 4.3 %collective-permute-done.16.refs_2_ = bf16[128,1024]{1,0:T(8,128)(2,1)S(1)} collective-permute-done((bf16[128,1024]{1,0:T(8,128)(2,1)S(1)}, bf16[128,1024]{1,0:T(8,128)(2,1)S(1)}, u32[]{:S(2)}, u32[]{:S(2)}) %collective-permute-start.16) | collective-permute-done | bytes 262176 | tf_op jit(solution)/shard_map/ppermute | solution.py:37
  70.2 5.8 %collective-permute-done.17.refs_3_ = bf16[128,1024]{1,0:T(8,128)(2,1)S(1)} collective-permute-done((bf16[128,1024]{1,0:T(8,128)(2,1)S(1)}, bf16[128,1024]{1,0:T(8,128)(2,1)S(1)}, u32[]{:S(2)}, u32[]{:S(2)}) %collective-permute-start.17) | collective-permute-done | bytes 262176 | tf_op jit(solution)/shard_map/ppermute | solution.py:37
  76.1 1.1 %shard_map.80 = f32[128,1024]{1,0:T(8,128)} custom-call(f32[1]{0:T(128)S(6)} %copy.10.scale, bf16[128,1024]{1,0:T(8,128)(2,1)S(1)} %copy-done.3, f32[128,1024]{1,0:T(8,128)S(1)} %get-tuple-element.42.refs_0_, bf16[128,1024]{1,0:T(8,128)(2,1)S(1)} %collective-permute-done.15.refs_1_, bf16[128,1024]{1,0:T(8,128)(2,1)S(1)} %collective-permute-done.16.refs_2_, ...), custom_call_target="tpu_custom_call" | custom-call | tf_op jit(solution)/shard_map/pallas_call | solution.py:248
  (24 shorter events, 3.1 us)
Async XLA Ops:
  0.6 20.0 %copy-start.4 = (s32[1,128]{1,0:T(1,128)S(1)}, s32[1,128]{1,0:T(1,128)}, u32[]{:S(2)}) copy-start(s32[1,128]{1,0:T(1,128)} %positive.5) | copy-start | bytes 1540
  0.6 7.3 %collective-permute-start.2 = (bf16[128,1024]{1,0:T(8,128)(2,1)}, bf16[128,1024]{1,0:T(8,128)(2,1)S(1)}, u32[]{:S(2)}, u32[]{:S(2)}) collective-permute-start(bf16[128,1024]{1,0:T(8,128)(2,1)} %raw.2), channel_id=1, source_target_pairs={{0,20},{4,24},{8,28},{12,0},{16,4},{20,8},{24,12},{28,16},{1,21},{... | collective-permute-start | bytes 786440 | tf_op jit(solution)/shard_map/ppermute | solution.py:42
  1.7 9.4 %collective-permute-start.1 = (bf16[128,1024]{1,0:T(8,128)(2,1)}, bf16[128,1024]{1,0:T(8,128)(2,1)S(1)}, u32[]{:S(2)}, u32[]{:S(2)}) collective-permute-start(bf16[128,1024]{1,0:T(8,128)(2,1)} %raw.2), channel_id=1, source_target_pairs={{0,24},{4,28},{8,0},{12,4},{16,8},{20,12},{24,16},{28,20},{1,25},{... | collective-permute-start | bytes 786440 | tf_op jit(solution)/shard_map/ppermute | solution.py:42
  3.2 12.0 %collective-permute-start = (bf16[128,1024]{1,0:T(8,128)(2,1)}, bf16[128,1024]{1,0:T(8,128)(2,1)S(1)}, u32[]{:S(2)}, u32[]{:S(2)}) collective-permute-start(bf16[128,1024]{1,0:T(8,128)(2,1)} %raw.2), channel_id=1, source_target_pairs={{0,28},{4,0},{8,4},{12,8},{16,12},{20,16},{24,20},{28,24},{1,29},{... | collective-permute-start | bytes 786440 | tf_op jit(solution)/shard_map/ppermute | solution.py:42
  4.5 14.9 %collective-permute-start.4 = (bf16[128,1024]{1,0:T(8,128)(2,1)}, bf16[128,1024]{1,0:T(8,128)(2,1)S(1)}, u32[]{:S(2)}, u32[]{:S(2)}) collective-permute-start(bf16[128,1024]{1,0:T(8,128)(2,1)} %raw.3), channel_id=1, source_target_pairs={{2,0},{3,1},{0,2},{1,3},{6,4},{7,5},{4,6},{5,7},{10,8},{11,9},{8,1... | collective-permute-start | bytes 786440 | tf_op jit(solution)/shard_map/ppermute | solution.py:32
  7.1 13.5 %collective-permute-start.3 = (bf16[128,1024]{1,0:T(8,128)(2,1)}, bf16[128,1024]{1,0:T(8,128)(2,1)S(1)}, u32[]{:S(2)}, u32[]{:S(2)}) collective-permute-start(bf16[128,1024]{1,0:T(8,128)(2,1)} %raw.3), channel_id=1, source_target_pairs={{1,0},{0,1},{3,2},{2,3},{5,4},{4,5},{7,6},{6,7},{9,8},{8,9},{11,10... | collective-permute-start | bytes 786440 | tf_op jit(solution)/shard_map/ppermute | solution.py:32
  8.0 21.1 %collective-permute-start.5 = (bf16[128,1024]{1,0:T(8,128)(2,1)}, bf16[128,1024]{1,0:T(8,128)(2,1)S(1)}, u32[]{:S(2)}, u32[]{:S(2)}) collective-permute-start(bf16[128,1024]{1,0:T(8,128)(2,1)} %raw.3), channel_id=1, source_target_pairs={{3,0},{2,1},{1,2},{0,3},{7,4},{6,5},{5,6},{4,7},{11,8},{10,9},{9,1... | collective-permute-start | bytes 786440 | tf_op jit(solution)/shard_map/ppermute | solution.py:32
  20.6 1.0 %copy-start = (bf16[128,1024]{1,0:T(8,128)(2,1)S(1)}, bf16[128,1024]{1,0:T(8,128)(2,1)}, u32[]{:S(2)}) copy-start(bf16[128,1024]{1,0:T(8,128)(2,1)} %raw.2) | copy-start | bytes 786436
  21.5 0.9 %copy-start.2 = (bf16[128,1024]{1,0:T(8,128)(2,1)S(1)}, bf16[128,1024]{1,0:T(8,128)(2,1)}, u32[]{:S(2)}) copy-start(bf16[128,1024]{1,0:T(8,128)(2,1)} %raw.3) | copy-start | bytes 786436
  29.8 5.3 %collective-permute-start.7 = (f32[8,128]{1,0:T(8,128)S(1)}, f32[8,128]{1,0:T(8,128)S(1)}, u32[]{:S(2)}, u32[]{:S(2)}) collective-permute-start(f32[8,128]{1,0:T(8,128)S(1)} %get-tuple-element.31.refs_0_), channel_id=1, source_target_pairs={{0,4},{4,8},{8,12},{12,16},{16,20},{20,24},{24,28},{28,0},{1,5},{5... | collective-permute-start | bytes 12296 | tf_op jit(solution)/shard_map/ppermute | solution.py:42
  29.9 8.7 %collective-permute-start.6 = (f32[8,128]{1,0:T(8,128)S(1)}, f32[8,128]{1,0:T(8,128)S(1)}, u32[]{:S(2)}, u32[]{:S(2)}) collective-permute-start(f32[8,128]{1,0:T(8,128)S(1)} %get-tuple-element.31.refs_0_), channel_id=1, source_target_pairs={{0,28},{4,0},{8,4},{12,8},{16,12},{20,16},{24,20},{28,24},{1,29},{... | collective-permute-start | bytes 12296 | tf_op jit(solution)/shard_map/ppermute | solution.py:42
  33.9 3.7 %collective-permute-start.10 = (f32[16,128]{1,0:T(8,128)S(1)}, f32[16,128]{1,0:T(8,128)S(1)}, u32[]{:S(2)}, u32[]{:S(2)}) collective-permute-start(f32[16,128]{1,0:T(8,128)S(1)} %get-tuple-element.32.refs_5_), channel_id=1, source_target_pairs={{1,0},{0,1},{3,2},{2,3},{5,4},{4,5},{7,6},{6,7},{9,8},{8,9},{11,10... | collective-permute-start | bytes 24584 | tf_op jit(solution)/shard_map/ppermute | solution.py:32
  37.5 6.7 %collective-permute-start.11 = (f32[32,128]{1,0:T(8,128)S(1)}, f32[32,128]{1,0:T(8,128)S(1)}, u32[]{:S(2)}, u32[]{:S(2)}) collective-permute-start(f32[32,128]{1,0:T(8,128)S(1)} %pad_maximum_fusion), channel_id=1, source_target_pairs={{2,0},{3,1},{0,2},{1,3},{6,4},{7,5},{4,6},{5,7},{10,8},{11,9},{8,1... | collective-permute-start | bytes 49160 | tf_op jit(solution)/shard_map/ppermute | solution.py:32
  38.6 4.6 %collective-permute-start.9 = (f32[24,128]{1,0:T(8,128)S(1)}, f32[24,128]{1,0:T(8,128)S(1)}, u32[]{:S(2)}, u32[]{:S(2)}) collective-permute-start(f32[24,128]{1,0:T(8,128)S(1)} %constant_dynamic-update-slice_fusion), channel_id=1, source_target_pairs={{0,8},{4,12},{8,16},{12,20},{16,24},{20,28},{24,0},{28,4},{1,9},{5... | collective-permute-start | bytes 36872 | tf_op jit(solution)/shard_map/ppermute | solution.py:42
  40.6 3.7 %collective-permute-start.8 = (f32[24,128]{1,0:T(8,128)S(1)}, f32[24,128]{1,0:T(8,128)S(1)}, u32[]{:S(2)}, u32[]{:S(2)}) collective-permute-start(f32[24,128]{1,0:T(8,128)S(1)} %constant_dynamic-update-slice_fusion), channel_id=1, source_target_pairs={{0,24},{4,28},{8,0},{12,4},{16,8},{20,12},{24,16},{28,20},{1,25},{... | collective-permute-start | bytes 36872 | tf_op jit(solution)/shard_map/ppermute | solution.py:42
  45.9 19.0 %copy-start.1 = (bf16[128,1024]{1,0:T(8,128)(2,1)S(1)}, bf16[128,1024]{1,0:T(8,128)(2,1)}, u32[]{:S(2)}) copy-start(bf16[128,1024]{1,0:T(8,128)(2,1)} %raw.2) | copy-start | bytes 786436
  46.9 9.0 %collective-permute-start.12 = (bf16[128,1024]{1,0:T(8,128)(2,1)S(1)}, bf16[128,1024]{1,0:T(8,128)(2,1)S(1)}, u32[]{:S(2)}, u32[]{:S(2)}) collective-permute-start(bf16[128,1024]{1,0:T(8,128)(2,1)S(1)} %get-tuple-element.39), channel_id=1, source_target_pairs={{0,4},{4,8},{8,12},{12,16},{16,20},{20,24},{24,28},{28,0},{1,5},{5... | collective-permute-start | bytes 786440 | tf_op jit(solution)/shard_map/ppermute | solution.py:42
  46.9 10.2 %collective-permute-start.13 = (bf16[128,1024]{1,0:T(8,128)(2,1)S(1)}, bf16[128,1024]{1,0:T(8,128)(2,1)S(1)}, u32[]{:S(2)}, u32[]{:S(2)}) collective-permute-start(bf16[128,1024]{1,0:T(8,128)(2,1)S(1)} %get-tuple-element.40), channel_id=1, source_target_pairs={{0,8},{4,12},{8,16},{12,20},{16,24},{20,28},{24,0},{28,4},{1,9},{5... | collective-permute-start | bytes 786440 | tf_op jit(solution)/shard_map/ppermute | solution.py:42
  48.6 16.2 %collective-permute-start.14 = (bf16[128,1024]{1,0:T(8,128)(2,1)S(1)}, bf16[128,1024]{1,0:T(8,128)(2,1)S(1)}, u32[]{:S(2)}, u32[]{:S(2)}) collective-permute-start(bf16[128,1024]{1,0:T(8,128)(2,1)S(1)} %get-tuple-element.41), channel_id=1, source_target_pairs={{0,12},{4,16},{8,20},{12,24},{16,28},{20,0},{24,4},{28,8},{1,13},{... | collective-permute-start | bytes 786440 | tf_op jit(solution)/shard_map/ppermute | solution.py:42
  50.2 15.8 %collective-permute-start.15 = (bf16[128,1024]{1,0:T(8,128)(2,1)S(1)}, bf16[128,1024]{1,0:T(8,128)(2,1)S(1)}, u32[]{:S(2)}, u32[]{:S(2)}) collective-permute-start(bf16[128,1024]{1,0:T(8,128)(2,1)S(1)} %get-tuple-element.43), channel_id=1, source_target_pairs={{0,1},{1,0},{2,3},{3,2},{4,5},{5,4},{6,7},{7,6},{8,9},{9,8},{10,11... | collective-permute-start | bytes 786440 | tf_op jit(solution)/shard_map/ppermute | solution.py:37
  52.2 18.0 %collective-permute-start.16 = (bf16[128,1024]{1,0:T(8,128)(2,1)S(1)}, bf16[128,1024]{1,0:T(8,128)(2,1)S(1)}, u32[]{:S(2)}, u32[]{:S(2)}) collective-permute-start(bf16[128,1024]{1,0:T(8,128)(2,1)S(1)} %get-tuple-element.44), channel_id=1, source_target_pairs={{0,2},{1,3},{2,0},{3,1},{4,6},{5,7},{6,4},{7,5},{8,10},{9,11},{10,... | collective-permute-start | bytes 786440 | tf_op jit(solution)/shard_map/ppermute | solution.py:37
  55.9 20.2 %collective-permute-start.17 = (bf16[128,1024]{1,0:T(8,128)(2,1)S(1)}, bf16[128,1024]{1,0:T(8,128)(2,1)S(1)}, u32[]{:S(2)}, u32[]{:S(2)}) collective-permute-start(bf16[128,1024]{1,0:T(8,128)(2,1)S(1)} %get-tuple-element.45), channel_id=1, source_target_pairs={{0,3},{1,2},{2,1},{3,0},{4,7},{5,6},{6,5},{7,4},{8,11},{9,10},{10,... | collective-permute-start | bytes 786440 | tf_op jit(solution)/shard_map/ppermute | solution.py:37
  64.9 11.2 %copy-start.3 = (bf16[128,1024]{1,0:T(8,128)(2,1)S(1)}, bf16[128,1024]{1,0:T(8,128)(2,1)}, u32[]{:S(2)}) copy-start(bf16[128,1024]{1,0:T(8,128)(2,1)} %raw.3) | copy-start | bytes 786436

commit v4 on v3

--- a/solution.py
+++ b/solution.py
@@ -40,6 +40,20 @@
 def passed_along(array, axis, by):
     count = lax.axis_size(axis)
     return lax.ppermute(array, axis, [(i, (i + by) % count) for i in range(count)])
+
+
+def neighbour_swapped(array):
+    count = lax.axis_size("blk")
+    return lax.ppermute(array, "blk", [(i, i ^ 1) for i in range(count)])
+
+
+def direct_pairs():
+    count = lax.axis_size("blk")
+    return [(i, (i + (3 if i % 2 else 1)) % count) for i in range(count)]
+
+
+def direct_step():
+    return jnp.where(lax.axis_index("blk") % 2 == 0, 1, 3)
 
 
 def table_rows(parts):
@@ -63,6 +77,10 @@
     return held
 
 
+def whole_axis_known(count):
+    return power_of_two(count) and count <= 2 * STEPS
+
+
 def slot_counts(parts):
     counts = [1]
     while sum(counts) < parts:
@@ -74,10 +92,16 @@
     return lax.rsqrt(jnp.sum(wide * wide, axis=-1, keepdims=True) + 1e-06)
 
 
-def store_units(raw, out, base):
-    for at in range(0, raw.shape[0], CHUNK):
-        wide = raw[at : at + CHUNK, :].astype(F32)
-        out[base + at : base + at + CHUNK, :] = (wide * inverse_norm(wide)).astype(BF16)
+def store_units(raws, out, base):
+    for at in range(0, raws[0].shape[0], CHUNK):
+        wide = sum(raw[at : at + CHUNK, :].astype(F32) for raw in raws)
+        here = pl.multiple_of(base + at, CHUNK)
+        out[pl.ds(here, CHUNK), :] = (wide * inverse_norm(wide)).astype(BF16)
+
+
+def own_kernel(image, text, img_out, txt_out):
+    store_units([image], img_out, 0)
+    store_units([text], txt_out, 0)
 
 
 def diagonal(rows):
@@ -101,14 +125,12 @@
     return [wanted == (lane + place(quarter, s, parts) * rows).astype(F32) for s in range(parts)]
 
 
-def scores_kernel(parts, slots, factor, positive, images, texts, scores, txt_out, row_out, col_out):
-    rows = texts[0].shape[0]
+def scores_kernel(parts, slots, factor, positive, images, scores, txt_out, row_out, col_out):
+    rows = positive.shape[1]
     eye = diagonal(rows)
     wanted = to_column(positive.astype(F32), eye)
     lane = lax.broadcasted_iota(jnp.int32, (rows, rows), 1)
     quarter = lax.axis_index("rep")
-    for n, text in enumerate(texts):
-        store_units(text, txt_out, n * rows)
     scores[...] = factor * lax.dot_general(
         images[...], txt_out[...], (((1,), (1,)), ((), ())), preferred_element_type=F32
     )
@@ -134,20 +156,28 @@
 
 
 def first_kernel(parts, scale, positive, *refs):
-    images, texts = refs[:STEPS], refs[STEPS : STEPS + parts - 1]
-    img_out, *outs = refs[STEPS + parts - 1 :]
-    rows = images[0].shape[0]
-    for k in range(STEPS):
-        store_units(images[k], img_out, k * rows)
+    own_image, direct, second, other, own_text = refs[:5]
+    texts = refs[5 : 5 + parts - 2]
+    img_out, scores, txt_out, *stats = refs[5 + parts - 2 :]
+    rows = own_image.shape[0]
+    step = direct_step()
+    img_out[:rows, :] = own_image[...]
+    store_units([direct], img_out, step * rows)
+    store_units([second], img_out, 2 * rows)
+    store_units([other], img_out, (STEPS - step) * rows)
+    txt_out[:rows, :] = own_text[...]
+    for n, text in enumerate(texts):
+        store_units([text], txt_out, (n + 1) * rows)
     slots = range(parts - 1)
-    scores_kernel(parts, slots, scale[0], positive[...], img_out, texts, *outs)
-
-
-def last_kernel(parts, scale, positive, images, text, row_first, col_first, *outs):
-    *outs, row_stats, col_stats, row_pos, row_last, col_last = outs
+    scores_kernel(parts, slots, scale[0], positive[...], img_out, scores, txt_out, *stats)
+
+
+def last_kernel(parts, scale, positive, images, row_first, col_first, *refs):
+    *texts, scores, txt_out, row_stats, col_stats, row_pos, row_last, col_last = refs
+    store_units(texts, txt_out, 0)
     slots = [parts - 1]
     scores_kernel(
-        parts, slots, scale[0], positive[...], images, [text], *outs, row_last, col_last
+        parts, slots, scale[0], positive[...], images, scores, txt_out, row_last, col_last
     )
     peaks = jnp.maximum(row_first[:STEPS, :], row_last[:STEPS, :])
     sums = sum(
@@ -168,19 +198,35 @@
     return peak + jnp.log(sum(s * jnp.exp(p - peak) for p, s in pairs))
 
 
-def weights_kernel(parts, positive, first, last, images, row_pos, *refs):
-    places = known_places(STEPS - 1)
-    row_refs, refs = refs[: len(places)], refs[len(places) :]
+def row_table_lookup(refs, tables):
+    height = 2 * STEPS
+    at = 0
+    for ref in refs:
+        tables[at : at + ref.shape[0], :] = ref[...]
+        at += ref.shape[0]
+    if whole_axis_known(lax.axis_size("blk")):
+        count = lax.axis_size("blk")
+        own = lax.axis_index("blk")
+
+        def lookup(shift):
+            slot = own ^ ((own + shift + count) % count)
+            return tables[pl.ds(pl.multiple_of(slot * height, height), height), :]
+
+        return lookup
+    order = [shift for held in known_places(STEPS - 1) for shift in held]
+    return lambda shift: tables[pl.ds(order.index(shift) * height, height), :]
+
+
+def weights_kernel(parts, n_rows, positive, first, last, images, row_pos, *refs):
+    row_refs, refs = refs[:n_rows], refs[n_rows:]
     held = slot_counts(parts)
     col_refs, refs = refs[: len(held)], refs[len(held) :]
-    row_loss, col_loss, weights, *txt_parts = refs
+    row_loss, col_loss, weights, *txt_parts, row_scratch = refs
     rows = row_pos.shape[1]
     eye = diagonal(rows)
     onehot = onehot_of(positive[...], eye, parts, rows)
-    row_tables = {}
-    for ref, shifts in zip(row_refs, places):
-        for n, shift in enumerate(shifts):
-            row_tables[shift] = ref[n * 2 * STEPS : (n + 1) * 2 * STEPS, :]
+    row_table = row_table_lookup(row_refs, row_scratch)
+    row_tables = {shift: row_table(shift) for shift in range(1 - STEPS, STEPS)}
     height = table_rows(parts)
     col_tables = []
     for ref, count in zip(col_refs, held):
@@ -218,17 +264,19 @@
             (((0,), (0,)), ((), ())),
             preferred_element_type=F32,
         )
-        txt_parts[s][...] = part.astype(txt_parts[s].dtype)
-
-
-def images_kernel(weights, first, last, *img_parts):
-    rows = img_parts[0].shape[0]
+        for out in txt_parts[2 * s : 2 * s + 2]:
+            out[...] = part.astype(out.dtype)
+
+
+def images_kernel(weights, first, last, own, direct, second, other):
+    rows = own.shape[0]
     split = first.shape[0]
-    for k in range(STEPS):
-        strip = slice(k * rows, (k + 1) * rows)
+    step = direct_step()
+    for out, k in ((other, STEPS - step), (direct, step), (second, 2), (own, 0)):
+        strip = pl.ds(pl.multiple_of(k * rows, rows), rows)
         part = jnp.dot(weights[strip, :split], first[...], preferred_element_type=F32)
         part = part + jnp.dot(weights[strip, split:], last[...], preferred_element_type=F32)
-        img_parts[k][...] = part.astype(img_parts[k].dtype)
+        out[...] = part.astype(out.dtype)
 
 
 def final_kernel(scale, raw, *refs):
@@ -255,14 +303,74 @@
     )(*args)
 
 
+def is_line(parts):
+    return parts == 4
+
+
+def gathered_texts(text):
+    parts = lax.axis_size("rep")
+    if not is_line(parts):
+        return [[fetched(text, "rep", s)] for s in range(1, parts)]
+    from_ends = lax.ppermute(text, "rep", [(0, 2), (3, 1)])
+    near = fetched(text, "rep", 1)
+    to_ends = lax.ppermute(text, "rep", [(1, 3), (2, 0)])
+    middle = lax.ppermute(text, "rep", [(1, 2), (2, 1)])
+    onward = lax.ppermute(from_ends, "rep", [(2, 3), (1, 0)])
+    return [[near], [from_ends, to_ends], [middle, onward]]
+
+
+def returned_texts(parts_of):
+    parts = len(parts_of)
+    if not is_line(parts):
+        return [returned(parts_of[s][1], "rep", s) for s in range(1, parts)]
+    (_, near), (second, second_sent), (_, far) = parts_of[1:]
+    early = lax.ppermute(far, "rep", [(0, 1), (3, 2)])
+    middle = lax.ppermute(far, "rep", [(1, 2), (2, 1)])
+    from_ends = lax.ppermute(second_sent, "rep", [(0, 2), (3, 1)])
+    next_one = returned(near, "rep", 1)
+    joined = (second + early.astype(F32)).astype(BF16)
+    to_ends = lax.ppermute(joined, "rep", [(1, 3), (2, 0)])
+    return [next_one, middle, from_ends, to_ends]
+
+
+def gathered_images(image):
+    direct = lax.ppermute(image, "blk", [(b, a) for a, b in direct_pairs()])
+    second = passed_along(image, "blk", -2)
+    return direct, second, neighbour_swapped(second)
+
+
+def known_row_tables(own):
+    count = lax.axis_size("blk")
+    tables = [own]
+    if whole_axis_known(count):
+        while sum(t.shape[0] for t in tables) < count * own.shape[0]:
+            sent = jnp.concatenate(tables, axis=0)
+            n = len(tables) - 1
+            tables.append(fetched(sent, "blk", 2**n))
+        return tables
+    for n, (shift, known) in enumerate(doublings(STEPS - 1)):
+        by_shift = {}
+        for array, shifts in zip(tables, known_places(STEPS - 1)):
+            for at, shifted in enumerate(shifts):
+                by_shift[shifted] = array[at * 2 * STEPS : (at + 1) * 2 * STEPS]
+        sent = jnp.concatenate([by_shift[t] for t in range(-known, known + 1)], axis=0)
+        for sign in (1, -1):
+            tables.append(passed_along(sent, "blk", -sign * shift))
+    return tables
+
+
 def on_device(image, text, positive, logit_scale):
     rows, width = image.shape
     parts = lax.axis_size("rep")
     height = table_rows(parts)
     shape = jax.ShapeDtypeStruct
-    texts = [text] + [fetched(text, "rep", s) for s in range(1, parts)]
-    images = [image] + [passed_along(image, "blk", -k) for k in range(1, STEPS)]
+    *texts, text_last = gathered_texts(text)
+    direct, second, other = gathered_images(image)
+    own_image, own_text = call(
+        own_kernel, [shape((rows, width), BF16)] * 2, [VMEM] * 2, (image, text)
+    )
     split = (parts - 1) * rows
+    joined_texts = [sum(arrays[1:], arrays[0]) for arrays in texts]
     img_tiles, first, txt_first, row_first, col_first = call(
         functools.partial(first_kernel, parts),
         (
@@ -272,8 +380,8 @@
             shape((2 * STEPS + 1, rows), F32),
             shape((3 * (parts - 1), rows), F32),
         ),
-        [SMEM] + [VMEM] * (STEPS + parts),
-        (logit_scale, positive, *images, *texts[:-1]),
+        [SMEM] + [VMEM] * (6 + len(joined_texts)),
+        (logit_scale, positive, own_image, direct, second, other, own_text, *joined_texts),
     )
     last, txt_last, row_stats, col_stats, row_pos = call(
         functools.partial(last_kernel, parts),
@@ -284,42 +392,38 @@
             shape((height, rows), F32),
             shape((1, rows), F32),
         ),
-        [SMEM] + [VMEM] * 5,
-        (logit_scale, positive, img_tiles, texts[-1], row_first, col_first),
+        [SMEM] + [VMEM] * (4 + len(text_last)),
+        (logit_scale, positive, img_tiles, row_first, col_first, *text_last),
         [pltpu.VMEM((2 * STEPS + 1, rows), F32), pltpu.VMEM((3, rows), F32)],
     )
     col_tables = [col_stats]
     for n, count in enumerate(slot_counts(parts)[1:]):
         sent = jnp.concatenate(col_tables, axis=0)[: count * height]
         col_tables.append(fetched(sent, "rep", 2**n))
-    row_tables = [row_stats]
-    for shift, known in doublings(STEPS - 1):
-        by_shift = {}
-        for array, shifts in zip(row_tables, known_places(STEPS - 1)):
-            for at, place_ in enumerate(shifts):
-                by_shift[place_] = array[at * 2 * STEPS : (at + 1) * 2 * STEPS]
-        sent = jnp.concatenate([by_shift[t] for t in range(-known, known + 1)], axis=0)
-        for sign in (1, -1):
-            row_tables.append(passed_along(sent, "blk", -sign * shift))
+    row_tables = known_row_tables(row_stats)
     row_loss, col_loss, weights, *txt_parts = call(
-        functools.partial(weights_kernel, parts),
+        functools.partial(weights_kernel, parts, len(row_tables)),
         (
             shape((1, rows), F32),
             shape((1, rows), F32),
             shape((STEPS * rows, parts * rows), BF16),
-            *[shape((rows, width), BF16 if s else F32) for s in range(parts)],
+            *[shape((rows, width), t) for _ in range(parts) for t in (F32, BF16)],
         ),
         [VMEM] * (5 + len(row_tables) + len(col_tables)),
         (positive, first, last, img_tiles, row_pos, *row_tables, *col_tables),
-    )
-    txt_sums = [txt_parts[0]] + [returned(txt_parts[s], "rep", s) for s in range(1, parts)]
-    img_parts = call(
+        [pltpu.VMEM((sum(t.shape[0] for t in row_tables), rows), F32)],
+    )
+    txt_parts = list(zip(txt_parts[::2], txt_parts[1::2]))
+    txt_sums = [txt_parts[0][0], *returned_texts(txt_parts)]
+    own, direct, second, other = call(
         images_kernel,
-        [shape((rows, width), BF16 if k else F32) for k in range(STEPS)],
+        [shape((rows, width), t) for t in (F32, BF16, F32, BF16)],
         [VMEM] * 3,
         (weights, txt_first, txt_last),
     )
-    img_sums = [img_parts[0]] + [passed_along(img_parts[k], "blk", k) for k in range(1, STEPS)]
+    swapped = neighbour_swapped(other)
+    joined = (second + swapped.astype(F32)).astype(BF16)
+    img_sums = [own, lax.ppermute(direct, "blk", direct_pairs()), passed_along(joined, "blk", 2)]
     grads = [
         call(
             final_kernel,

time: 77.4 us -> 75 us (0.969)
  the two profiles are of different devices: /device:TPU:8 before, /device:TPU:0 now
where the time goes in v4:
time: 75 us; the launch traced here: 74.6 us
  waiting for transfers between devices  35.2 us (47%)
  starting transfers between devices  27.5 us (37%)
  Pallas kernels  7.71 us (10%)
  local copies, waits for them, and re-layouts  2.56 us (3%)
  between operations  1.51 us (2%)
    ppermute x1, waiting for transfers between devices, on_device(): lax.ppermute(direct, 'blk', direct_pairs())  9.51 us
    pallas_call x7, Pallas kernels, call(): pl.pallas_call(kernel, out_shape=outs, in_specs=[pl.BlockSpec(memory_spac...  7.71 us
    ppermute x1, waiting for transfers between devices, gathered_texts(): to_ends = lax.ppermute(text, 'rep', [(1, 3), (2, 0)])  7.37 us
    ppermute x1, waiting for transfers between devices, returned_texts(): to_ends = lax.ppermute(joined, 'rep', [(1, 3), (2, 0)])  6.74 us
    ppermute x6, waiting for transfers between devices, fetched(): lax.ppermute(array, axis, [(place(i, slot, count), i) for i in range(coun...  6.24 us
    ppermute x1, starting transfers between devices, gathered_texts(): from_ends = lax.ppermute(text, 'rep', [(0, 2), (3, 1)])  5.48 us
    ppermute x6, starting transfers between devices, fetched(): lax.ppermute(array, axis, [(place(i, slot, count), i) for i in range(coun...  4.66 us
    ppermute x2, starting transfers between devices, passed_along(): lax.ppermute(array, axis, [(i, (i + by) % count) for i in range(count)])  3.98 us
  transfers between devices with their start and end apart: 21, of which 9 were waited for; matrix products, arithmetic and copies ran while one was open for 0% of the time, Pallas kernels for 4%

profile of v4, /device:TPU:0, one launch (start us, length us, event | category | flops | bytes accessed | tf_op | source)
XLA Modules:
  0.0 74.6 jit_solution(14732226511454739257)
XLA Ops:
  0.6 4.0 %collective-permute-start.1 = (bf16[128,1024]{1,0:T(8,128)(2,1)}, bf16[128,1024]{1,0:T(8,128)(2,1)S(1)}, u32[]{:S(2)}, u32[]{:S(2)}) collective-permute-start(bf16[128,1024]{1,0:T(8,128)(2,1)} %raw.2), channel_id=1, source_target_pairs={{0,24},{4,28},{8,0},{12,4},{16,8},{20,12},{24,16},{28,20},{1,25},{... | collective-permute-start | bytes 786440 | tf_op jit(solution)/shard_map/ppermute | solution.py:42
  4.6 1.3 %collective-permute-start.5 = (bf16[128,1024]{1,0:T(8,128)(2,1)}, bf16[128,1024]{1,0:T(8,128)(2,1)S(1)}, u32[]{:S(2)}, u32[]{:S(2)}) collective-permute-start(bf16[128,1024]{1,0:T(8,128)(2,1)} %raw.3), channel_id=1, source_target_pairs={{1,3},{2,0},{5,7},{6,4},{9,11},{10,8},{13,15},{14,12},{17,19},{18,... | collective-permute-start | bytes 786440 | tf_op jit(solution)/shard_map/ppermute | solution.py:316
  5.9 5.5 %collective-permute-start.4 = (bf16[128,1024]{1,0:T(8,128)(2,1)}, bf16[128,1024]{1,0:T(8,128)(2,1)S(1)}, u32[]{:S(2)}, u32[]{:S(2)}) collective-permute-start(bf16[128,1024]{1,0:T(8,128)(2,1)} %raw.3), channel_id=1, source_target_pairs={{0,2},{3,1},{4,6},{7,5},{8,10},{11,9},{12,14},{15,13},{16,18},{19,... | collective-permute-start | bytes 786440 | tf_op jit(solution)/shard_map/ppermute | solution.py:314
  11.4 0.7 collective-permute-start.3
  12.3 7.4 %collective-permute-done.5 = bf16[128,1024]{1,0:T(8,128)(2,1)S(1)} collective-permute-done((bf16[128,1024]{1,0:T(8,128)(2,1)}, bf16[128,1024]{1,0:T(8,128)(2,1)S(1)}, u32[]{:S(2)}, u32[]{:S(2)}) %collective-permute-start.5) | collective-permute-done | bytes 262176 | tf_op jit(solution)/shard_map/ppermute | solution.py:316
  19.6 0.7 collective-permute-start.6
  20.3 1.3 %collective-permute-start.7 = (bf16[128,1024]{1,0:T(8,128)(2,1)S(1)}, bf16[128,1024]{1,0:T(8,128)(2,1)S(1)}, u32[]{:S(2)}, u32[]{:S(2)}) collective-permute-start(bf16[128,1024]{1,0:T(8,128)(2,1)S(1)} %collective-permute-done.4), channel_id=1, source_target_pairs={{2,3},{1,0},{6,7},{5,4},{10,11},{9,8},{14,15},{13,12},{18,19},{17,... | collective-permute-start | bytes 786440 | tf_op jit(solution)/shard_map/ppermute | solution.py:318
  21.6 0.9 %copy-done = bf16[128,1024]{1,0:T(8,128)(2,1)S(1)} copy-done((bf16[128,1024]{1,0:T(8,128)(2,1)S(1)}, bf16[128,1024]{1,0:T(8,128)(2,1)}, u32[]{:S(2)}) %copy-start) | copy-done | bytes 262168
  22.6 0.9 %copy-done.2 = bf16[128,1024]{1,0:T(8,128)(2,1)S(1)} copy-done((bf16[128,1024]{1,0:T(8,128)(2,1)S(1)}, bf16[128,1024]{1,0:T(8,128)(2,1)}, u32[]{:S(2)}) %copy-start.2) | copy-done | bytes 262168
  24.5 0.6 copy-done.4
  25.1 1.4 %shard_map.76 = (bf16[512,1024]{1,0:T(8,128)(2,1)S(1)}, f32[512,384]{1,0:T(8,128)S(1)}, bf16[384,1024]{1,0:T(8,128)(2,1)S(1)}, f32[9,128]{1,0:T(8,128)S(1)}, f32[9,128]{1,0:T(8,128)S(1)}) custom-call(f32[1]{0:T(128)S(6)} %copy.8.scale, s32[1,128]{1,0:T(1,128)S(1)} %copy-done.4, bf16[128,1024]{1,0:T(8,128)(2,1)S(1)} %get-tuple-element.28.refs_0_, ...), custom_call_target="tpu_custom_call" | custom-call | tf_op jit(solution)/shard_map/pallas_call | solution.py:296
  26.6 3.5 %collective-permute-done.7.refs_1_ = bf16[128,1024]{1,0:T(8,128)(2,1)S(1)} collective-permute-done((bf16[128,1024]{1,0:T(8,128)(2,1)S(1)}, bf16[128,1024]{1,0:T(8,128)(2,1)S(1)}, u32[]{:S(2)}, u32[]{:S(2)}) %collective-permute-start.7) | collective-permute-done | bytes 262176 | tf_op jit(solution)/shard_map/ppermute | solution.py:318
  30.1 0.8 %shard_map.77 = (f32[512,128]{1,0:T(8,128)S(1)}, bf16[128,1024]{1,0:T(8,128)(2,1)S(1)}, f32[8,128]{1,0:T(8,128)S(1)}, f32[16,128]{1,0:T(8,128)S(1)}, f32[1,128]{1,0:T(1,128)S(1)}) custom-call(f32[1]{0:T(128)S(6)} %copy.8.scale, s32[1,128]{1,0:T(1,128)S(1)} %copy-done.4, bf16[512,1024]{1,0:T(8,128)(2,1)S(1)} %get-tuple-element.31.images, ...), custom_call_target="tpu_custom_call" | custom-call | tf_op jit(solution)/shard_map/pallas_call | solution.py:296
  31.0 0.7 collective-permute-start.11
  31.7 0.5 collective-permute-done.8.refs_1_
  32.1 2.6 %collective-permute-done.11.refs_5_ = f32[16,128]{1,0:T(8,128)S(1)} collective-permute-done((f32[16,128]{1,0:T(8,128)S(1)}, f32[16,128]{1,0:T(8,128)S(1)}, u32[]{:S(2)}, u32[]{:S(2)}) %collective-permute-start.11) | collective-permute-done | bytes 8224 | tf_op jit(solution)/shard_map/ppermute | solution.py:32
  34.7 2.7 %collective-permute-start.12 = (f32[32,128]{1,0:T(8,128)S(1)}, f32[32,128]{1,0:T(8,128)S(1)}, u32[]{:S(2)}, u32[]{:S(2)}) collective-permute-start(f32[32,128]{1,0:T(8,128)S(1)} %pad_maximum_fusion.1), channel_id=1, source_target_pairs={{2,0},{3,1},{0,2},{1,3},{6,4},{7,5},{4,6},{5,7},{10,8},{11,9},{8,1... | collective-permute-start | bytes 49160 | tf_op jit(solution)/shard_map/ppermute | solution.py:32
  37.4 0.5 collective-permute-start.10
  37.9 1.4 %collective-permute-done.12.refs_6_ = f32[32,128]{1,0:T(8,128)S(1)} collective-permute-done((f32[32,128]{1,0:T(8,128)S(1)}, f32[32,128]{1,0:T(8,128)S(1)}, u32[]{:S(2)}, u32[]{:S(2)}) %collective-permute-start.12) | collective-permute-done | bytes 16416 | tf_op jit(solution)/shard_map/ppermute | solution.py:32
  39.3 1.8 %collective-permute-done.10.refs_3_ = f32[32,128]{1,0:T(8,128)S(1)} collective-permute-done((f32[32,128]{1,0:T(8,128)S(1)}, f32[32,128]{1,0:T(8,128)S(1)}, u32[]{:S(2)}, u32[]{:S(2)}) %collective-permute-start.10) | collective-permute-done | bytes 16416 | tf_op jit(solution)/shard_map/ppermute | solution.py:32
  41.1 2.2 %shard_map.78 = (f32[1,128]{1,0:T(1,128)}, f32[1,128]{1,0:T(1,128)}, bf16[512,512]{1,0:T(8,128)(2,1)S(1)}, f32[128,1024]{1,0:T(8,128)S(1)}, bf16[128,1024]{1,0:T...) custom-call(s32[1,128]{1,0:T(1,128)S(1)} %copy-done.4, ...), custom_call_target="tpu_custom_call" | custom-call | tf_op jit(solution)/shard_map/pallas_call | solution.py:296
  43.3 1.0 %shard_map.79 = (f32[128,1024]{1,0:T(8,128)S(1)}, bf16[128,1024]{1,0:T(8,128)(2,1)S(1)}, f32[128,1024]{1,0:T(8,128)S(1)}, bf16[128,1024]{1,0:T(8,128)(2,1)S(1)}) custom-call(bf16[512,512]{1,0:T(8,128)(2,1)S(1)} %get-tuple-element.40.weights, bf16[384,1024]{1,0:T(8,128)(2,1)S(1)} %get-tuple-element.41.first, bf16[128,1024]{1,0:T(8,128)(2,1)S(1)} %get-tuple-element.42.last), custom_call_target="tpu_custom_call" | custom-call | tf_op jit(solution)/shard_map/pallas_call | solution.py:296
  44.3 3.8 %collective-permute-start.19 = (bf16[128,1024]{1,0:T(8,128)(2,1)S(1)}, bf16[128,1024]{1,0:T(8,128)(2,1)S(1)}, u32[]{:S(2)}, u32[]{:S(2)}) collective-permute-start(bf16[128,1024]{1,0:T(8,128)(2,1)S(1)} %get-tuple-element.49), channel_id=1, source_target_pairs={{0,1},{3,2},{4,5},{7,6},{8,9},{11,10},{12,13},{15,14},{16,17},{19,... | collective-permute-start | bytes 786440 | tf_op jit(solution)/shard_map/ppermute | solution.py:327
  48.1 0.7 collective-permute-start.17
  48.8 1.2 %collective-permute-start.16 = (bf16[128,1024]{1,0:T(8,128)(2,1)S(1)}, bf16[128,1024]{1,0:T(8,128)(2,1)S(1)}, u32[]{:S(2)}, u32[]{:S(2)}) collective-permute-start(bf16[128,1024]{1,0:T(8,128)(2,1)S(1)} %get-tuple-element.48), channel_id=1, source_target_pairs={{0,1},{1,0},{2,3},{3,2},{4,5},{5,4},{6,7},{7,6},{8,9},{9,8},{10,11... | collective-permute-start | bytes 786440 | tf_op jit(solution)/shard_map/ppermute | solution.py:37
  50.0 2.8 %collective-permute-start.18 = (bf16[128,1024]{1,0:T(8,128)(2,1)S(1)}, bf16[128,1024]{1,0:T(8,128)(2,1)S(1)}, u32[]{:S(2)}, u32[]{:S(2)}) collective-permute-start(bf16[128,1024]{1,0:T(8,128)(2,1)S(1)} %get-tuple-element.50), channel_id=1, source_target_pairs={{0,2},{3,1},{4,6},{7,5},{8,10},{11,9},{12,14},{15,13},{16,18},{19,... | collective-permute-start | bytes 786440 | tf_op jit(solution)/shard_map/ppermute | solution.py:329
  53.0 1.8 %collective-permute-done.19 = bf16[128,1024]{1,0:T(8,128)(2,1)S(1)} collective-permute-done((bf16[128,1024]{1,0:T(8,128)(2,1)S(1)}, bf16[128,1024]{1,0:T(8,128)(2,1)S(1)}, u32[]{:S(2)}, u32[]{:S(2)}) %collective-permute-start.19) | collective-permute-done | bytes 262176 | tf_op jit(solution)/shard_map/ppermute | solution.py:327
  54.8 9.5 %collective-permute-done.13.refs_1_ = bf16[128,1024]{1,0:T(8,128)(2,1)S(1)} collective-permute-done((bf16[128,1024]{1,0:T(8,128)(2,1)S(1)}, bf16[128,1024]{1,0:T(8,128)(2,1)S(1)}, u32[]{:S(2)}, u32[]{:S(2)}) %collective-permute-start.13) | collective-permute-done | bytes 262176 | tf_op jit(solution)/shard_map/ppermute | solution.py:426
  64.3 1.3 %collective-permute-start.20 = (bf16[128,1024]{1,0:T(8,128)(2,1)S(1)}, bf16[128,1024]{1,0:T(8,128)(2,1)S(1)}, u32[]{:S(2)}, u32[]{:S(2)}) collective-permute-start(bf16[128,1024]{1,0:T(8,128)(2,1)S(1)} %add_convert_fusion), channel_id=1, source_target_pairs={{1,3},{2,0},{5,7},{6,4},{9,11},{10,8},{13,15},{14,12},{17,19},{18,... | collective-permute-start | bytes 786440 | tf_op jit(solution)/shard_map/ppermute | solution.py:332
  65.6 1.1 %shard_map.80 = f32[128,1024]{1,0:T(8,128)} custom-call(f32[1]{0:T(128)S(6)} %copy.8.scale, bf16[128,1024]{1,0:T(8,128)(2,1)S(1)} %copy-done.3, f32[128,1024]{1,0:T(8,128)S(1)} %get-tuple-element.43.refs_0_, bf16[128,1024]{1,0:T(8,128)(2,1)S(1)} %collective-permute-done.13.refs_1_, bf16[128,1024]{1,0:T(8,128)(2,1)S(1)} %collective-permute-done.15.refs_2_), custom_call_target="tpu_custom_call" | custom-call | tf_op jit(solution)/shard_map/pallas_call | solution.py:296
  66.7 6.7 %collective-permute-done.20.refs_4_ = bf16[128,1024]{1,0:T(8,128)(2,1)S(1)} collective-permute-done((bf16[128,1024]{1,0:T(8,128)(2,1)S(1)}, bf16[128,1024]{1,0:T(8,128)(2,1)S(1)}, u32[]{:S(2)}, u32[]{:S(2)}) %collective-permute-start.20) | collective-permute-done | bytes 262176 | tf_op jit(solution)/shard_map/ppermute | solution.py:332
  73.5 1.1 %shard_map.81 = f32[128,1024]{1,0:T(8,128)} custom-call(f32[1]{0:T(128)S(6)} %copy.8.scale, bf16[128,1024]{1,0:T(8,128)(2,1)S(1)} %copy-done.1, f32[128,1024]{1,0:T(8,128)S(1)} %get-tuple-element.47.refs_0_, bf16[128,1024]{1,0:T(8,128)(2,1)S(1)} %collective-permute-done.16.refs_1_, bf16[128,1024]{1,0:T(8,128)(2,1)S(1)} %collective-permute-done.17.refs_2_, ...), custom_call_target="tpu_custom_call" | custom-call | tf_op jit(solution)/shard_map/pallas_call | solution.py:296
  (33 shorter events, 0.8 us)
Async XLA Ops:
  0.6 11.5 %collective-permute-start.1 = (bf16[128,1024]{1,0:T(8,128)(2,1)}, bf16[128,1024]{1,0:T(8,128)(2,1)S(1)}, u32[]{:S(2)}, u32[]{:S(2)}) collective-permute-start(bf16[128,1024]{1,0:T(8,128)(2,1)} %raw.2), channel_id=1, source_target_pairs={{0,24},{4,28},{8,0},{12,4},{16,8},{20,12},{24,16},{28,20},{1,25},{... | collective-permute-start | bytes 786440 | tf_op jit(solution)/shard_map/ppermute | solution.py:42
  4.6 15.0 %collective-permute-start.5 = (bf16[128,1024]{1,0:T(8,128)(2,1)}, bf16[128,1024]{1,0:T(8,128)(2,1)S(1)}, u32[]{:S(2)}, u32[]{:S(2)}) collective-permute-start(bf16[128,1024]{1,0:T(8,128)(2,1)} %raw.3), channel_id=1, source_target_pairs={{1,3},{2,0},{5,7},{6,4},{9,11},{10,8},{13,15},{14,12},{17,19},{18,... | collective-permute-start | bytes 786440 | tf_op jit(solution)/shard_map/ppermute | solution.py:316
  5.9 14.4 %collective-permute-start.4 = (bf16[128,1024]{1,0:T(8,128)(2,1)}, bf16[128,1024]{1,0:T(8,128)(2,1)S(1)}, u32[]{:S(2)}, u32[]{:S(2)}) collective-permute-start(bf16[128,1024]{1,0:T(8,128)(2,1)} %raw.3), channel_id=1, source_target_pairs={{0,2},{3,1},{4,6},{7,5},{8,10},{11,9},{12,14},{15,13},{16,18},{19,... | collective-permute-start | bytes 786440 | tf_op jit(solution)/shard_map/ppermute | solution.py:314
  11.4 13.1 %collective-permute-start = (bf16[128,1024]{1,0:T(8,128)(2,1)}, bf16[128,1024]{1,0:T(8,128)(2,1)S(1)}, u32[]{:S(2)}, u32[]{:S(2)}) collective-permute-start(bf16[128,1024]{1,0:T(8,128)(2,1)} %raw.2), channel_id=1, source_target_pairs={{4,0},{16,4},{12,8},{24,12},{20,16},{0,20},{28,24},{8,28},{5,1},{1... | collective-permute-start | bytes 786440 | tf_op jit(solution)/shard_map/ppermute | solution.py:337
  11.4 13.0 %collective-permute-start.3 = (bf16[128,1024]{1,0:T(8,128)(2,1)}, bf16[128,1024]{1,0:T(8,128)(2,1)S(1)}, u32[]{:S(2)}, u32[]{:S(2)}) collective-permute-start(bf16[128,1024]{1,0:T(8,128)(2,1)} %raw.3), channel_id=1, source_target_pairs={{1,0},{0,1},{3,2},{2,3},{5,4},{4,5},{7,6},{6,7},{9,8},{8,9},{11,10... | collective-permute-start | bytes 786440 | tf_op jit(solution)/shard_map/ppermute | solution.py:32
  12.1 12.4 %collective-permute-start.2 = (bf16[128,1024]{1,0:T(8,128)(2,1)S(1)}, bf16[128,1024]{1,0:T(8,128)(2,1)S(1)}, u32[]{:S(2)}, u32[]{:S(2)}) collective-permute-start(bf16[128,1024]{1,0:T(8,128)(2,1)S(1)} %collective-permute-done.1.refs_2_), channel_id=1, source_target_pairs={{0,4},{4,0},{8,12},{12,8},{16,20},{20,16},{24,28},{28,24},{1,5},{5... | collective-permute-start | bytes 786440 | tf_op jit(solution)/shard_map/ppermute | solution.py:47
  19.6 6.9 %collective-permute-start.6 = (bf16[128,1024]{1,0:T(8,128)(2,1)}, bf16[128,1024]{1,0:T(8,128)(2,1)S(1)}, u32[]{:S(2)}, u32[]{:S(2)}) collective-permute-start(bf16[128,1024]{1,0:T(8,128)(2,1)} %raw.3), channel_id=1, source_target_pairs={{1,2},{2,1},{5,6},{6,5},{9,10},{10,9},{13,14},{14,13},{17,18},{18,... | collective-permute-start | bytes 786440 | tf_op jit(solution)/shard_map/ppermute | solution.py:317
  20.3 9.8 %collective-permute-start.7 = (bf16[128,1024]{1,0:T(8,128)(2,1)S(1)}, bf16[128,1024]{1,0:T(8,128)(2,1)S(1)}, u32[]{:S(2)}, u32[]{:S(2)}) collective-permute-start(bf16[128,1024]{1,0:T(8,128)(2,1)S(1)} %collective-permute-done.4), channel_id=1, source_target_pairs={{2,3},{1,0},{6,7},{5,4},{10,11},{9,8},{14,15},{13,12},{18,19},{17,... | collective-permute-start | bytes 786440 | tf_op jit(solution)/shard_map/ppermute | solution.py:318
  21.6 1.0 %copy-start = (bf16[128,1024]{1,0:T(8,128)(2,1)S(1)}, bf16[128,1024]{1,0:T(8,128)(2,1)}, u32[]{:S(2)}) copy-start(bf16[128,1024]{1,0:T(8,128)(2,1)} %raw.3) | copy-start | bytes 786436
  22.6 0.9 %copy-start.2 = (bf16[128,1024]{1,0:T(8,128)(2,1)S(1)}, bf16[128,1024]{1,0:T(8,128)(2,1)}, u32[]{:S(2)}) copy-start(bf16[128,1024]{1,0:T(8,128)(2,1)} %raw.2) | copy-start | bytes 786436
  24.5 0.7 copy-start.4
  30.9 1.2 %collective-permute-start.8 = (f32[8,128]{1,0:T(8,128)S(1)}, f32[8,128]{1,0:T(8,128)S(1)}, u32[]{:S(2)}, u32[]{:S(2)}) collective-permute-start(f32[8,128]{1,0:T(8,128)S(1)} %get-tuple-element.36.refs_0_), channel_id=1, source_target_pairs={{4,0},{0,4},{12,8},{8,12},{20,16},{16,20},{28,24},{24,28},{5,1},{1... | collective-permute-start | bytes 12296 | tf_op jit(solution)/shard_map/ppermute | solution.py:32
  31.0 3.7 %collective-permute-start.11 = (f32[16,128]{1,0:T(8,128)S(1)}, f32[16,128]{1,0:T(8,128)S(1)}, u32[]{:S(2)}, u32[]{:S(2)}) collective-permute-start(f32[16,128]{1,0:T(8,128)S(1)} %get-tuple-element.37.refs_4_), channel_id=1, source_target_pairs={{1,0},{0,1},{3,2},{2,3},{5,4},{4,5},{7,6},{6,7},{9,8},{8,9},{11,10... | collective-permute-start | bytes 24584 | tf_op jit(solution)/shard_map/ppermute | solution.py:32
  32.1 5.3 %collective-permute-start.9 = (f32[16,128]{1,0:T(8,128)S(1)}, f32[16,128]{1,0:T(8,128)S(1)}, u32[]{:S(2)}, u32[]{:S(2)}) collective-permute-start(f32[16,128]{1,0:T(8,128)S(1)} %pad_maximum_fusion.2), channel_id=1, source_target_pairs={{8,0},{12,4},{0,8},{4,12},{24,16},{28,20},{16,24},{20,28},{9,1},{1... | collective-permute-start | bytes 24584 | tf_op jit(solution)/shard_map/ppermute | solution.py:32
  34.7 4.6 %collective-permute-start.12 = (f32[32,128]{1,0:T(8,128)S(1)}, f32[32,128]{1,0:T(8,128)S(1)}, u32[]{:S(2)}, u32[]{:S(2)}) collective-permute-start(f32[32,128]{1,0:T(8,128)S(1)} %pad_maximum_fusion.1), channel_id=1, source_target_pairs={{2,0},{3,1},{0,2},{1,3},{6,4},{7,5},{4,6},{5,7},{10,8},{11,9},{8,1... | collective-permute-start | bytes 49160 | tf_op jit(solution)/shard_map/ppermute | solution.py:32
  37.4 3.7 %collective-permute-start.10 = (f32[32,128]{1,0:T(8,128)S(1)}, f32[32,128]{1,0:T(8,128)S(1)}, u32[]{:S(2)}, u32[]{:S(2)}) collective-permute-start(f32[32,128]{1,0:T(8,128)S(1)} %pad_maximum_fusion), channel_id=1, source_target_pairs={{16,0},{20,4},{24,8},{28,12},{0,16},{4,20},{8,24},{12,28},{17,1},{... | collective-permute-start | bytes 49160 | tf_op jit(solution)/shard_map/ppermute | solution.py:32
  44.2 8.6 %collective-permute-start.14 = (bf16[128,1024]{1,0:T(8,128)(2,1)S(1)}, bf16[128,1024]{1,0:T(8,128)(2,1)S(1)}, u32[]{:S(2)}, u32[]{:S(2)}) collective-permute-start(bf16[128,1024]{1,0:T(8,128)(2,1)S(1)} %get-tuple-element.46), channel_id=1, source_target_pairs={{0,4},{4,0},{8,12},{12,8},{16,20},{20,16},{24,28},{28,24},{1,5},{5... | collective-permute-start | bytes 786440 | tf_op jit(solution)/shard_map/ppermute | solution.py:47
  44.3 10.4 %collective-permute-start.19 = (bf16[128,1024]{1,0:T(8,128)(2,1)S(1)}, bf16[128,1024]{1,0:T(8,128)(2,1)S(1)}, u32[]{:S(2)}, u32[]{:S(2)}) collective-permute-start(bf16[128,1024]{1,0:T(8,128)(2,1)S(1)} %get-tuple-element.49), channel_id=1, source_target_pairs={{0,1},{3,2},{4,5},{7,6},{8,9},{11,10},{12,13},{15,14},{16,17},{19,... | collective-permute-start | bytes 786440 | tf_op jit(solution)/shard_map/ppermute | solution.py:327
  48.1 18.6 %collective-permute-start.17 = (bf16[128,1024]{1,0:T(8,128)(2,1)S(1)}, bf16[128,1024]{1,0:T(8,128)(2,1)S(1)}, u32[]{:S(2)}, u32[]{:S(2)}) collective-permute-start(bf16[128,1024]{1,0:T(8,128)(2,1)S(1)} %get-tuple-element.49), channel_id=1, source_target_pairs={{1,2},{2,1},{5,6},{6,5},{9,10},{10,9},{13,14},{14,13},{17,18},{18,... | collective-permute-start | bytes 786440 | tf_op jit(solution)/shard_map/ppermute | solution.py:328
  48.8 18.0 %collective-permute-start.16 = (bf16[128,1024]{1,0:T(8,128)(2,1)S(1)}, bf16[128,1024]{1,0:T(8,128)(2,1)S(1)}, u32[]{:S(2)}, u32[]{:S(2)}) collective-permute-start(bf16[128,1024]{1,0:T(8,128)(2,1)S(1)} %get-tuple-element.48), channel_id=1, source_target_pairs={{0,1},{1,0},{2,3},{3,2},{4,5},{5,4},{6,7},{7,6},{8,9},{9,8},{10,11... | collective-permute-start | bytes 786440 | tf_op jit(solution)/shard_map/ppermute | solution.py:37
  50.0 16.7 %collective-permute-start.18 = (bf16[128,1024]{1,0:T(8,128)(2,1)S(1)}, bf16[128,1024]{1,0:T(8,128)(2,1)S(1)}, u32[]{:S(2)}, u32[]{:S(2)}) collective-permute-start(bf16[128,1024]{1,0:T(8,128)(2,1)S(1)} %get-tuple-element.50), channel_id=1, source_target_pairs={{0,2},{3,1},{4,6},{7,5},{8,10},{11,9},{12,14},{15,13},{16,18},{19,... | collective-permute-start | bytes 786440 | tf_op jit(solution)/shard_map/ppermute | solution.py:329
  52.9 11.5 %collective-permute-start.13 = (bf16[128,1024]{1,0:T(8,128)(2,1)S(1)}, bf16[128,1024]{1,0:T(8,128)(2,1)S(1)}, u32[]{:S(2)}, u32[]{:S(2)}) collective-permute-start(bf16[128,1024]{1,0:T(8,128)(2,1)S(1)} %get-tuple-element.44), channel_id=1, source_target_pairs={{0,4},{4,16},{8,12},{12,24},{16,20},{20,0},{24,28},{28,8},{1,5},{5... | collective-permute-start | bytes 786440 | tf_op jit(solution)/shard_map/ppermute | solution.py:426
  54.7 10.9 %collective-permute-start.15 = (bf16[128,1024]{1,0:T(8,128)(2,1)S(1)}, bf16[128,1024]{1,0:T(8,128)(2,1)S(1)}, u32[]{:S(2)}, u32[]{:S(2)}) collective-permute-start(bf16[128,1024]{1,0:T(8,128)(2,1)S(1)} %add_convert_fusion.1), channel_id=1, source_target_pairs={{0,8},{4,12},{8,16},{12,20},{16,24},{20,28},{24,0},{28,4},{1,9},{5... | collective-permute-start | bytes 786440 | tf_op jit(solution)/shard_map/ppermute | solution.py:42
  54.8 10.9 %copy-start.3 = (bf16[128,1024]{1,0:T(8,128)(2,1)S(1)}, bf16[128,1024]{1,0:T(8,128)(2,1)}, u32[]{:S(2)}) copy-start(bf16[128,1024]{1,0:T(8,128)(2,1)} %raw.2) | copy-start | bytes 786436
  64.3 9.2 %collective-permute-start.20 = (bf16[128,1024]{1,0:T(8,128)(2,1)S(1)}, bf16[128,1024]{1,0:T(8,128)(2,1)S(1)}, u32[]{:S(2)}, u32[]{:S(2)}) collective-permute-start(bf16[128,1024]{1,0:T(8,128)(2,1)S(1)} %add_convert_fusion), channel_id=1, source_target_pairs={{1,3},{2,0},{5,7},{6,4},{9,11},{10,8},{13,15},{14,12},{17,19},{18,... | collective-permute-start | bytes 786440 | tf_op jit(solution)/shard_map/ppermute | solution.py:332
  65.6 7.8 %copy-start.1 = (bf16[128,1024]{1,0:T(8,128)(2,1)S(1)}, bf16[128,1024]{1,0:T(8,128)(2,1)}, u32[]{:S(2)}) copy-start(bf16[128,1024]{1,0:T(8,128)(2,1)} %raw.3) | copy-start | bytes 786436

commit v5 on v4

--- a/solution.py
+++ b/solution.py
@@ -92,16 +92,16 @@
     return lax.rsqrt(jnp.sum(wide * wide, axis=-1, keepdims=True) + 1e-06)
 
 
-def store_units(raws, out, base):
-    for at in range(0, raws[0].shape[0], CHUNK):
-        wide = sum(raw[at : at + CHUNK, :].astype(F32) for raw in raws)
+def store_units(raw, out, base):
+    for at in range(0, raw.shape[0], CHUNK):
+        wide = raw[at : at + CHUNK, :].astype(F32)
         here = pl.multiple_of(base + at, CHUNK)
         out[pl.ds(here, CHUNK), :] = (wide * inverse_norm(wide)).astype(BF16)
 
 
 def own_kernel(image, text, img_out, txt_out):
-    store_units([image], img_out, 0)
-    store_units([text], txt_out, 0)
+    store_units(image, img_out, 0)
+    store_units(text, txt_out, 0)
 
 
 def diagonal(rows):
@@ -162,19 +162,24 @@
     rows = own_image.shape[0]
     step = direct_step()
     img_out[:rows, :] = own_image[...]
-    store_units([direct], img_out, step * rows)
-    store_units([second], img_out, 2 * rows)
-    store_units([other], img_out, (STEPS - step) * rows)
+    store_units(direct, img_out, step * rows)
+    store_units(second, img_out, 2 * rows)
+    store_units(other, img_out, (STEPS - step) * rows)
     txt_out[:rows, :] = own_text[...]
-    for n, text in enumerate(texts):
-        store_units([text], txt_out, (n + 1) * rows)
+    for slot, text in zip(near_slots(parts), texts):
+        store_units(text, txt_out, slot * rows)
     slots = range(parts - 1)
     scores_kernel(parts, slots, scale[0], positive[...], img_out, scores, txt_out, *stats)
 
 
 def last_kernel(parts, scale, positive, images, row_first, col_first, *refs):
     *texts, scores, txt_out, row_stats, col_stats, row_pos, row_last, col_last = refs
-    store_units(texts, txt_out, 0)
+    if len(texts) == 1:
+        store_units(texts[0], txt_out, 0)
+    else:
+        end = at_end(parts)
+        pl.when(end)(lambda: store_units(texts[0], txt_out, 0))
+        pl.when(jnp.logical_not(end))(lambda: store_units(texts[1], txt_out, 0))
     slots = [parts - 1]
     scores_kernel(
         parts, slots, scale[0], positive[...], images, scores, txt_out, row_last, col_last
@@ -217,11 +222,11 @@
     return lambda shift: tables[pl.ds(order.index(shift) * height, height), :]
 
 
-def weights_kernel(parts, n_rows, positive, first, last, images, row_pos, *refs):
+def weights_kernel(parts, n_rows, positive, first, last, images, txt_first, txt_last, row_pos, *refs):
     row_refs, refs = refs[:n_rows], refs[n_rows:]
     held = slot_counts(parts)
     col_refs, refs = refs[: len(held)], refs[len(held) :]
-    row_loss, col_loss, weights, *txt_parts, row_scratch = refs
+    row_loss, col_loss, weights, other, *narrow, row_scratch = refs
     rows = row_pos.shape[1]
     eye = diagonal(rows)
     onehot = onehot_of(positive[...], eye, parts, rows)
@@ -257,37 +262,60 @@
             if k == 0:
                 weight = weight - onehot[s].astype(F32)
             weights[k * rows : (k + 1) * rows, s * rows : (s + 1) * rows] = weight.astype(BF16)
-    for s in range(parts):
-        part = lax.dot_general(
-            weights[:, s * rows : (s + 1) * rows],
-            images[...],
-            (((0,), (0,)), ((), ())),
-            preferred_element_type=F32,
-        )
-        for out in txt_parts[2 * s : 2 * s + 2]:
-            out[...] = part.astype(out.dtype)
-
-
-def images_kernel(weights, first, last, own, direct, second, other):
+    for slot, out in zip(sent_slots(parts)[0], narrow):
+        text_part(weights, images, slot, out)
+    other[...] = image_part(weights, txt_first, txt_last, STEPS - direct_step(), rows).astype(BF16)
+
+
+def text_part(weights, images, slot, out):
+    rows = out.shape[0]
+    strip = pl.ds(pl.multiple_of(slot * rows, rows), rows)
+    part = lax.dot_general(
+        weights[:, strip], images[...], (((0,), (0,)), ((), ())), preferred_element_type=F32
+    )
+    out[...] = part.astype(out.dtype)
+
+
+def image_part(weights, first, last, k, rows):
+    strip = pl.ds(pl.multiple_of(k * rows, rows), rows)
+    split = first.shape[0]
+    part = jnp.dot(weights[strip, :split], first[...], preferred_element_type=F32)
+    return part + jnp.dot(weights[strip, split:], last[...], preferred_element_type=F32)
+
+
+def rest_kernel(parts, weights, images, first, last, swapped, own, direct, second, *kept):
     rows = own.shape[0]
-    split = first.shape[0]
-    step = direct_step()
-    for out, k in ((other, STEPS - step), (direct, step), (second, 2), (own, 0)):
-        strip = pl.ds(pl.multiple_of(k * rows, rows), rows)
-        part = jnp.dot(weights[strip, :split], first[...], preferred_element_type=F32)
-        part = part + jnp.dot(weights[strip, split:], last[...], preferred_element_type=F32)
-        out[...] = part.astype(out.dtype)
-
-
-def final_kernel(scale, raw, *refs):
-    grad = refs[-1]
+    joined = image_part(weights, first, last, 2, rows) + swapped[...].astype(F32)
+    second[...] = joined.astype(BF16)
+    direct[...] = image_part(weights, first, last, direct_step(), rows).astype(BF16)
+    own[...] = image_part(weights, first, last, 0, rows)
+    for slot, out in zip(sent_slots(parts)[1], kept):
+        text_part(weights, images, slot, out)
+
+
+def join_kernel(parts, kept, arrived, joined):
+    end = at_end(parts)
+    for at in range(0, kept.shape[0], CHUNK):
+        chunk = slice(at, at + CHUNK)
+        added = jnp.where(end, 0.0, arrived[chunk, :].astype(F32))
+        joined[chunk, :] = (kept[chunk, :] + added).astype(BF16)
+
+
+def final_kernel(n_always, n_end, parts, scale, raw, *refs):
+    *refs, grad = refs
+    always, ends, others = refs[:n_always], refs[n_always : n_always + n_end], refs[n_always + n_end :]
     factor = scale[0]
+    end = at_end(parts)
     for at in range(0, raw.shape[0], CHUNK):
         chunk = slice(at, at + CHUNK)
         wide = raw[chunk, :].astype(F32)
         inverse = inverse_norm(wide)
         unit = wide * inverse
-        total = factor * sum(part[chunk, :].astype(F32) for part in refs[:-1])
+        total = sum(part[chunk, :].astype(F32) for part in always)
+        if ends:
+            at_ends = sum(part[chunk, :].astype(F32) for part in ends)
+            total += jnp.where(end, at_ends, sum(part[chunk, :].astype(F32) for part in others))
+        total = factor * total
         along = jnp.sum(unit * total, axis=-1, keepdims=True)
         grad[chunk, :] = (total - unit * along) * inverse
 
@@ -307,30 +335,54 @@
     return parts == 4
 
 
+def at_end(parts):
+    quarter = lax.axis_index("rep")
+    return (quarter == 0) | (quarter == parts - 1)
+
+
+def near_slots(parts):
+    if not is_line(parts):
+        return list(range(1, parts - 1))
+    first = jnp.where(at_end(parts), 1, 2)
+    return [first, 3 - first]
+
+
+def sent_slots(parts):
+    if not is_line(parts):
+        return list(range(1, parts)), [0]
+    end = at_end(parts)
+    return [jnp.where(end, 3, 1), jnp.where(end, 2, 3)], [0, jnp.where(end, 1, 2)]
+
+
 def gathered_texts(text):
     parts = lax.axis_size("rep")
     if not is_line(parts):
-        return [[fetched(text, "rep", s)] for s in range(1, parts)]
-    from_ends = lax.ppermute(text, "rep", [(0, 2), (3, 1)])
-    near = fetched(text, "rep", 1)
-    to_ends = lax.ppermute(text, "rep", [(1, 3), (2, 0)])
-    middle = lax.ppermute(text, "rep", [(1, 2), (2, 1)])
-    onward = lax.ppermute(from_ends, "rep", [(2, 3), (1, 0)])
-    return [[near], [from_ends, to_ends], [middle, onward]]
-
-
-def returned_texts(parts_of):
-    parts = len(parts_of)
+        texts = [fetched(text, "rep", s) for s in range(1, parts)]
+        return texts[:-1], texts[-1:]
+    one = lax.ppermute(text, "rep", [(0, 2), (3, 1), (1, 0), (2, 3)])
+    two = lax.ppermute(text, "rep", [(0, 1), (3, 2), (1, 3), (2, 0)])
+    middle = lax.ppermute(text, "rep", [(1, 2), (2, 1), (0, 0), (3, 3)])
+    onward = lax.ppermute(one, "rep", [(1, 0), (2, 3), (0, 1), (3, 2)])
+    return [one, two], [onward, middle]
+
+
+def returned_texts(narrow, kept):
+    parts = lax.axis_size("rep")
     if not is_line(parts):
-        return [returned(parts_of[s][1], "rep", s) for s in range(1, parts)]
-    (_, near), (second, second_sent), (_, far) = parts_of[1:]
-    early = lax.ppermute(far, "rep", [(0, 1), (3, 2)])
-    middle = lax.ppermute(far, "rep", [(1, 2), (2, 1)])
-    from_ends = lax.ppermute(second_sent, "rep", [(0, 2), (3, 1)])
-    next_one = returned(near, "rep", 1)
-    joined = (second + early.astype(F32)).astype(BF16)
-    to_ends = lax.ppermute(joined, "rep", [(1, 3), (2, 0)])
-    return [next_one, middle, from_ends, to_ends]
+        back = [returned(part, "rep", s) for s, part in enumerate(narrow, 1)]
+        return [kept[0], *back], [], []
+    early, late = narrow
+    one = lax.ppermute(early, "rep", [(0, 1), (3, 2), (1, 0), (2, 3)])
+    middle = lax.ppermute(late, "rep", [(1, 2), (2, 1), (0, 0), (3, 3)])
+    ends = lax.ppermute(late, "rep", [(0, 2), (3, 1), (1, 0), (2, 3)])
+    joined = call(
+        functools.partial(join_kernel, parts),
+        jax.ShapeDtypeStruct(one.shape, BF16),
+        [VMEM] * 2,
+        (kept[1], one),
+    )
+    joined = lax.ppermute(joined, "rep", [(0, 1), (3, 2), (1, 3), (2, 0)])
+    return [kept[0], joined], [one], [middle, ends]
 
 
 def gathered_images(image):
@@ -364,13 +416,12 @@
     parts = lax.axis_size("rep")
     height = table_rows(parts)
     shape = jax.ShapeDtypeStruct
-    *texts, text_last = gathered_texts(text)
+    texts, text_last = gathered_texts(text)
     direct, second, other = gathered_images(image)
     own_image, own_text = call(
         own_kernel, [shape((rows, width), BF16)] * 2, [VMEM] * 2, (image, text)
     )
     split = (parts - 1) * rows
-    joined_texts = [sum(arrays[1:], arrays[0]) for arrays in texts]
     img_tiles, first, txt_first, row_first, col_first = call(
         functools.partial(first_kernel, parts),
         (
@@ -380,8 +431,8 @@
             shape((2 * STEPS + 1, rows), F32),
             shape((3 * (parts - 1), rows), F32),
         ),
-        [SMEM] + [VMEM] * (6 + len(joined_texts)),
-        (logit_scale, positive, own_image, direct, second, other, own_text, *joined_texts),
+        [SMEM] + [VMEM] * (6 + len(texts)),
+        (logit_scale, positive, own_image, direct, second, other, own_text, *texts),
     )
     last, txt_last, row_stats, col_stats, row_pos = call(
         functools.partial(last_kernel, parts),
@@ -401,38 +452,49 @@
         sent = jnp.concatenate(col_tables, axis=0)[: count * height]
         col_tables.append(fetched(sent, "rep", 2**n))
     row_tables = known_row_tables(row_stats)
-    row_loss, col_loss, weights, *txt_parts = call(
+    narrow_slots, kept_slots = sent_slots(parts)
+    row_loss, col_loss, weights, other, *narrow = call(
         functools.partial(weights_kernel, parts, len(row_tables)),
         (
             shape((1, rows), F32),
             shape((1, rows), F32),
             shape((STEPS * rows, parts * rows), BF16),
-            *[shape((rows, width), t) for _ in range(parts) for t in (F32, BF16)],
+            *[shape((rows, width), BF16) for _ in range(1 + len(narrow_slots))],
         ),
-        [VMEM] * (5 + len(row_tables) + len(col_tables)),
-        (positive, first, last, img_tiles, row_pos, *row_tables, *col_tables),
+        [VMEM] * (7 + len(row_tables) + len(col_tables)),
+        (
+            positive,
+            first,
+            last,
+            img_tiles,
+            txt_first,
+            txt_last,
+            row_pos,
+            *row_tables,
+            *col_tables,
+        ),
         [pltpu.VMEM((sum(t.shape[0] for t in row_tables), rows), F32)],
     )
-    txt_parts = list(zip(txt_parts[::2], txt_parts[1::2]))
-    txt_sums = [txt_parts[0][0], *returned_texts(txt_parts)]
-    own, direct, second, other = call(
-        images_kernel,
-        [shape((rows, width), t) for t in (F32, BF16, F32, BF16)],
-        [VMEM] * 3,
-        (weights, txt_first, txt_last),
-    )
     swapped = neighbour_swapped(other)
-    joined = (second + swapped.astype(F32)).astype(BF16)
-    img_sums = [own, lax.ppermute(direct, "blk", direct_pairs()), passed_along(joined, "blk", 2)]
-    grads = [
-        call(
-            final_kernel,
-            shape((rows, width), F32),
-            [SMEM] + [VMEM] * (1 + len(sums)),
-            (logit_scale, raw, *sums),
+    own, direct, second, *kept = call(
+        functools.partial(rest_kernel, parts),
+        [shape((rows, width), t) for t in (F32, BF16, BF16, *[F32 for _ in kept_slots])],
+        [VMEM] * 5,
+        (weights, img_tiles, txt_first, txt_last, swapped),
+    )
+    img_sums = [own, lax.ppermute(direct, "blk", direct_pairs()), passed_along(second, "blk", 2)]
+    txt_sums = returned_texts(narrow, kept)
+    grads = []
+    for raw, (always, ends, others) in ((image, (img_sums, [], [])), (text, txt_sums)):
+        sums = [*always, *ends, *others]
+        grads.append(
+            call(
+                functools.partial(final_kernel, len(always), len(ends), parts),
+                shape((rows, width), F32),
+                [SMEM] + [VMEM] * (1 + len(sums)),
+                (logit_scale, raw, *sums),
+            )
         )
-        for raw, sums in ((image, img_sums), (text, txt_sums))
-    ]
     return (row_loss[0], col_loss[0], *grads)
 
 

time: 75 us -> 64.7 us (0.86)
  starting transfers between devices: 27.5 us -> 18.2 us
    ppermute x9 -> x8, starting transfers between devices: 18.5 us -> 11.1 us  [the longest x1 2.59 us: gathered_texts(): one = lax.ppermute(text, 'rep', [(0, 2), (3, 1), (1, 0), (2, 3)])]
    ppermute x1, waiting for transfers between devices: 9.51 us -> 4.33 us  [on_device(): lax.ppermute(direct, 'blk', direct_pairs())]
    ppermute x2, waiting for transfers between devices: 0.01 us -> 3.33 us  [passed_along(): lax.ppermute(array, axis, [(i, (i + by) % count) for i in range(count)])]
    ppermute x9 -> x8, waiting for transfers between devices: 19.4 us -> 21.3 us  [the longest x1 9.96 us: returned_texts(): joined = lax.ppermute(joined, 'rep', [(0, 1), (3, 2), (1, 3), (2, 0)])]
    ppermute x6 -> x5, starting transfers between devices: 4.66 us -> 3.01 us  [fetched(): lax.ppermute(array, axis, [(place(i, slot, count), i) for i in range(coun...]
    pallas_call x7 -> x8, Pallas kernels: 7.71 us -> 7.26 us  [call(): pl.pallas_call(kernel, out_shape=outs, in_specs=[pl.BlockSpec(memory_spac...]
    ppermute x6 -> x5, waiting for transfers between devices: 6.24 us -> 6.15 us  [fetched(): lax.ppermute(array, axis, [(place(i, slot, count), i) for i in range(coun...]
  transfers between devices with their start and end apart: 21 -> 19, of which waited for: 9 -> 11; matrix products, arithmetic and copies ran while one was open for 0% -> 0% of each run, Pallas kernels for 4% -> 6%
where the time goes in v5:
time: 64.7 us; the launch traced here: 64.5 us
  waiting for transfers between devices  35.1 us (54%)
  starting transfers between devices  18.2 us (28%)
  Pallas kernels  7.26 us (11%)
  local copies, waits for them, and re-layouts  2.56 us (4%)
  between operations  1.36 us (2%)
    ppermute x1, waiting for transfers between devices, returned_texts(): joined = lax.ppermute(joined, 'rep', [(0, 1), (3, 2), (1, 3), (2, 0)])  9.96 us
    pallas_call x8, Pallas kernels, call(): pl.pallas_call(kernel, out_shape=outs, in_specs=[pl.BlockSpec(memory_spac...  7.26 us
    ppermute x5, waiting for transfers between devices, fetched(): lax.ppermute(array, axis, [(place(i, slot, count), i) for i in range(coun...  6.15 us
    ppermute x1, waiting for transfers between devices, returned_texts(): one = lax.ppermute(early, 'rep', [(0, 1), (3, 2), (1, 0), (2, 3)])  4.79 us
    ppermute x1, waiting for transfers between devices, on_device(): lax.ppermute(direct, 'blk', direct_pairs())  4.33 us
    ppermute x2, starting transfers between devices, passed_along(): lax.ppermute(array, axis, [(i, (i + by) % count) for i in range(count)])  4.03 us
    ppermute x1, waiting for transfers between devices, gathered_texts(): onward = lax.ppermute(one, 'rep', [(1, 0), (2, 3), (0, 1), (3, 2)])  3.43 us
    ppermute x2, waiting for transfers between devices, passed_along(): lax.ppermute(array, axis, [(i, (i + by) % count) for i in range(count)])  3.33 us
  transfers between devices with their start and end apart: 19, of which 11 were waited for; matrix products, arithmetic and copies ran while one was open for 0% of the time, Pallas kernels for 6%

profile of v5, /device:TPU:0, one launch (start us, length us, event | category | flops | bytes accessed | tf_op | source)
XLA Modules:
  0.0 64.5 jit_solution(4034153398911902680)
XLA Ops:
  0.6 4.0 %collective-permute-start.1 = (bf16[128,1024]{1,0:T(8,128)(2,1)}, bf16[128,1024]{1,0:T(8,128)(2,1)S(1)}, u32[]{:S(2)}, u32[]{:S(2)}) collective-permute-start(bf16[128,1024]{1,0:T(8,128)(2,1)} %raw.2), channel_id=1, source_target_pairs={{0,24},{4,28},{8,0},{12,4},{16,8},{20,12},{24,16},{28,20},{1,25},{... | collective-permute-start | bytes 786440 | tf_op jit(solution)/shard_map/ppermute | solution.py:42
  4.6 2.6 %collective-permute-start.3 = (bf16[128,1024]{1,0:T(8,128)(2,1)}, bf16[128,1024]{1,0:T(8,128)(2,1)S(1)}, u32[]{:S(2)}, u32[]{:S(2)}) collective-permute-start(bf16[128,1024]{1,0:T(8,128)(2,1)} %raw.3), channel_id=1, source_target_pairs={{0,2},{3,1},{1,0},{2,3},{4,6},{7,5},{5,4},{6,7},{8,10},{11,9},{9,8... | collective-permute-start | bytes 786440 | tf_op jit(solution)/shard_map/ppermute | solution.py:362
  7.2 3.3 %collective-permute-done.1.refs_2_ = bf16[128,1024]{1,0:T(8,128)(2,1)S(1)} collective-permute-done((bf16[128,1024]{1,0:T(8,128)(2,1)}, bf16[128,1024]{1,0:T(8,128)(2,1)S(1)}, u32[]{:S(2)}, u32[]{:S(2)}) %collective-permute-start.1) | collective-permute-done | bytes 262176 | tf_op jit(solution)/shard_map/ppermute | solution.py:42
  10.5 1.6 %collective-permute-start.6 = (bf16[128,1024]{1,0:T(8,128)(2,1)}, bf16[128,1024]{1,0:T(8,128)(2,1)S(1)}, u32[]{:S(2)}, u32[]{:S(2)}) collective-permute-start(bf16[128,1024]{1,0:T(8,128)(2,1)} %raw.3), channel_id=1, source_target_pairs={{1,2},{2,1},{0,0},{3,3},{5,6},{6,5},{4,4},{7,7},{9,10},{10,9},{8,8... | collective-permute-start | bytes 786440 | tf_op jit(solution)/shard_map/ppermute | solution.py:364
  12.1 2.1 %collective-permute-done.3.refs_5_ = bf16[128,1024]{1,0:T(8,128)(2,1)S(1)} collective-permute-done((bf16[128,1024]{1,0:T(8,128)(2,1)}, bf16[128,1024]{1,0:T(8,128)(2,1)S(1)}, u32[]{:S(2)}, u32[]{:S(2)}) %collective-permute-start.3) | collective-permute-done | bytes 262176 | tf_op jit(solution)/shard_map/ppermute | solution.py:362
  14.2 2.2 %collective-permute-start.5 = (bf16[128,1024]{1,0:T(8,128)(2,1)S(1)}, bf16[128,1024]{1,0:T(8,128)(2,1)S(1)}, u32[]{:S(2)}, u32[]{:S(2)}) collective-permute-start(bf16[128,1024]{1,0:T(8,128)(2,1)S(1)} %collective-permute-done.3.refs_5_), channel_id=1, source_target_pairs={{1,0},{2,3},{0,1},{3,2},{5,4},{6,7},{4,5},{7,6},{9,8},{10,11},{8,9... | collective-permute-start | bytes 786440 | tf_op jit(solution)/shard_map/ppermute | solution.py:365
  16.5 0.9 %copy-done = bf16[128,1024]{1,0:T(8,128)(2,1)S(1)} copy-done((bf16[128,1024]{1,0:T(8,128)(2,1)S(1)}, bf16[128,1024]{1,0:T(8,128)(2,1)}, u32[]{:S(2)}) %copy-start) | copy-done | bytes 262168
  17.4 0.9 %copy-done.2 = bf16[128,1024]{1,0:T(8,128)(2,1)S(1)} copy-done((bf16[128,1024]{1,0:T(8,128)(2,1)S(1)}, bf16[128,1024]{1,0:T(8,128)(2,1)}, u32[]{:S(2)}) %copy-start.2) | copy-done | bytes 262168
  18.4 0.2 shard_map.75
  19.2 1.0 %collective-permute-done.4.refs_6_ = bf16[128,1024]{1,0:T(8,128)(2,1)S(1)} collective-permute-done((bf16[128,1024]{1,0:T(8,128)(2,1)}, bf16[128,1024]{1,0:T(8,128)(2,1)S(1)}, u32[]{:S(2)}, u32[]{:S(2)}) %collective-permute-start.4) | collective-permute-done | bytes 262176 | tf_op jit(solution)/shard_map/ppermute | solution.py:363
  20.2 0.7 %copy-done.4 = s32[1,128]{1,0:T(1,128)S(1)} copy-done((s32[1,128]{1,0:T(1,128)S(1)}, s32[1,128]{1,0:T(1,128)}, u32[]{:S(2)}) %copy-start.4) | copy-done | bytes 536
  20.9 1.4 %shard_map.76 = (bf16[512,1024]{1,0:T(8,128)(2,1)S(1)}, f32[512,384]{1,0:T(8,128)S(1)}, bf16[384,1024]{1,0:T(8,128)(2,1)S(1)}, f32[9,128]{1,0:T(8,128)S(1)}, f32[9,128]{1,0:T(8,128)S(1)}) custom-call(f32[1]{0:T(128)S(6)} %copy.8.scale, s32[1,128]{1,0:T(1,128)S(1)} %copy-done.4, bf16[128,1024]{1,0:T(8,128)(2,1)S(1)} %get-tuple-element.27.refs_0_, ...), custom_call_target="tpu_custom_call" | custom-call | tf_op jit(solution)/shard_map/pallas_call | solution.py:324
  22.3 3.4 %collective-permute-done.5.refs_0_ = bf16[128,1024]{1,0:T(8,128)(2,1)S(1)} collective-permute-done((bf16[128,1024]{1,0:T(8,128)(2,1)S(1)}, bf16[128,1024]{1,0:T(8,128)(2,1)S(1)}, u32[]{:S(2)}, u32[]{:S(2)}) %collective-permute-start.5) | collective-permute-done | bytes 262176 | tf_op jit(solution)/shard_map/ppermute | solution.py:365
  25.7 0.8 %shard_map.77 = (f32[512,128]{1,0:T(8,128)S(1)}, bf16[128,1024]{1,0:T(8,128)(2,1)S(1)}, f32[8,128]{1,0:T(8,128)S(1)}, f32[16,128]{1,0:T(8,128)S(1)}, f32[1,128]{1,0:T(1,128)S(1)}) custom-call(f32[1]{0:T(128)S(6)} %copy.8.scale, s32[1,128]{1,0:T(1,128)S(1)} %copy-done.4, bf16[512,1024]{1,0:T(8,128)(2,1)S(1)} %get-tuple-element.30.images, ...), custom_call_target="tpu_custom_call" | custom-call | tf_op jit(solution)/shard_map/pallas_call | solution.py:324
  26.6 0.8 %collective-permute-start.10 = (f32[16,128]{1,0:T(8,128)S(1)}, f32[16,128]{1,0:T(8,128)S(1)}, u32[]{:S(2)}, u32[]{:S(2)}) collective-permute-start(f32[16,128]{1,0:T(8,128)S(1)} %get-tuple-element.38.refs_4_), channel_id=1, source_target_pairs={{1,0},{0,1},{3,2},{2,3},{5,4},{4,5},{7,6},{6,7},{9,8},{8,9},{11,10... | collective-permute-start | bytes 24584 | tf_op jit(solution)/shard_map/ppermute | solution.py:32
  27.4 0.4 collective-permute-done.7.refs_1_
  27.7 2.6 %collective-permute-done.10.refs_5_ = f32[16,128]{1,0:T(8,128)S(1)} collective-permute-done((f32[16,128]{1,0:T(8,128)S(1)}, f32[16,128]{1,0:T(8,128)S(1)}, u32[]{:S(2)}, u32[]{:S(2)}) %collective-permute-start.10) | collective-permute-done | bytes 8224 | tf_op jit(solution)/shard_map/ppermute | solution.py:32
  30.3 1.6 %collective-permute-start.11 = (f32[32,128]{1,0:T(8,128)S(1)}, f32[32,128]{1,0:T(8,128)S(1)}, u32[]{:S(2)}, u32[]{:S(2)}) collective-permute-start(f32[32,128]{1,0:T(8,128)S(1)} %pad_maximum_fusion.1), channel_id=1, source_target_pairs={{2,0},{3,1},{0,2},{1,3},{6,4},{7,5},{4,6},{5,7},{10,8},{11,9},{8,1... | collective-permute-start | bytes 49160 | tf_op jit(solution)/shard_map/ppermute | solution.py:32
  31.9 0.5 collective-permute-start.9
  32.4 2.5 %collective-permute-done.11.refs_6_ = f32[32,128]{1,0:T(8,128)S(1)} collective-permute-done((f32[32,128]{1,0:T(8,128)S(1)}, f32[32,128]{1,0:T(8,128)S(1)}, u32[]{:S(2)}, u32[]{:S(2)}) %collective-permute-start.11) | collective-permute-done | bytes 16416 | tf_op jit(solution)/shard_map/ppermute | solution.py:32
  34.9 0.7 %collective-permute-done.9.refs_3_ = f32[32,128]{1,0:T(8,128)S(1)} collective-permute-done((f32[32,128]{1,0:T(8,128)S(1)}, f32[32,128]{1,0:T(8,128)S(1)}, u32[]{:S(2)}, u32[]{:S(2)}) %collective-permute-start.9) | collective-permute-done | bytes 16416 | tf_op jit(solution)/shard_map/ppermute | solution.py:32
  35.7 1.5 %shard_map.78 = (f32[1,128]{1,0:T(1,128)}, f32[1,128]{1,0:T(1,128)}, bf16[512,512]{1,0:T(8,128)(2,1)S(1)}, bf16[128,1024]{1,0:T(8,128)(2,1)S(1)}, bf16[128,1024]...) custom-call(s32[1,128]{1,0:T(1,128)S(1)} %copy-done.4, f32[512,384]{1,0:T(8,128)S(1)} %get-tuple-element.29.first, ...), custom_call_target="tpu_custom_call" | custom-call | tf_op jit(solution)/shard_map/pallas_call | solution.py:324
  37.2 1.4 %collective-permute-start.15 = (bf16[128,1024]{1,0:T(8,128)(2,1)S(1)}, bf16[128,1024]{1,0:T(8,128)(2,1)S(1)}, u32[]{:S(2)}, u32[]{:S(2)}) collective-permute-start(bf16[128,1024]{1,0:T(8,128)(2,1)S(1)} %get-tuple-element.48), channel_id=1, source_target_pairs={{0,1},{3,2},{1,0},{2,3},{4,5},{7,6},{5,4},{6,7},{8,9},{11,10},{9,8... | collective-permute-start | bytes 786440 | tf_op jit(solution)/shard_map/ppermute | solution.py:375
  38.6 1.1 %collective-permute-start.18 = (bf16[128,1024]{1,0:T(8,128)(2,1)S(1)}, bf16[128,1024]{1,0:T(8,128)(2,1)S(1)}, u32[]{:S(2)}, u32[]{:S(2)}) collective-permute-start(bf16[128,1024]{1,0:T(8,128)(2,1)S(1)} %get-tuple-element.49), channel_id=1, source_target_pairs={{0,2},{3,1},{1,0},{2,3},{4,6},{7,5},{5,4},{6,7},{8,10},{11,9},{9,8... | collective-permute-start | bytes 786440 | tf_op jit(solution)/shard_map/ppermute | solution.py:377
  39.7 1.1 %shard_map.79 = (f32[128,1024]{1,0:T(8,128)S(1)}, bf16[128,1024]{1,0:T(8,128)(2,1)S(1)}, bf16[128,1024]{1,0:T(8,128)(2,1)S(1)}, f32[128,1024]{1,0:T(8,128)S(1)}, f32[128,1024]{1,0:T(8,128)S(1)}) custom-call(bf16[512,512]{1,0:T(8,128)(2,1)S(1)} %get-tuple-element.41.weights, bf16[512,1024]{1,0:T(8,128)(2,1)S(1)} %get-tuple-element.30.images, ...), custom_call_target="tpu_custom_call" | custom-call | tf_op jit(solution)/shard_map/pallas_call | solution.py:324
  40.9 0.7 %collective-permute-start.17 = (bf16[128,1024]{1,0:T(8,128)(2,1)S(1)}, bf16[128,1024]{1,0:T(8,128)(2,1)S(1)}, u32[]{:S(2)}, u32[]{:S(2)}) collective-permute-start(bf16[128,1024]{1,0:T(8,128)(2,1)S(1)} %get-tuple-element.49), channel_id=1, source_target_pairs={{1,2},{2,1},{0,0},{3,3},{5,6},{6,5},{4,4},{7,7},{9,10},{10,9},{8,8... | collective-permute-start | bytes 786440 | tf_op jit(solution)/shard_map/ppermute | solution.py:376
  41.6 4.8 %collective-permute-done.15.arrived.refs_2_ = bf16[128,1024]{1,0:T(8,128)(2,1)S(1)} collective-permute-done((bf16[128,1024]{1,0:T(8,128)(2,1)S(1)}, bf16[128,1024]{1,0:T(8,128)(2,1)S(1)}, u32[]{:S(2)}, u32[]{:S(2)}) %collective-permute-start.15) | collective-permute-done | bytes 262176 | tf_op jit(solution)/shard_map/ppermute | solution.py:375
  46.5 1.5 %collective-permute-start.16 = (bf16[128,1024]{1,0:T(8,128)(2,1)S(1)}, bf16[128,1024]{1,0:T(8,128)(2,1)S(1)}, u32[]{:S(2)}, u32[]{:S(2)}) collective-permute-start(bf16[128,1024]{1,0:T(8,128)(2,1)S(1)} %shard_map.81), channel_id=1, source_target_pairs={{0,1},{3,2},{1,3},{2,0},{4,5},{7,6},{5,7},{6,4},{8,9},{11,10},{9,1... | collective-permute-start | bytes 786440 | tf_op jit(solution)/shard_map/ppermute | solution.py:384
  47.9 4.3 %collective-permute-done.13.refs_1_ = bf16[128,1024]{1,0:T(8,128)(2,1)S(1)} collective-permute-done((bf16[128,1024]{1,0:T(8,128)(2,1)S(1)}, bf16[128,1024]{1,0:T(8,128)(2,1)S(1)}, u32[]{:S(2)}, u32[]{:S(2)}) %collective-permute-start.13) | collective-permute-done | bytes 262176 | tf_op jit(solution)/shard_map/ppermute | solution.py:485
  52.3 1.1 %shard_map.80 = f32[128,1024]{1,0:T(8,128)} custom-call(f32[1]{0:T(128)S(6)} %copy.8.scale, bf16[128,1024]{1,0:T(8,128)(2,1)S(1)} %copy-done.3, f32[128,1024]{1,0:T(8,128)S(1)} %get-tuple-element.43.refs_0_, bf16[128,1024]{1,0:T(8,128)(2,1)S(1)} %collective-permute-done.13.refs_1_, bf16[128,1024]{1,0:T(8,128)(2,1)S(1)} %collective-permute-done.14.refs_2_), custom_call_target="tpu_custom_call" | custom-call | tf_op jit(solution)/shard_map/pallas_call | solution.py:324
  53.3 10.0 %collective-permute-done.16.refs_1_ = bf16[128,1024]{1,0:T(8,128)(2,1)S(1)} collective-permute-done((bf16[128,1024]{1,0:T(8,128)(2,1)S(1)}, bf16[128,1024]{1,0:T(8,128)(2,1)S(1)}, u32[]{:S(2)}, u32[]{:S(2)}) %collective-permute-start.16) | collective-permute-done | bytes 262176 | tf_op jit(solution)/shard_map/ppermute | solution.py:384
  63.3 1.1 %shard_map.82 = f32[128,1024]{1,0:T(8,128)} custom-call(f32[1]{0:T(128)S(6)} %copy.8.scale, bf16[128,1024]{1,0:T(8,128)(2,1)S(1)} %copy-done.1, f32[128,1024]{1,0:T(8,128)S(1)} %get-tuple-element.46.refs_0_, bf16[128,1024]{1,0:T(8,128)(2,1)S(1)} %collective-permute-done.16.refs_1_, bf16[128,1024]{1,0:T(8,128)(2,1)S(1)} %collective-permute-done.15.arrived.refs_2_, ...), custom_call_target="tpu_custom_call" | custom-call | tf_op jit(solution)/shard_map/pallas_call | solution.py:324
  (27 shorter events, 0.3 us)
Async XLA Ops:
  0.6 9.9 %collective-permute-start.1 = (bf16[128,1024]{1,0:T(8,128)(2,1)}, bf16[128,1024]{1,0:T(8,128)(2,1)S(1)}, u32[]{:S(2)}, u32[]{:S(2)}) collective-permute-start(bf16[128,1024]{1,0:T(8,128)(2,1)} %raw.2), channel_id=1, source_target_pairs={{0,24},{4,28},{8,0},{12,4},{16,8},{20,12},{24,16},{28,20},{1,25},{... | collective-permute-start | bytes 786440 | tf_op jit(solution)/shard_map/ppermute | solution.py:42
  4.6 9.6 %collective-permute-start.3 = (bf16[128,1024]{1,0:T(8,128)(2,1)}, bf16[128,1024]{1,0:T(8,128)(2,1)S(1)}, u32[]{:S(2)}, u32[]{:S(2)}) collective-permute-start(bf16[128,1024]{1,0:T(8,128)(2,1)} %raw.3), channel_id=1, source_target_pairs={{0,2},{3,1},{1,0},{2,3},{4,6},{7,5},{5,4},{6,7},{8,10},{11,9},{9,8... | collective-permute-start | bytes 786440 | tf_op jit(solution)/shard_map/ppermute | solution.py:362
  7.2 12.0 %collective-permute-start = (bf16[128,1024]{1,0:T(8,128)(2,1)}, bf16[128,1024]{1,0:T(8,128)(2,1)S(1)}, u32[]{:S(2)}, u32[]{:S(2)}) collective-permute-start(bf16[128,1024]{1,0:T(8,128)(2,1)} %raw.2), channel_id=1, source_target_pairs={{4,0},{16,4},{12,8},{24,12},{20,16},{0,20},{28,24},{8,28},{5,1},{1... | collective-permute-start | bytes 786440 | tf_op jit(solution)/shard_map/ppermute | solution.py:389
  7.2 13.0 %collective-permute-start.4 = (bf16[128,1024]{1,0:T(8,128)(2,1)}, bf16[128,1024]{1,0:T(8,128)(2,1)S(1)}, u32[]{:S(2)}, u32[]{:S(2)}) collective-permute-start(bf16[128,1024]{1,0:T(8,128)(2,1)} %raw.3), channel_id=1, source_target_pairs={{0,1},{3,2},{1,3},{2,0},{4,5},{7,6},{5,7},{6,4},{8,9},{11,10},{9,1... | collective-permute-start | bytes 786440 | tf_op jit(solution)/shard_map/ppermute | solution.py:363
  10.5 9.7 %collective-permute-start.2 = (bf16[128,1024]{1,0:T(8,128)(2,1)S(1)}, bf16[128,1024]{1,0:T(8,128)(2,1)S(1)}, u32[]{:S(2)}, u32[]{:S(2)}) collective-permute-start(bf16[128,1024]{1,0:T(8,128)(2,1)S(1)} %collective-permute-done.1.refs_2_), channel_id=1, source_target_pairs={{0,4},{4,0},{8,12},{12,8},{16,20},{20,16},{24,28},{28,24},{1,5},{5... | collective-permute-start | bytes 786440 | tf_op jit(solution)/shard_map/ppermute | solution.py:47
  10.5 11.8 %collective-permute-start.6 = (bf16[128,1024]{1,0:T(8,128)(2,1)}, bf16[128,1024]{1,0:T(8,128)(2,1)S(1)}, u32[]{:S(2)}, u32[]{:S(2)}) collective-permute-start(bf16[128,1024]{1,0:T(8,128)(2,1)} %raw.3), channel_id=1, source_target_pairs={{1,2},{2,1},{0,0},{3,3},{5,6},{6,5},{4,4},{7,7},{9,10},{10,9},{8,8... | collective-permute-start | bytes 786440 | tf_op jit(solution)/shard_map/ppermute | solution.py:364
  14.2 11.5 %collective-permute-start.5 = (bf16[128,1024]{1,0:T(8,128)(2,1)S(1)}, bf16[128,1024]{1,0:T(8,128)(2,1)S(1)}, u32[]{:S(2)}, u32[]{:S(2)}) collective-permute-start(bf16[128,1024]{1,0:T(8,128)(2,1)S(1)} %collective-permute-done.3.refs_5_), channel_id=1, source_target_pairs={{1,0},{2,3},{0,1},{3,2},{5,4},{6,7},{4,5},{7,6},{9,8},{10,11},{8,9... | collective-permute-start | bytes 786440 | tf_op jit(solution)/shard_map/ppermute | solution.py:365
  16.5 0.9 %copy-start = (bf16[128,1024]{1,0:T(8,128)(2,1)S(1)}, bf16[128,1024]{1,0:T(8,128)(2,1)}, u32[]{:S(2)}) copy-start(bf16[128,1024]{1,0:T(8,128)(2,1)} %raw.3) | copy-start | bytes 786436
  17.4 0.9 %copy-start.2 = (bf16[128,1024]{1,0:T(8,128)(2,1)S(1)}, bf16[128,1024]{1,0:T(8,128)(2,1)}, u32[]{:S(2)}) copy-start(bf16[128,1024]{1,0:T(8,128)(2,1)} %raw.2) | copy-start | bytes 786436
  20.2 0.7 %copy-start.4 = (s32[1,128]{1,0:T(1,128)S(1)}, s32[1,128]{1,0:T(1,128)}, u32[]{:S(2)}) copy-start(s32[1,128]{1,0:T(1,128)} %positive.5) | copy-start | bytes 1540
  26.5 1.2 %collective-permute-start.7 = (f32[8,128]{1,0:T(8,128)S(1)}, f32[8,128]{1,0:T(8,128)S(1)}, u32[]{:S(2)}, u32[]{:S(2)}) collective-permute-start(f32[8,128]{1,0:T(8,128)S(1)} %get-tuple-element.37.refs_0_), channel_id=1, source_target_pairs={{4,0},{0,4},{12,8},{8,12},{20,16},{16,20},{28,24},{24,28},{5,1},{1... | collective-permute-start | bytes 12296 | tf_op jit(solution)/shard_map/ppermute | solution.py:32
  26.6 3.7 %collective-permute-start.10 = (f32[16,128]{1,0:T(8,128)S(1)}, f32[16,128]{1,0:T(8,128)S(1)}, u32[]{:S(2)}, u32[]{:S(2)}) collective-permute-start(f32[16,128]{1,0:T(8,128)S(1)} %get-tuple-element.38.refs_4_), channel_id=1, source_target_pairs={{1,0},{0,1},{3,2},{2,3},{5,4},{4,5},{7,6},{6,7},{9,8},{8,9},{11,10... | collective-permute-start | bytes 24584 | tf_op jit(solution)/shard_map/ppermute | solution.py:32
  27.7 4.2 %collective-permute-start.8 = (f32[16,128]{1,0:T(8,128)S(1)}, f32[16,128]{1,0:T(8,128)S(1)}, u32[]{:S(2)}, u32[]{:S(2)}) collective-permute-start(f32[16,128]{1,0:T(8,128)S(1)} %pad_maximum_fusion.2), channel_id=1, source_target_pairs={{8,0},{12,4},{0,8},{4,12},{24,16},{28,20},{16,24},{20,28},{9,1},{1... | collective-permute-start | bytes 24584 | tf_op jit(solution)/shard_map/ppermute | solution.py:32
  30.3 4.6 %collective-permute-start.11 = (f32[32,128]{1,0:T(8,128)S(1)}, f32[32,128]{1,0:T(8,128)S(1)}, u32[]{:S(2)}, u32[]{:S(2)}) collective-permute-start(f32[32,128]{1,0:T(8,128)S(1)} %pad_maximum_fusion.1), channel_id=1, source_target_pairs={{2,0},{3,1},{0,2},{1,3},{6,4},{7,5},{4,6},{5,7},{10,8},{11,9},{8,1... | collective-permute-start | bytes 49160 | tf_op jit(solution)/shard_map/ppermute | solution.py:32
  31.9 3.7 %collective-permute-start.9 = (f32[32,128]{1,0:T(8,128)S(1)}, f32[32,128]{1,0:T(8,128)S(1)}, u32[]{:S(2)}, u32[]{:S(2)}) collective-permute-start(f32[32,128]{1,0:T(8,128)S(1)} %pad_maximum_fusion), channel_id=1, source_target_pairs={{16,0},{20,4},{24,8},{28,12},{0,16},{4,20},{8,24},{12,28},{17,1},{... | collective-permute-start | bytes 49160 | tf_op jit(solution)/shard_map/ppermute | solution.py:32
  37.2 2.5 %collective-permute-start.12 = (bf16[128,1024]{1,0:T(8,128)(2,1)S(1)}, bf16[128,1024]{1,0:T(8,128)(2,1)S(1)}, u32[]{:S(2)}, u32[]{:S(2)}) collective-permute-start(bf16[128,1024]{1,0:T(8,128)(2,1)S(1)} %get-tuple-element.42), channel_id=1, source_target_pairs={{0,4},{4,0},{8,12},{12,8},{16,20},{20,16},{24,28},{28,24},{1,5},{5... | collective-permute-start | bytes 786440 | tf_op jit(solution)/shard_map/ppermute | solution.py:47
  37.2 9.2 %collective-permute-start.15 = (bf16[128,1024]{1,0:T(8,128)(2,1)S(1)}, bf16[128,1024]{1,0:T(8,128)(2,1)S(1)}, u32[]{:S(2)}, u32[]{:S(2)}) collective-permute-start(bf16[128,1024]{1,0:T(8,128)(2,1)S(1)} %get-tuple-element.48), channel_id=1, source_target_pairs={{0,1},{3,2},{1,0},{2,3},{4,5},{7,6},{5,4},{6,7},{8,9},{11,10},{9,8... | collective-permute-start | bytes 786440 | tf_op jit(solution)/shard_map/ppermute | solution.py:375
  38.6 14.7 %collective-permute-start.18 = (bf16[128,1024]{1,0:T(8,128)(2,1)S(1)}, bf16[128,1024]{1,0:T(8,128)(2,1)S(1)}, u32[]{:S(2)}, u32[]{:S(2)}) collective-permute-start(bf16[128,1024]{1,0:T(8,128)(2,1)S(1)} %get-tuple-element.49), channel_id=1, source_target_pairs={{0,2},{3,1},{1,0},{2,3},{4,6},{7,5},{5,4},{6,7},{8,10},{11,9},{9,8... | collective-permute-start | bytes 786440 | tf_op jit(solution)/shard_map/ppermute | solution.py:377
  40.8 11.5 %collective-permute-start.13 = (bf16[128,1024]{1,0:T(8,128)(2,1)S(1)}, bf16[128,1024]{1,0:T(8,128)(2,1)S(1)}, u32[]{:S(2)}, u32[]{:S(2)}) collective-permute-start(bf16[128,1024]{1,0:T(8,128)(2,1)S(1)} %get-tuple-element.44), channel_id=1, source_target_pairs={{0,4},{4,16},{8,12},{12,24},{16,20},{20,0},{24,28},{28,8},{1,5},{5... | collective-permute-start | bytes 786440 | tf_op jit(solution)/shard_map/ppermute | solution.py:485
  40.9 11.4 %collective-permute-start.14 = (bf16[128,1024]{1,0:T(8,128)(2,1)S(1)}, bf16[128,1024]{1,0:T(8,128)(2,1)S(1)}, u32[]{:S(2)}, u32[]{:S(2)}) collective-permute-start(bf16[128,1024]{1,0:T(8,128)(2,1)S(1)} %get-tuple-element.45), channel_id=1, source_target_pairs={{0,8},{4,12},{8,16},{12,20},{16,24},{20,28},{24,0},{28,4},{1,9},{5... | collective-permute-start | bytes 786440 | tf_op jit(solution)/shard_map/ppermute | solution.py:42
  40.9 12.4 %collective-permute-start.17 = (bf16[128,1024]{1,0:T(8,128)(2,1)S(1)}, bf16[128,1024]{1,0:T(8,128)(2,1)S(1)}, u32[]{:S(2)}, u32[]{:S(2)}) collective-permute-start(bf16[128,1024]{1,0:T(8,128)(2,1)S(1)} %get-tuple-element.49), channel_id=1, source_target_pairs={{1,2},{2,1},{0,0},{3,3},{5,6},{6,5},{4,4},{7,7},{9,10},{10,9},{8,8... | collective-permute-start | bytes 786440 | tf_op jit(solution)/shard_map/ppermute | solution.py:376
  46.4 5.9 %copy-start.3 = (bf16[128,1024]{1,0:T(8,128)(2,1)S(1)}, bf16[128,1024]{1,0:T(8,128)(2,1)}, u32[]{:S(2)}) copy-start(bf16[128,1024]{1,0:T(8,128)(2,1)} %raw.2) | copy-start | bytes 786436
  46.5 16.8 %collective-permute-start.16 = (bf16[128,1024]{1,0:T(8,128)(2,1)S(1)}, bf16[128,1024]{1,0:T(8,128)(2,1)S(1)}, u32[]{:S(2)}, u32[]{:S(2)}) collective-permute-start(bf16[128,1024]{1,0:T(8,128)(2,1)S(1)} %shard_map.81), channel_id=1, source_target_pairs={{0,1},{3,2},{1,3},{2,0},{4,5},{7,6},{5,7},{6,4},{8,9},{11,10},{9,1... | collective-permute-start | bytes 786440 | tf_op jit(solution)/shard_map/ppermute | solution.py:384
  52.3 11.0 %copy-start.1 = (bf16[128,1024]{1,0:T(8,128)(2,1)S(1)}, bf16[128,1024]{1,0:T(8,128)(2,1)}, u32[]{:S(2)}) copy-start(bf16[128,1024]{1,0:T(8,128)(2,1)} %raw.3) | copy-start | bytes 786436

commit v6 on v5

--- a/solution.py
+++ b/solution.py
@@ -40,6 +40,16 @@
 def passed_along(array, axis, by):
     count = lax.axis_size(axis)
     return lax.ppermute(array, axis, [(i, (i + by) % count) for i in range(count)])
+
+
+def middle_swapped(array):
+    parts, blocks = lax.axis_size("rep"), lax.axis_size("blk")
+    pairs = [
+        (b * parts + r, b * parts + parts - 1 - r if 0 < r < parts - 1 else (b ^ 1) * parts + r)
+        for b in range(blocks)
+        for r in range(parts)
+    ]
+    return lax.ppermute(array, ("blk", "rep"), pairs)
 
 
 def neighbour_swapped(array):
@@ -361,7 +371,7 @@
         return texts[:-1], texts[-1:]
     one = lax.ppermute(text, "rep", [(0, 2), (3, 1), (1, 0), (2, 3)])
     two = lax.ppermute(text, "rep", [(0, 1), (3, 2), (1, 3), (2, 0)])
-    middle = lax.ppermute(text, "rep", [(1, 2), (2, 1), (0, 0), (3, 3)])
+    middle = middle_swapped(text)
     onward = lax.ppermute(one, "rep", [(1, 0), (2, 3), (0, 1), (3, 2)])
     return [one, two], [onward, middle]
 
@@ -373,7 +383,7 @@
         return [kept[0], *back], [], []
     early, late = narrow
     one = lax.ppermute(early, "rep", [(0, 1), (3, 2), (1, 0), (2, 3)])
-    middle = lax.ppermute(late, "rep", [(1, 2), (2, 1), (0, 0), (3, 3)])
+    middle = middle_swapped(late)
     ends = lax.ppermute(late, "rep", [(0, 2), (3, 1), (1, 0), (2, 3)])
     joined = call(
         functools.partial(join_kernel, parts),

time: 64.7 us -> 62.4 us (0.964)
  waiting for transfers between devices: 35.1 us -> 33.1 us
    ppermute x1, waiting for transfers between devices: 9.96 us -> 8.16 us  [returned_texts(): joined = lax.ppermute(joined, 'rep', [(0, 1), (3, 2), (1, 3), (2, 0)])]
    ppermute x5, starting transfers between devices: 3.01 us -> 4.16 us  [fetched(): lax.ppermute(array, axis, [(place(i, slot, count), i) for i in range(coun...]
    ppermute x1, waiting for transfers between devices: 2.12 us -> 3.21 us  [gathered_texts(): one = lax.ppermute(text, 'rep', [(0, 2), (3, 1), (1, 0), (2, 3)])]
  transfers between devices with their start and end apart: 19 -> 19, of which waited for: 11 -> 10; matrix products, arithmetic and copies ran while one was open for 0% -> 0% of each run, Pallas kernels for 6% -> 6%
where the time goes in v6:
time: 62.4 us; the launch traced here: 62.2 us
  waiting for transfers between devices  33.1 us (53%)
  starting transfers between devices  18 us (29%)
  Pallas kernels  7.26 us (12%)
  local copies, waits for them, and re-layouts  2.56 us (4%)
  between operations  1.36 us (2%)
    ppermute x1, waiting for transfers between devices, returned_texts(): joined = lax.ppermute(joined, 'rep', [(0, 1), (3, 2), (1, 3), (2, 0)])  8.16 us
    pallas_call x8, Pallas kernels, call(): pl.pallas_call(kernel, out_shape=outs, in_specs=[pl.BlockSpec(memory_spac...  7.26 us
    ppermute x5, waiting for transfers between devices, fetched(): lax.ppermute(array, axis, [(place(i, slot, count), i) for i in range(coun...  5.57 us
    ppermute x1, waiting for transfers between devices, returned_texts(): one = lax.ppermute(early, 'rep', [(0, 1), (3, 2), (1, 0), (2, 3)])  4.63 us
    ppermute x1, waiting for transfers between devices, on_device(): lax.ppermute(direct, 'blk', direct_pairs())  4.33 us
    ppermute x5, starting transfers between devices, fetched(): lax.ppermute(array, axis, [(place(i, slot, count), i) for i in range(coun...  4.16 us
    ppermute x2, starting transfers between devices, passed_along(): lax.ppermute(array, axis, [(i, (i + by) % count) for i in range(count)])  4.03 us
    ppermute x2, waiting for transfers between devices, passed_along(): lax.ppermute(array, axis, [(i, (i + by) % count) for i in range(count)])  3.33 us
  transfers between devices with their start and end apart: 19, of which 10 were waited for; matrix products, arithmetic and copies ran while one was open for 0% of the time, Pallas kernels for 6%

profile of v6, /device:TPU:0, one launch (start us, length us, event | category | flops | bytes accessed | tf_op | source)
XLA Modules:
  0.0 62.2 jit_solution(9782904190844682617)
XLA Ops:
  0.6 4.0 %collective-permute-start.1 = (bf16[128,1024]{1,0:T(8,128)(2,1)}, bf16[128,1024]{1,0:T(8,128)(2,1)S(1)}, u32[]{:S(2)}, u32[]{:S(2)}) collective-permute-start(bf16[128,1024]{1,0:T(8,128)(2,1)} %raw.2), channel_id=1, source_target_pairs={{0,24},{4,28},{8,0},{12,4},{16,8},{20,12},{24,16},{28,20},{1,25},{... | collective-permute-start | bytes 786440 | tf_op jit(solution)/shard_map/ppermute | solution.py:42
  4.6 2.6 %collective-permute-start.3 = (bf16[128,1024]{1,0:T(8,128)(2,1)}, bf16[128,1024]{1,0:T(8,128)(2,1)S(1)}, u32[]{:S(2)}, u32[]{:S(2)}) collective-permute-start(bf16[128,1024]{1,0:T(8,128)(2,1)} %raw.3), channel_id=1, source_target_pairs={{0,2},{3,1},{1,0},{2,3},{4,6},{7,5},{5,4},{6,7},{8,10},{11,9},{9,8... | collective-permute-start | bytes 786440 | tf_op jit(solution)/shard_map/ppermute | solution.py:372
  7.2 3.3 %collective-permute-done.1.refs_2_ = bf16[128,1024]{1,0:T(8,128)(2,1)S(1)} collective-permute-done((bf16[128,1024]{1,0:T(8,128)(2,1)}, bf16[128,1024]{1,0:T(8,128)(2,1)S(1)}, u32[]{:S(2)}, u32[]{:S(2)}) %collective-permute-start.1) | collective-permute-done | bytes 262176 | tf_op jit(solution)/shard_map/ppermute | solution.py:42
  10.5 0.5 collective-permute-start.6
  11.0 3.2 %collective-permute-done.3.refs_5_ = bf16[128,1024]{1,0:T(8,128)(2,1)S(1)} collective-permute-done((bf16[128,1024]{1,0:T(8,128)(2,1)}, bf16[128,1024]{1,0:T(8,128)(2,1)S(1)}, u32[]{:S(2)}, u32[]{:S(2)}) %collective-permute-start.3) | collective-permute-done | bytes 262176 | tf_op jit(solution)/shard_map/ppermute | solution.py:372
  14.2 2.2 %collective-permute-start.5 = (bf16[128,1024]{1,0:T(8,128)(2,1)S(1)}, bf16[128,1024]{1,0:T(8,128)(2,1)S(1)}, u32[]{:S(2)}, u32[]{:S(2)}) collective-permute-start(bf16[128,1024]{1,0:T(8,128)(2,1)S(1)} %collective-permute-done.3.refs_5_), channel_id=1, source_target_pairs={{1,0},{2,3},{0,1},{3,2},{5,4},{6,7},{4,5},{7,6},{9,8},{10,11},{8,9... | collective-permute-start | bytes 786440 | tf_op jit(solution)/shard_map/ppermute | solution.py:375
  16.5 0.9 %copy-done = bf16[128,1024]{1,0:T(8,128)(2,1)S(1)} copy-done((bf16[128,1024]{1,0:T(8,128)(2,1)S(1)}, bf16[128,1024]{1,0:T(8,128)(2,1)}, u32[]{:S(2)}) %copy-start) | copy-done | bytes 262168
  17.4 0.9 %copy-done.2 = bf16[128,1024]{1,0:T(8,128)(2,1)S(1)} copy-done((bf16[128,1024]{1,0:T(8,128)(2,1)S(1)}, bf16[128,1024]{1,0:T(8,128)(2,1)}, u32[]{:S(2)}) %copy-start.2) | copy-done | bytes 262168
  18.4 0.2 shard_map.75
  19.2 1.0 %collective-permute-done.4.refs_6_ = bf16[128,1024]{1,0:T(8,128)(2,1)S(1)} collective-permute-done((bf16[128,1024]{1,0:T(8,128)(2,1)}, bf16[128,1024]{1,0:T(8,128)(2,1)S(1)}, u32[]{:S(2)}, u32[]{:S(2)}) %collective-permute-start.4) | collective-permute-done | bytes 262176 | tf_op jit(solution)/shard_map/ppermute | solution.py:373
  20.2 0.7 %copy-done.4 = s32[1,128]{1,0:T(1,128)S(1)} copy-done((s32[1,128]{1,0:T(1,128)S(1)}, s32[1,128]{1,0:T(1,128)}, u32[]{:S(2)}) %copy-start.4) | copy-done | bytes 536
  20.9 1.4 %shard_map.76 = (bf16[512,1024]{1,0:T(8,128)(2,1)S(1)}, f32[512,384]{1,0:T(8,128)S(1)}, bf16[384,1024]{1,0:T(8,128)(2,1)S(1)}, f32[9,128]{1,0:T(8,128)S(1)}, f32[9,128]{1,0:T(8,128)S(1)}) custom-call(f32[1]{0:T(128)S(6)} %copy.8.scale, s32[1,128]{1,0:T(1,128)S(1)} %copy-done.4, bf16[128,1024]{1,0:T(8,128)(2,1)S(1)} %get-tuple-element.27.refs_0_, ...), custom_call_target="tpu_custom_call" | custom-call | tf_op jit(solution)/shard_map/pallas_call | solution.py:334
  22.3 2.8 %collective-permute-done.5.refs_0_ = bf16[128,1024]{1,0:T(8,128)(2,1)S(1)} collective-permute-done((bf16[128,1024]{1,0:T(8,128)(2,1)S(1)}, bf16[128,1024]{1,0:T(8,128)(2,1)S(1)}, u32[]{:S(2)}, u32[]{:S(2)}) %collective-permute-start.5) | collective-permute-done | bytes 262176 | tf_op jit(solution)/shard_map/ppermute | solution.py:375
  25.1 0.8 %shard_map.77 = (f32[512,128]{1,0:T(8,128)S(1)}, bf16[128,1024]{1,0:T(8,128)(2,1)S(1)}, f32[8,128]{1,0:T(8,128)S(1)}, f32[16,128]{1,0:T(8,128)S(1)}, f32[1,128]{1,0:T(1,128)S(1)}) custom-call(f32[1]{0:T(128)S(6)} %copy.8.scale, s32[1,128]{1,0:T(1,128)S(1)} %copy-done.4, bf16[512,1024]{1,0:T(8,128)(2,1)S(1)} %get-tuple-element.30.images, ...), custom_call_target="tpu_custom_call" | custom-call | tf_op jit(solution)/shard_map/pallas_call | solution.py:334
  25.9 0.1 collective-permute-start.7
  26.0 1.4 %collective-permute-start.10 = (f32[16,128]{1,0:T(8,128)S(1)}, f32[16,128]{1,0:T(8,128)S(1)}, u32[]{:S(2)}, u32[]{:S(2)}) collective-permute-start(f32[16,128]{1,0:T(8,128)S(1)} %get-tuple-element.38.refs_4_), channel_id=1, source_target_pairs={{1,0},{0,1},{3,2},{2,3},{5,4},{4,5},{7,6},{6,7},{9,8},{8,9},{11,10... | collective-permute-start | bytes 24584 | tf_op jit(solution)/shard_map/ppermute | solution.py:32
  27.4 2.3 %collective-permute-done.10.refs_5_ = f32[16,128]{1,0:T(8,128)S(1)} collective-permute-done((f32[16,128]{1,0:T(8,128)S(1)}, f32[16,128]{1,0:T(8,128)S(1)}, u32[]{:S(2)}, u32[]{:S(2)}) %collective-permute-start.10) | collective-permute-done | bytes 8224 | tf_op jit(solution)/shard_map/ppermute | solution.py:32
  29.7 2.2 %collective-permute-start.11 = (f32[32,128]{1,0:T(8,128)S(1)}, f32[32,128]{1,0:T(8,128)S(1)}, u32[]{:S(2)}, u32[]{:S(2)}) collective-permute-start(f32[32,128]{1,0:T(8,128)S(1)} %pad_maximum_fusion.1), channel_id=1, source_target_pairs={{2,0},{3,1},{0,2},{1,3},{6,4},{7,5},{4,6},{5,7},{10,8},{11,9},{8,1... | collective-permute-start | bytes 49160 | tf_op jit(solution)/shard_map/ppermute | solution.py:32
  31.9 0.5 collective-permute-start.9
  32.4 1.9 %collective-permute-done.11.refs_6_ = f32[32,128]{1,0:T(8,128)S(1)} collective-permute-done((f32[32,128]{1,0:T(8,128)S(1)}, f32[32,128]{1,0:T(8,128)S(1)}, u32[]{:S(2)}, u32[]{:S(2)}) %collective-permute-start.11) | collective-permute-done | bytes 16416 | tf_op jit(solution)/shard_map/ppermute | solution.py:32
  34.4 1.3 %collective-permute-done.9.refs_3_ = f32[32,128]{1,0:T(8,128)S(1)} collective-permute-done((f32[32,128]{1,0:T(8,128)S(1)}, f32[32,128]{1,0:T(8,128)S(1)}, u32[]{:S(2)}, u32[]{:S(2)}) %collective-permute-start.9) | collective-permute-done | bytes 16416 | tf_op jit(solution)/shard_map/ppermute | solution.py:32
  35.7 1.5 %shard_map.78 = (f32[1,128]{1,0:T(1,128)}, f32[1,128]{1,0:T(1,128)}, bf16[512,512]{1,0:T(8,128)(2,1)S(1)}, bf16[128,1024]{1,0:T(8,128)(2,1)S(1)}, bf16[128,1024]...) custom-call(s32[1,128]{1,0:T(1,128)S(1)} %copy-done.4, f32[512,384]{1,0:T(8,128)S(1)} %get-tuple-element.29.first, ...), custom_call_target="tpu_custom_call" | custom-call | tf_op jit(solution)/shard_map/pallas_call | solution.py:334
  37.2 1.0 %collective-permute-start.15 = (bf16[128,1024]{1,0:T(8,128)(2,1)S(1)}, bf16[128,1024]{1,0:T(8,128)(2,1)S(1)}, u32[]{:S(2)}, u32[]{:S(2)}) collective-permute-start(bf16[128,1024]{1,0:T(8,128)(2,1)S(1)} %get-tuple-element.48), channel_id=1, source_target_pairs={{0,1},{3,2},{1,0},{2,3},{4,5},{7,6},{5,4},{6,7},{8,9},{11,10},{9,8... | collective-permute-start | bytes 786440 | tf_op jit(solution)/shard_map/ppermute | solution.py:385
  38.2 1.1 %collective-permute-start.18 = (bf16[128,1024]{1,0:T(8,128)(2,1)S(1)}, bf16[128,1024]{1,0:T(8,128)(2,1)S(1)}, u32[]{:S(2)}, u32[]{:S(2)}) collective-permute-start(bf16[128,1024]{1,0:T(8,128)(2,1)S(1)} %get-tuple-element.49), channel_id=1, source_target_pairs={{0,2},{3,1},{1,0},{2,3},{4,6},{7,5},{5,4},{6,7},{8,10},{11,9},{9,8... | collective-permute-start | bytes 786440 | tf_op jit(solution)/shard_map/ppermute | solution.py:387
  39.3 1.1 %shard_map.79 = (f32[128,1024]{1,0:T(8,128)S(1)}, bf16[128,1024]{1,0:T(8,128)(2,1)S(1)}, bf16[128,1024]{1,0:T(8,128)(2,1)S(1)}, f32[128,1024]{1,0:T(8,128)S(1)}, f32[128,1024]{1,0:T(8,128)S(1)}) custom-call(bf16[512,512]{1,0:T(8,128)(2,1)S(1)} %get-tuple-element.41.weights, bf16[512,1024]{1,0:T(8,128)(2,1)S(1)} %get-tuple-element.30.images, ...), custom_call_target="tpu_custom_call" | custom-call | tf_op jit(solution)/shard_map/pallas_call | solution.py:334
  40.5 1.3 %collective-permute-start.17 = (bf16[128,1024]{1,0:T(8,128)(2,1)S(1)}, bf16[128,1024]{1,0:T(8,128)(2,1)S(1)}, u32[]{:S(2)}, u32[]{:S(2)}) collective-permute-start(bf16[128,1024]{1,0:T(8,128)(2,1)S(1)} %get-tuple-element.49), channel_id=1, source_target_pairs={{0,4},{1,2},{2,1},{3,7},{4,0},{5,6},{6,5},{7,3},{8,12},{9,10},{10,... | collective-permute-start | bytes 786440 | tf_op jit(solution)/shard_map/ppermute | solution.py:52
  41.8 4.6 %collective-permute-done.15.arrived.refs_2_ = bf16[128,1024]{1,0:T(8,128)(2,1)S(1)} collective-permute-done((bf16[128,1024]{1,0:T(8,128)(2,1)S(1)}, bf16[128,1024]{1,0:T(8,128)(2,1)S(1)}, u32[]{:S(2)}, u32[]{:S(2)}) %collective-permute-start.15) | collective-permute-done | bytes 262176 | tf_op jit(solution)/shard_map/ppermute | solution.py:385
  46.5 1.0 %collective-permute-start.16 = (bf16[128,1024]{1,0:T(8,128)(2,1)S(1)}, bf16[128,1024]{1,0:T(8,128)(2,1)S(1)}, u32[]{:S(2)}, u32[]{:S(2)}) collective-permute-start(bf16[128,1024]{1,0:T(8,128)(2,1)S(1)} %shard_map.81), channel_id=1, source_target_pairs={{0,1},{3,2},{1,3},{2,0},{4,5},{7,6},{5,7},{6,4},{8,9},{11,10},{9,1... | collective-permute-start | bytes 786440 | tf_op jit(solution)/shard_map/ppermute | solution.py:394
  47.5 4.3 %collective-permute-done.13.refs_1_ = bf16[128,1024]{1,0:T(8,128)(2,1)S(1)} collective-permute-done((bf16[128,1024]{1,0:T(8,128)(2,1)S(1)}, bf16[128,1024]{1,0:T(8,128)(2,1)S(1)}, u32[]{:S(2)}, u32[]{:S(2)}) %collective-permute-start.13) | collective-permute-done | bytes 262176 | tf_op jit(solution)/shard_map/ppermute | solution.py:495
  51.8 1.1 %shard_map.80 = f32[128,1024]{1,0:T(8,128)} custom-call(f32[1]{0:T(128)S(6)} %copy.8.scale, bf16[128,1024]{1,0:T(8,128)(2,1)S(1)} %copy-done.3, f32[128,1024]{1,0:T(8,128)S(1)} %get-tuple-element.43.refs_0_, bf16[128,1024]{1,0:T(8,128)(2,1)S(1)} %collective-permute-done.13.refs_1_, bf16[128,1024]{1,0:T(8,128)(2,1)S(1)} %collective-permute-done.14.refs_2_), custom_call_target="tpu_custom_call" | custom-call | tf_op jit(solution)/shard_map/pallas_call | solution.py:334
  52.9 8.2 %collective-permute-done.16.refs_1_ = bf16[128,1024]{1,0:T(8,128)(2,1)S(1)} collective-permute-done((bf16[128,1024]{1,0:T(8,128)(2,1)S(1)}, bf16[128,1024]{1,0:T(8,128)(2,1)S(1)}, u32[]{:S(2)}, u32[]{:S(2)}) %collective-permute-start.16) | collective-permute-done | bytes 262176 | tf_op jit(solution)/shard_map/ppermute | solution.py:394
  61.1 1.1 %shard_map.82 = f32[128,1024]{1,0:T(8,128)} custom-call(f32[1]{0:T(128)S(6)} %copy.8.scale, bf16[128,1024]{1,0:T(8,128)(2,1)S(1)} %copy-done.1, f32[128,1024]{1,0:T(8,128)S(1)} %get-tuple-element.46.refs_0_, bf16[128,1024]{1,0:T(8,128)(2,1)S(1)} %collective-permute-done.16.refs_1_, bf16[128,1024]{1,0:T(8,128)(2,1)S(1)} %collective-permute-done.15.arrived.refs_2_, ...), custom_call_target="tpu_custom_call" | custom-call | tf_op jit(solution)/shard_map/pallas_call | solution.py:334
  (27 shorter events, 0.2 us)
Async XLA Ops:
  0.6 9.9 %collective-permute-start.1 = (bf16[128,1024]{1,0:T(8,128)(2,1)}, bf16[128,1024]{1,0:T(8,128)(2,1)S(1)}, u32[]{:S(2)}, u32[]{:S(2)}) collective-permute-start(bf16[128,1024]{1,0:T(8,128)(2,1)} %raw.2), channel_id=1, source_target_pairs={{0,24},{4,28},{8,0},{12,4},{16,8},{20,12},{24,16},{28,20},{1,25},{... | collective-permute-start | bytes 786440 | tf_op jit(solution)/shard_map/ppermute | solution.py:42
  4.6 9.6 %collective-permute-start.3 = (bf16[128,1024]{1,0:T(8,128)(2,1)}, bf16[128,1024]{1,0:T(8,128)(2,1)S(1)}, u32[]{:S(2)}, u32[]{:S(2)}) collective-permute-start(bf16[128,1024]{1,0:T(8,128)(2,1)} %raw.3), channel_id=1, source_target_pairs={{0,2},{3,1},{1,0},{2,3},{4,6},{7,5},{5,4},{6,7},{8,10},{11,9},{9,8... | collective-permute-start | bytes 786440 | tf_op jit(solution)/shard_map/ppermute | solution.py:372
  7.2 12.0 %collective-permute-start = (bf16[128,1024]{1,0:T(8,128)(2,1)}, bf16[128,1024]{1,0:T(8,128)(2,1)S(1)}, u32[]{:S(2)}, u32[]{:S(2)}) collective-permute-start(bf16[128,1024]{1,0:T(8,128)(2,1)} %raw.2), channel_id=1, source_target_pairs={{4,0},{16,4},{12,8},{24,12},{20,16},{0,20},{28,24},{8,28},{5,1},{1... | collective-permute-start | bytes 786440 | tf_op jit(solution)/shard_map/ppermute | solution.py:399
  7.2 13.0 %collective-permute-start.4 = (bf16[128,1024]{1,0:T(8,128)(2,1)}, bf16[128,1024]{1,0:T(8,128)(2,1)S(1)}, u32[]{:S(2)}, u32[]{:S(2)}) collective-permute-start(bf16[128,1024]{1,0:T(8,128)(2,1)} %raw.3), channel_id=1, source_target_pairs={{0,1},{3,2},{1,3},{2,0},{4,5},{7,6},{5,7},{6,4},{8,9},{11,10},{9,1... | collective-permute-start | bytes 786440 | tf_op jit(solution)/shard_map/ppermute | solution.py:373
  10.5 9.7 %collective-permute-start.2 = (bf16[128,1024]{1,0:T(8,128)(2,1)S(1)}, bf16[128,1024]{1,0:T(8,128)(2,1)S(1)}, u32[]{:S(2)}, u32[]{:S(2)}) collective-permute-start(bf16[128,1024]{1,0:T(8,128)(2,1)S(1)} %collective-permute-done.1.refs_2_), channel_id=1, source_target_pairs={{0,4},{4,0},{8,12},{12,8},{16,20},{20,16},{24,28},{28,24},{1,5},{5... | collective-permute-start | bytes 786440 | tf_op jit(solution)/shard_map/ppermute | solution.py:57
  10.5 11.8 %collective-permute-start.6 = (bf16[128,1024]{1,0:T(8,128)(2,1)}, bf16[128,1024]{1,0:T(8,128)(2,1)S(1)}, u32[]{:S(2)}, u32[]{:S(2)}) collective-permute-start(bf16[128,1024]{1,0:T(8,128)(2,1)} %raw.3), channel_id=1, source_target_pairs={{0,4},{1,2},{2,1},{3,7},{4,0},{5,6},{6,5},{7,3},{8,12},{9,10},{10,... | collective-permute-start | bytes 786440 | tf_op jit(solution)/shard_map/ppermute | solution.py:52
  14.2 10.9 %collective-permute-start.5 = (bf16[128,1024]{1,0:T(8,128)(2,1)S(1)}, bf16[128,1024]{1,0:T(8,128)(2,1)S(1)}, u32[]{:S(2)}, u32[]{:S(2)}) collective-permute-start(bf16[128,1024]{1,0:T(8,128)(2,1)S(1)} %collective-permute-done.3.refs_5_), channel_id=1, source_target_pairs={{1,0},{2,3},{0,1},{3,2},{5,4},{6,7},{4,5},{7,6},{9,8},{10,11},{8,9... | collective-permute-start | bytes 786440 | tf_op jit(solution)/shard_map/ppermute | solution.py:375
  16.5 0.9 %copy-start = (bf16[128,1024]{1,0:T(8,128)(2,1)S(1)}, bf16[128,1024]{1,0:T(8,128)(2,1)}, u32[]{:S(2)}) copy-start(bf16[128,1024]{1,0:T(8,128)(2,1)} %raw.3) | copy-start | bytes 786436
  17.4 0.9 %copy-start.2 = (bf16[128,1024]{1,0:T(8,128)(2,1)S(1)}, bf16[128,1024]{1,0:T(8,128)(2,1)}, u32[]{:S(2)}) copy-start(bf16[128,1024]{1,0:T(8,128)(2,1)} %raw.2) | copy-start | bytes 786436
  20.2 0.7 %copy-start.4 = (s32[1,128]{1,0:T(1,128)S(1)}, s32[1,128]{1,0:T(1,128)}, u32[]{:S(2)}) copy-start(s32[1,128]{1,0:T(1,128)} %positive.5) | copy-start | bytes 1540
  25.9 1.5 %collective-permute-start.7 = (f32[8,128]{1,0:T(8,128)S(1)}, f32[8,128]{1,0:T(8,128)S(1)}, u32[]{:S(2)}, u32[]{:S(2)}) collective-permute-start(f32[8,128]{1,0:T(8,128)S(1)} %get-tuple-element.37.refs_0_), channel_id=1, source_target_pairs={{4,0},{0,4},{12,8},{8,12},{20,16},{16,20},{28,24},{24,28},{5,1},{1... | collective-permute-start | bytes 12296 | tf_op jit(solution)/shard_map/ppermute | solution.py:32
  26.0 3.7 %collective-permute-start.10 = (f32[16,128]{1,0:T(8,128)S(1)}, f32[16,128]{1,0:T(8,128)S(1)}, u32[]{:S(2)}, u32[]{:S(2)}) collective-permute-start(f32[16,128]{1,0:T(8,128)S(1)} %get-tuple-element.38.refs_4_), channel_id=1, source_target_pairs={{1,0},{0,1},{3,2},{2,3},{5,4},{4,5},{7,6},{6,7},{9,8},{8,9},{11,10... | collective-permute-start | bytes 24584 | tf_op jit(solution)/shard_map/ppermute | solution.py:32
  27.4 4.6 %collective-permute-start.8 = (f32[16,128]{1,0:T(8,128)S(1)}, f32[16,128]{1,0:T(8,128)S(1)}, u32[]{:S(2)}, u32[]{:S(2)}) collective-permute-start(f32[16,128]{1,0:T(8,128)S(1)} %pad_maximum_fusion.2), channel_id=1, source_target_pairs={{8,0},{12,4},{0,8},{4,12},{24,16},{28,20},{16,24},{20,28},{9,1},{1... | collective-permute-start | bytes 24584 | tf_op jit(solution)/shard_map/ppermute | solution.py:32
  29.7 4.6 %collective-permute-start.11 = (f32[32,128]{1,0:T(8,128)S(1)}, f32[32,128]{1,0:T(8,128)S(1)}, u32[]{:S(2)}, u32[]{:S(2)}) collective-permute-start(f32[32,128]{1,0:T(8,128)S(1)} %pad_maximum_fusion.1), channel_id=1, source_target_pairs={{2,0},{3,1},{0,2},{1,3},{6,4},{7,5},{4,6},{5,7},{10,8},{11,9},{8,1... | collective-permute-start | bytes 49160 | tf_op jit(solution)/shard_map/ppermute | solution.py:32
  31.9 3.7 %collective-permute-start.9 = (f32[32,128]{1,0:T(8,128)S(1)}, f32[32,128]{1,0:T(8,128)S(1)}, u32[]{:S(2)}, u32[]{:S(2)}) collective-permute-start(f32[32,128]{1,0:T(8,128)S(1)} %pad_maximum_fusion), channel_id=1, source_target_pairs={{16,0},{20,4},{24,8},{28,12},{0,16},{4,20},{8,24},{12,28},{17,1},{... | collective-permute-start | bytes 49160 | tf_op jit(solution)/shard_map/ppermute | solution.py:32
  37.2 2.1 %collective-permute-start.12 = (bf16[128,1024]{1,0:T(8,128)(2,1)S(1)}, bf16[128,1024]{1,0:T(8,128)(2,1)S(1)}, u32[]{:S(2)}, u32[]{:S(2)}) collective-permute-start(bf16[128,1024]{1,0:T(8,128)(2,1)S(1)} %get-tuple-element.42), channel_id=1, source_target_pairs={{0,4},{4,0},{8,12},{12,8},{16,20},{20,16},{24,28},{28,24},{1,5},{5... | collective-permute-start | bytes 786440 | tf_op jit(solution)/shard_map/ppermute | solution.py:57
  37.2 9.2 %collective-permute-start.15 = (bf16[128,1024]{1,0:T(8,128)(2,1)S(1)}, bf16[128,1024]{1,0:T(8,128)(2,1)S(1)}, u32[]{:S(2)}, u32[]{:S(2)}) collective-permute-start(bf16[128,1024]{1,0:T(8,128)(2,1)S(1)} %get-tuple-element.48), channel_id=1, source_target_pairs={{0,1},{3,2},{1,0},{2,3},{4,5},{7,6},{5,4},{6,7},{8,9},{11,10},{9,8... | collective-permute-start | bytes 786440 | tf_op jit(solution)/shard_map/ppermute | solution.py:385
  38.2 14.7 %collective-permute-start.18 = (bf16[128,1024]{1,0:T(8,128)(2,1)S(1)}, bf16[128,1024]{1,0:T(8,128)(2,1)S(1)}, u32[]{:S(2)}, u32[]{:S(2)}) collective-permute-start(bf16[128,1024]{1,0:T(8,128)(2,1)S(1)} %get-tuple-element.49), channel_id=1, source_target_pairs={{0,2},{3,1},{1,0},{2,3},{4,6},{7,5},{5,4},{6,7},{8,10},{11,9},{9,8... | collective-permute-start | bytes 786440 | tf_op jit(solution)/shard_map/ppermute | solution.py:387
  40.4 11.5 %collective-permute-start.13 = (bf16[128,1024]{1,0:T(8,128)(2,1)S(1)}, bf16[128,1024]{1,0:T(8,128)(2,1)S(1)}, u32[]{:S(2)}, u32[]{:S(2)}) collective-permute-start(bf16[128,1024]{1,0:T(8,128)(2,1)S(1)} %get-tuple-element.44), channel_id=1, source_target_pairs={{0,4},{4,16},{8,12},{12,24},{16,20},{20,0},{24,28},{28,8},{1,5},{5... | collective-permute-start | bytes 786440 | tf_op jit(solution)/shard_map/ppermute | solution.py:495
  40.4 11.4 %collective-permute-start.14 = (bf16[128,1024]{1,0:T(8,128)(2,1)S(1)}, bf16[128,1024]{1,0:T(8,128)(2,1)S(1)}, u32[]{:S(2)}, u32[]{:S(2)}) collective-permute-start(bf16[128,1024]{1,0:T(8,128)(2,1)S(1)} %get-tuple-element.45), channel_id=1, source_target_pairs={{0,8},{4,12},{8,16},{12,20},{16,24},{20,28},{24,0},{28,4},{1,9},{5... | collective-permute-start | bytes 786440 | tf_op jit(solution)/shard_map/ppermute | solution.py:42
  40.5 12.4 %collective-permute-start.17 = (bf16[128,1024]{1,0:T(8,128)(2,1)S(1)}, bf16[128,1024]{1,0:T(8,128)(2,1)S(1)}, u32[]{:S(2)}, u32[]{:S(2)}) collective-permute-start(bf16[128,1024]{1,0:T(8,128)(2,1)S(1)} %get-tuple-element.49), channel_id=1, source_target_pairs={{0,4},{1,2},{2,1},{3,7},{4,0},{5,6},{6,5},{7,3},{8,12},{9,10},{10,... | collective-permute-start | bytes 786440 | tf_op jit(solution)/shard_map/ppermute | solution.py:52
  46.4 5.4 %copy-start.3 = (bf16[128,1024]{1,0:T(8,128)(2,1)S(1)}, bf16[128,1024]{1,0:T(8,128)(2,1)}, u32[]{:S(2)}) copy-start(bf16[128,1024]{1,0:T(8,128)(2,1)} %raw.2) | copy-start | bytes 786436
  46.5 14.6 %collective-permute-start.16 = (bf16[128,1024]{1,0:T(8,128)(2,1)S(1)}, bf16[128,1024]{1,0:T(8,128)(2,1)S(1)}, u32[]{:S(2)}, u32[]{:S(2)}) collective-permute-start(bf16[128,1024]{1,0:T(8,128)(2,1)S(1)} %shard_map.81), channel_id=1, source_target_pairs={{0,1},{3,2},{1,3},{2,0},{4,5},{7,6},{5,7},{6,4},{8,9},{11,10},{9,1... | collective-permute-start | bytes 786440 | tf_op jit(solution)/shard_map/ppermute | solution.py:394
  51.8 9.3 %copy-start.1 = (bf16[128,1024]{1,0:T(8,128)(2,1)S(1)}, bf16[128,1024]{1,0:T(8,128)(2,1)}, u32[]{:S(2)}) copy-start(bf16[128,1024]{1,0:T(8,128)(2,1)} %raw.3) | copy-start | bytes 786436

commit v7 on v6

--- a/solution.py
+++ b/solution.py
@@ -232,12 +232,12 @@
     return lambda shift: tables[pl.ds(order.index(shift) * height, height), :]
 
 
-def weights_kernel(parts, n_rows, positive, first, last, images, txt_first, txt_last, row_pos, *refs):
+def weights_kernel(parts, n_rows, positive, first, last, images, txt_first, txt_last, *refs):
     row_refs, refs = refs[:n_rows], refs[n_rows:]
     held = slot_counts(parts)
     col_refs, refs = refs[: len(held)], refs[len(held) :]
-    row_loss, col_loss, weights, other, *narrow, row_scratch = refs
-    rows = row_pos.shape[1]
+    row_out, col_out, col_picked, weights, other, *narrow, row_scratch = refs
+    rows = positive.shape[1]
     eye = diagonal(rows)
     onehot = onehot_of(positive[...], eye, parts, rows)
     row_table = row_table_lookup(row_refs, row_scratch)
@@ -255,14 +255,15 @@
     for k in range(STEPS):
         lse = merged([row_pair(t, k) for t in range(1 - STEPS, STEPS) if 0 <= k - t < STEPS])
         if k == 0:
-            row_loss[...] = lse - row_pos[...]
+            row_out[...] = lse
         row_lse.append(to_column(lse, eye))
     col_lse = []
     for s in range(parts):
         at = [(col_tables[t], slot_at(s, t, parts)) for t in range(parts)]
         lse = merged([(c[q : q + 1, :], c[parts + q : parts + q + 1, :]) for c, q in at])
         if s == 0:
-            col_loss[...] = lse - sum(c[2 * parts + q : 2 * parts + q + 1, :] for c, q in at)
+            col_out[...] = lse
+            col_picked[...] = sum(c[2 * parts + q : 2 * parts + q + 1, :] for c, q in at)
         col_lse.append(lse)
     for s in range(parts):
         source, base = (first, s * rows) if s < parts - 1 else (last, 0)
@@ -293,14 +294,17 @@
     return part + jnp.dot(weights[strip, split:], last[...], preferred_element_type=F32)
 
 
-def rest_kernel(parts, weights, images, first, last, swapped, own, direct, second, *kept):
-    rows = own.shape[0]
+def passed_kernel(weights, first, last, swapped, direct, second):
+    rows = second.shape[0]
     joined = image_part(weights, first, last, 2, rows) + swapped[...].astype(F32)
     second[...] = joined.astype(BF16)
     direct[...] = image_part(weights, first, last, direct_step(), rows).astype(BF16)
-    own[...] = image_part(weights, first, last, 0, rows)
-    for slot, out in zip(sent_slots(parts)[1], kept):
+
+
+def rest_kernel(parts, weights, images, first, last, own, *kept):
+    for slot, out in reversed(list(zip(sent_slots(parts)[1], kept))):
         text_part(weights, images, slot, out)
+    own[...] = image_part(weights, first, last, 0, own.shape[0])
 
 
 def join_kernel(parts, kept, arrived, joined):
@@ -463,15 +467,14 @@
         col_tables.append(fetched(sent, "rep", 2**n))
     row_tables = known_row_tables(row_stats)
     narrow_slots, kept_slots = sent_slots(parts)
-    row_loss, col_loss, weights, other, *narrow = call(
+    row_lse, col_lse, col_pos, weights, other, *narrow = call(
         functools.partial(weights_kernel, parts, len(row_tables)),
         (
-            shape((1, rows), F32),
-            shape((1, rows), F32),
+            *[shape((1, rows), F32)] * 3,
             shape((STEPS * rows, parts * rows), BF16),
             *[shape((rows, width), BF16) for _ in range(1 + len(narrow_slots))],
         ),
-        [VMEM] * (7 + len(row_tables) + len(col_tables)),
+        [VMEM] * (6 + len(row_tables) + len(col_tables)),
         (
             positive,
             first,
@@ -479,18 +482,23 @@
             img_tiles,
             txt_first,
             txt_last,
-            row_pos,
             *row_tables,
             *col_tables,
         ),
         [pltpu.VMEM((sum(t.shape[0] for t in row_tables), rows), F32)],
     )
     swapped = neighbour_swapped(other)
-    own, direct, second, *kept = call(
+    direct, second = call(
+        passed_kernel,
+        [shape((rows, width), BF16)] * 2,
+        [VMEM] * 4,
+        (weights, txt_first, txt_last, swapped),
+    )
+    own, *kept = call(
         functools.partial(rest_kernel, parts),
-        [shape((rows, width), t) for t in (F32, BF16, BF16, *[F32 for _ in kept_slots])],
-        [VMEM] * 5,
-        (weights, img_tiles, txt_first, txt_last, swapped),
+        [shape((rows, width), F32) for _ in range(1 + len(kept_slots))],
+        [VMEM] * 4,
+        (weights, img_tiles, txt_first, txt_last),
     )
     img_sums = [own, lax.ppermute(direct, "blk", direct_pairs()), passed_along(second, "blk", 2)]
     txt_sums = returned_texts(narrow, kept)
@@ -505,7 +513,9 @@
                 (logit_scale, raw, *sums),
             )
         )
-    return (row_loss[0], col_loss[0], *grads)
+    row_loss = row_lse[0] - row_pos[0]
+    col_loss = col_lse[0] - col_pos[0]
+    return (row_loss, col_loss, *grads)
 
 
 def solution(mesh):

time: 62.4 us -> 60.1 us (0.963)
  waiting for transfers between devices: 33.1 us -> 30 us
    ppermute x1, waiting for transfers between devices: 8.16 us -> 6.75 us  [returned_texts(): joined = lax.ppermute(joined, 'rep', [(0, 1), (3, 2), (1, 3), (2, 0)])]
    ppermute x1, waiting for transfers between devices: 4.33 us -> 3.16 us  [on_device(): lax.ppermute(direct, 'blk', direct_pairs())]
    ppermute x2, starting transfers between devices: 1.78 us -> 0.72 us  [middle_swapped(): return lax.ppermute(array, ('blk', 'rep'), pairs)]
    ppermute x1, starting transfers between devices: 1.1 us -> 2.11 us  [returned_texts(): ends = lax.ppermute(late, 'rep', [(0, 2), (3, 1), (1, 0), (2, 3)])]
    pallas_call x8 -> x9, Pallas kernels: 7.26 us -> 7.03 us  [call(): pl.pallas_call(kernel, out_shape=outs, in_specs=[pl.BlockSpec(memory_spac...]
  transfers between devices with their start and end apart: 19 -> 19, of which waited for: 10 -> 10; matrix products, arithmetic and copies ran while one was open for 0% -> 1% of each run, Pallas kernels for 6% -> 7%
where the time goes in v7:
time: 60.1 us; the launch traced here: 59.9 us
  waiting for transfers between devices  30 us (50%)
  starting transfers between devices  18.4 us (31%)
  Pallas kernels  7.03 us (12%)
  local copies, waits for them, and re-layouts  2.56 us (4%)
  between operations  1.37 us (2%)
    pallas_call x9, Pallas kernels, call(): pl.pallas_call(kernel, out_shape=outs, in_specs=[pl.BlockSpec(memory_spac...  7.03 us
    ppermute x1, waiting for transfers between devices, returned_texts(): joined = lax.ppermute(joined, 'rep', [(0, 1), (3, 2), (1, 3), (2, 0)])  6.75 us
    ppermute x5, waiting for transfers between devices, fetched(): lax.ppermute(array, axis, [(place(i, slot, count), i) for i in range(coun...  5.57 us
    ppermute x5, starting transfers between devices, fetched(): lax.ppermute(array, axis, [(place(i, slot, count), i) for i in range(coun...  4.16 us
    ppermute x1, waiting for transfers between devices, returned_texts(): one = lax.ppermute(early, 'rep', [(0, 1), (3, 2), (1, 0), (2, 3)])  4.15 us
    ppermute x2, starting transfers between devices, passed_along(): lax.ppermute(array, axis, [(i, (i + by) % count) for i in range(count)])  3.98 us
    ppermute x2, waiting for transfers between devices, passed_along(): lax.ppermute(array, axis, [(i, (i + by) % count) for i in range(count)])  3.33 us
    ppermute x1, waiting for transfers between devices, gathered_texts(): one = lax.ppermute(text, 'rep', [(0, 2), (3, 1), (1, 0), (2, 3)])  3.21 us
  transfers between devices with their start and end apart: 19, of which 10 were waited for; matrix products, arithmetic and copies ran while one was open for 1% of the time, Pallas kernels for 7%

profile of v7, /device:TPU:0, one launch (start us, length us, event | category | flops | bytes accessed | tf_op | source)
XLA Modules:
  0.0 59.9 jit_solution(15156030068836417152)
XLA Ops:
  0.6 4.0 %collective-permute-start.1 = (bf16[128,1024]{1,0:T(8,128)(2,1)}, bf16[128,1024]{1,0:T(8,128)(2,1)S(1)}, u32[]{:S(2)}, u32[]{:S(2)}) collective-permute-start(bf16[128,1024]{1,0:T(8,128)(2,1)} %raw.2), channel_id=1, source_target_pairs={{0,24},{4,28},{8,0},{12,4},{16,8},{20,12},{24,16},{28,20},{1,25},{... | collective-permute-start | bytes 786440 | tf_op jit(solution)/shard_map/ppermute | solution.py:42
  4.6 2.6 %collective-permute-start.3 = (bf16[128,1024]{1,0:T(8,128)(2,1)}, bf16[128,1024]{1,0:T(8,128)(2,1)S(1)}, u32[]{:S(2)}, u32[]{:S(2)}) collective-permute-start(bf16[128,1024]{1,0:T(8,128)(2,1)} %raw.3), channel_id=1, source_target_pairs={{0,2},{3,1},{1,0},{2,3},{4,6},{7,5},{5,4},{6,7},{8,10},{11,9},{9,8... | collective-permute-start | bytes 786440 | tf_op jit(solution)/shard_map/ppermute | solution.py:376
  7.2 3.3 %collective-permute-done.1.refs_2_ = bf16[128,1024]{1,0:T(8,128)(2,1)S(1)} collective-permute-done((bf16[128,1024]{1,0:T(8,128)(2,1)}, bf16[128,1024]{1,0:T(8,128)(2,1)S(1)}, u32[]{:S(2)}, u32[]{:S(2)}) %collective-permute-start.1) | collective-permute-done | bytes 262176 | tf_op jit(solution)/shard_map/ppermute | solution.py:42
  10.5 0.5 collective-permute-start.6
  11.0 3.2 %collective-permute-done.3.refs_5_ = bf16[128,1024]{1,0:T(8,128)(2,1)S(1)} collective-permute-done((bf16[128,1024]{1,0:T(8,128)(2,1)}, bf16[128,1024]{1,0:T(8,128)(2,1)S(1)}, u32[]{:S(2)}, u32[]{:S(2)}) %collective-permute-start.3) | collective-permute-done | bytes 262176 | tf_op jit(solution)/shard_map/ppermute | solution.py:376
  14.2 2.2 %collective-permute-start.5 = (bf16[128,1024]{1,0:T(8,128)(2,1)S(1)}, bf16[128,1024]{1,0:T(8,128)(2,1)S(1)}, u32[]{:S(2)}, u32[]{:S(2)}) collective-permute-start(bf16[128,1024]{1,0:T(8,128)(2,1)S(1)} %collective-permute-done.3.refs_5_), channel_id=1, source_target_pairs={{1,0},{2,3},{0,1},{3,2},{5,4},{6,7},{4,5},{7,6},{9,8},{10,11},{8,9... | collective-permute-start | bytes 786440 | tf_op jit(solution)/shard_map/ppermute | solution.py:379
  16.5 0.9 %copy-done = bf16[128,1024]{1,0:T(8,128)(2,1)S(1)} copy-done((bf16[128,1024]{1,0:T(8,128)(2,1)S(1)}, bf16[128,1024]{1,0:T(8,128)(2,1)}, u32[]{:S(2)}) %copy-start) | copy-done | bytes 262168
  17.4 0.9 %copy-done.2 = bf16[128,1024]{1,0:T(8,128)(2,1)S(1)} copy-done((bf16[128,1024]{1,0:T(8,128)(2,1)S(1)}, bf16[128,1024]{1,0:T(8,128)(2,1)}, u32[]{:S(2)}) %copy-start.2) | copy-done | bytes 262168
  19.2 1.0 %collective-permute-done.4.refs_6_ = bf16[128,1024]{1,0:T(8,128)(2,1)S(1)} collective-permute-done((bf16[128,1024]{1,0:T(8,128)(2,1)}, bf16[128,1024]{1,0:T(8,128)(2,1)S(1)}, u32[]{:S(2)}, u32[]{:S(2)}) %collective-permute-start.4) | collective-permute-done | bytes 262176 | tf_op jit(solution)/shard_map/ppermute | solution.py:377
  20.2 0.7 %copy-done.4 = s32[1,128]{1,0:T(1,128)S(1)} copy-done((s32[1,128]{1,0:T(1,128)S(1)}, s32[1,128]{1,0:T(1,128)}, u32[]{:S(2)}) %copy-start.4) | copy-done | bytes 536
  20.9 1.4 %shard_map.76 = (bf16[512,1024]{1,0:T(8,128)(2,1)S(1)}, f32[512,384]{1,0:T(8,128)S(1)}, bf16[384,1024]{1,0:T(8,128)(2,1)S(1)}, f32[9,128]{1,0:T(8,128)S(1)}, f32[9,128]{1,0:T(8,128)S(1)}) custom-call(f32[1]{0:T(128)S(6)} %copy.8.scale, s32[1,128]{1,0:T(1,128)S(1)} %copy-done.4, bf16[128,1024]{1,0:T(8,128)(2,1)S(1)} %get-tuple-element.28.refs_0_, ...), custom_call_target="tpu_custom_call" | custom-call | tf_op jit(solution)/shard_map/pallas_call | solution.py:338
  22.3 2.8 %collective-permute-done.5.refs_0_ = bf16[128,1024]{1,0:T(8,128)(2,1)S(1)} collective-permute-done((bf16[128,1024]{1,0:T(8,128)(2,1)S(1)}, bf16[128,1024]{1,0:T(8,128)(2,1)S(1)}, u32[]{:S(2)}, u32[]{:S(2)}) %collective-permute-start.5) | collective-permute-done | bytes 262176 | tf_op jit(solution)/shard_map/ppermute | solution.py:379
  25.1 0.8 %shard_map.77 = (f32[512,128]{1,0:T(8,128)S(1)}, bf16[128,1024]{1,0:T(8,128)(2,1)S(1)}, f32[8,128]{1,0:T(8,128)S(1)}, f32[16,128]{1,0:T(8,128)S(1)}, f32[1,128]{1,0:T(1,128)S(1)}) custom-call(f32[1]{0:T(128)S(6)} %copy.8.scale, s32[1,128]{1,0:T(1,128)S(1)} %copy-done.4, bf16[512,1024]{1,0:T(8,128)(2,1)S(1)} %get-tuple-element.31.images, ...), custom_call_target="tpu_custom_call" | custom-call | tf_op jit(solution)/shard_map/pallas_call | solution.py:338
  26.0 1.4 %collective-permute-start.10 = (f32[16,128]{1,0:T(8,128)S(1)}, f32[16,128]{1,0:T(8,128)S(1)}, u32[]{:S(2)}, u32[]{:S(2)}) collective-permute-start(f32[16,128]{1,0:T(8,128)S(1)} %get-tuple-element.38.refs_4_), channel_id=1, source_target_pairs={{1,0},{0,1},{3,2},{2,3},{5,4},{4,5},{7,6},{6,7},{9,8},{8,9},{11,10... | collective-permute-start | bytes 24584 | tf_op jit(solution)/shard_map/ppermute | solution.py:32
  27.4 2.3 %collective-permute-done.10.refs_5_ = f32[16,128]{1,0:T(8,128)S(1)} collective-permute-done((f32[16,128]{1,0:T(8,128)S(1)}, f32[16,128]{1,0:T(8,128)S(1)}, u32[]{:S(2)}, u32[]{:S(2)}) %collective-permute-start.10) | collective-permute-done | bytes 8224 | tf_op jit(solution)/shard_map/ppermute | solution.py:32
  29.7 2.2 %collective-permute-start.11 = (f32[32,128]{1,0:T(8,128)S(1)}, f32[32,128]{1,0:T(8,128)S(1)}, u32[]{:S(2)}, u32[]{:S(2)}) collective-permute-start(f32[32,128]{1,0:T(8,128)S(1)} %pad_maximum_fusion.1), channel_id=1, source_target_pairs={{2,0},{3,1},{0,2},{1,3},{6,4},{7,5},{4,6},{5,7},{10,8},{11,9},{8,1... | collective-permute-start | bytes 49160 | tf_op jit(solution)/shard_map/ppermute | solution.py:32
  31.9 0.5 collective-permute-start.9
  32.4 1.9 %collective-permute-done.11.refs_6_ = f32[32,128]{1,0:T(8,128)S(1)} collective-permute-done((f32[32,128]{1,0:T(8,128)S(1)}, f32[32,128]{1,0:T(8,128)S(1)}, u32[]{:S(2)}, u32[]{:S(2)}) %collective-permute-start.11) | collective-permute-done | bytes 16416 | tf_op jit(solution)/shard_map/ppermute | solution.py:32
  34.4 1.3 %collective-permute-done.9.refs_3_ = f32[32,128]{1,0:T(8,128)S(1)} collective-permute-done((f32[32,128]{1,0:T(8,128)S(1)}, f32[32,128]{1,0:T(8,128)S(1)}, u32[]{:S(2)}, u32[]{:S(2)}) %collective-permute-start.9) | collective-permute-done | bytes 16416 | tf_op jit(solution)/shard_map/ppermute | solution.py:32
  35.7 1.1 %shard_map.78 = (f32[1,128]{1,0:T(1,128)S(1)}, f32[1,128]{1,0:T(1,128)S(1)}, f32[1,128]{1,0:T(1,128)S(1)}, bf16[512,512]{1,0:T(8,128)(2,1)S(1)}, bf16[128,1024]{...) custom-call(s32[1,128]{1,0:T(1,128)S(1)} %copy-done.4, ...), custom_call_target="tpu_custom_call" | custom-call | tf_op jit(solution)/shard_map/pallas_call | solution.py:338
  36.9 1.1 %collective-permute-start.15 = (bf16[128,1024]{1,0:T(8,128)(2,1)S(1)}, bf16[128,1024]{1,0:T(8,128)(2,1)S(1)}, u32[]{:S(2)}, u32[]{:S(2)}) collective-permute-start(bf16[128,1024]{1,0:T(8,128)(2,1)S(1)} %get-tuple-element.50), channel_id=1, source_target_pairs={{0,1},{3,2},{1,0},{2,3},{4,5},{7,6},{5,4},{6,7},{8,9},{11,10},{9,8... | collective-permute-start | bytes 786440 | tf_op jit(solution)/shard_map/ppermute | solution.py:389
  37.9 0.7 %shard_map.79 = (f32[128,1024]{1,0:T(8,128)S(1)}, f32[128,1024]{1,0:T(8,128)S(1)}, f32[128,1024]{1,0:T(8,128)S(1)}) custom-call(bf16[512,512]{1,0:T(8,128)(2,1)S(1)} %get-tuple-element.43.weights, bf16[512,1024]{1,0:T(8,128)(2,1)S(1)} %get-tuple-element.31.images, bf16[384,1024]{1,0:T(8,128)(2,1)S(1)} %get-tuple-element.35.txt_first.first, ...), custom_call_target="tpu_custom_call" | custom-call | tf_op jit(solution)/shard_map/pallas_call | solution.py:338
  38.8 0.6 shard_map.80
  39.4 0.4 collective-permute-start.13
  39.8 2.1 %collective-permute-start.18 = (bf16[128,1024]{1,0:T(8,128)(2,1)S(1)}, bf16[128,1024]{1,0:T(8,128)(2,1)S(1)}, u32[]{:S(2)}, u32[]{:S(2)}) collective-permute-start(bf16[128,1024]{1,0:T(8,128)(2,1)S(1)} %get-tuple-element.51), channel_id=1, source_target_pairs={{0,2},{3,1},{1,0},{2,3},{4,6},{7,5},{5,4},{6,7},{8,10},{11,9},{9,8... | collective-permute-start | bytes 786440 | tf_op jit(solution)/shard_map/ppermute | solution.py:391
  42.0 4.2 %collective-permute-done.15.arrived.refs_2_ = bf16[128,1024]{1,0:T(8,128)(2,1)S(1)} collective-permute-done((bf16[128,1024]{1,0:T(8,128)(2,1)S(1)}, bf16[128,1024]{1,0:T(8,128)(2,1)S(1)}, u32[]{:S(2)}, u32[]{:S(2)}) %collective-permute-start.15) | collective-permute-done | bytes 262176 | tf_op jit(solution)/shard_map/ppermute | solution.py:389
  46.2 1.0 %collective-permute-start.16 = (bf16[128,1024]{1,0:T(8,128)(2,1)S(1)}, bf16[128,1024]{1,0:T(8,128)(2,1)S(1)}, u32[]{:S(2)}, u32[]{:S(2)}) collective-permute-start(bf16[128,1024]{1,0:T(8,128)(2,1)S(1)} %shard_map.82), channel_id=1, source_target_pairs={{0,1},{3,2},{1,3},{2,0},{4,5},{7,6},{5,7},{6,4},{8,9},{11,10},{9,1... | collective-permute-start | bytes 786440 | tf_op jit(solution)/shard_map/ppermute | solution.py:398
  47.2 0.5 subtract_bitcast_fusion
  47.7 3.2 %collective-permute-done.13.refs_1_ = bf16[128,1024]{1,0:T(8,128)(2,1)S(1)} collective-permute-done((bf16[128,1024]{1,0:T(8,128)(2,1)S(1)}, bf16[128,1024]{1,0:T(8,128)(2,1)S(1)}, u32[]{:S(2)}, u32[]{:S(2)}) %collective-permute-start.13) | collective-permute-done | bytes 262176 | tf_op jit(solution)/shard_map/ppermute | solution.py:503
  50.9 1.1 %shard_map.81 = f32[128,1024]{1,0:T(8,128)} custom-call(f32[1]{0:T(128)S(6)} %copy.8.scale, bf16[128,1024]{1,0:T(8,128)(2,1)S(1)} %copy-done.3, f32[128,1024]{1,0:T(8,128)S(1)} %get-tuple-element.44.refs_0_, bf16[128,1024]{1,0:T(8,128)(2,1)S(1)} %collective-permute-done.13.refs_1_, bf16[128,1024]{1,0:T(8,128)(2,1)S(1)} %collective-permute-done.14.refs_2_), custom_call_target="tpu_custom_call" | custom-call | tf_op jit(solution)/shard_map/pallas_call | solution.py:338
  52.0 6.8 %collective-permute-done.16.refs_1_ = bf16[128,1024]{1,0:T(8,128)(2,1)S(1)} collective-permute-done((bf16[128,1024]{1,0:T(8,128)(2,1)S(1)}, bf16[128,1024]{1,0:T(8,128)(2,1)S(1)}, u32[]{:S(2)}, u32[]{:S(2)}) %collective-permute-start.16) | collective-permute-done | bytes 262176 | tf_op jit(solution)/shard_map/ppermute | solution.py:398
  58.7 1.1 %shard_map.83 = f32[128,1024]{1,0:T(8,128)} custom-call(f32[1]{0:T(128)S(6)} %copy.8.scale, bf16[128,1024]{1,0:T(8,128)(2,1)S(1)} %copy-done.1, f32[128,1024]{1,0:T(8,128)S(1)} %get-tuple-element.48.refs_0_, bf16[128,1024]{1,0:T(8,128)(2,1)S(1)} %collective-permute-done.16.refs_1_, bf16[128,1024]{1,0:T(8,128)(2,1)S(1)} %collective-permute-done.15.arrived.refs_2_, ...), custom_call_target="tpu_custom_call" | custom-call | tf_op jit(solution)/shard_map/pallas_call | solution.py:338
  (29 shorter events, 0.7 us)
Async XLA Ops:
  0.6 9.9 %collective-permute-start.1 = (bf16[128,1024]{1,0:T(8,128)(2,1)}, bf16[128,1024]{1,0:T(8,128)(2,1)S(1)}, u32[]{:S(2)}, u32[]{:S(2)}) collective-permute-start(bf16[128,1024]{1,0:T(8,128)(2,1)} %raw.2), channel_id=1, source_target_pairs={{0,24},{4,28},{8,0},{12,4},{16,8},{20,12},{24,16},{28,20},{1,25},{... | collective-permute-start | bytes 786440 | tf_op jit(solution)/shard_map/ppermute | solution.py:42
  4.6 9.6 %collective-permute-start.3 = (bf16[128,1024]{1,0:T(8,128)(2,1)}, bf16[128,1024]{1,0:T(8,128)(2,1)S(1)}, u32[]{:S(2)}, u32[]{:S(2)}) collective-permute-start(bf16[128,1024]{1,0:T(8,128)(2,1)} %raw.3), channel_id=1, source_target_pairs={{0,2},{3,1},{1,0},{2,3},{4,6},{7,5},{5,4},{6,7},{8,10},{11,9},{9,8... | collective-permute-start | bytes 786440 | tf_op jit(solution)/shard_map/ppermute | solution.py:376
  7.2 12.0 %collective-permute-start = (bf16[128,1024]{1,0:T(8,128)(2,1)}, bf16[128,1024]{1,0:T(8,128)(2,1)S(1)}, u32[]{:S(2)}, u32[]{:S(2)}) collective-permute-start(bf16[128,1024]{1,0:T(8,128)(2,1)} %raw.2), channel_id=1, source_target_pairs={{4,0},{16,4},{12,8},{24,12},{20,16},{0,20},{28,24},{8,28},{5,1},{1... | collective-permute-start | bytes 786440 | tf_op jit(solution)/shard_map/ppermute | solution.py:403
  7.2 13.0 %collective-permute-start.4 = (bf16[128,1024]{1,0:T(8,128)(2,1)}, bf16[128,1024]{1,0:T(8,128)(2,1)S(1)}, u32[]{:S(2)}, u32[]{:S(2)}) collective-permute-start(bf16[128,1024]{1,0:T(8,128)(2,1)} %raw.3), channel_id=1, source_target_pairs={{0,1},{3,2},{1,3},{2,0},{4,5},{7,6},{5,7},{6,4},{8,9},{11,10},{9,1... | collective-permute-start | bytes 786440 | tf_op jit(solution)/shard_map/ppermute | solution.py:377
  10.5 9.7 %collective-permute-start.2 = (bf16[128,1024]{1,0:T(8,128)(2,1)S(1)}, bf16[128,1024]{1,0:T(8,128)(2,1)S(1)}, u32[]{:S(2)}, u32[]{:S(2)}) collective-permute-start(bf16[128,1024]{1,0:T(8,128)(2,1)S(1)} %collective-permute-done.1.refs_2_), channel_id=1, source_target_pairs={{0,4},{4,0},{8,12},{12,8},{16,20},{20,16},{24,28},{28,24},{1,5},{5... | collective-permute-start | bytes 786440 | tf_op jit(solution)/shard_map/ppermute | solution.py:57
  10.5 11.8 %collective-permute-start.6 = (bf16[128,1024]{1,0:T(8,128)(2,1)}, bf16[128,1024]{1,0:T(8,128)(2,1)S(1)}, u32[]{:S(2)}, u32[]{:S(2)}) collective-permute-start(bf16[128,1024]{1,0:T(8,128)(2,1)} %raw.3), channel_id=1, source_target_pairs={{0,4},{1,2},{2,1},{3,7},{4,0},{5,6},{6,5},{7,3},{8,12},{9,10},{10,... | collective-permute-start | bytes 786440 | tf_op jit(solution)/shard_map/ppermute | solution.py:52
  14.2 10.9 %collective-permute-start.5 = (bf16[128,1024]{1,0:T(8,128)(2,1)S(1)}, bf16[128,1024]{1,0:T(8,128)(2,1)S(1)}, u32[]{:S(2)}, u32[]{:S(2)}) collective-permute-start(bf16[128,1024]{1,0:T(8,128)(2,1)S(1)} %collective-permute-done.3.refs_5_), channel_id=1, source_target_pairs={{1,0},{2,3},{0,1},{3,2},{5,4},{6,7},{4,5},{7,6},{9,8},{10,11},{8,9... | collective-permute-start | bytes 786440 | tf_op jit(solution)/shard_map/ppermute | solution.py:379
  16.5 0.9 %copy-start = (bf16[128,1024]{1,0:T(8,128)(2,1)S(1)}, bf16[128,1024]{1,0:T(8,128)(2,1)}, u32[]{:S(2)}) copy-start(bf16[128,1024]{1,0:T(8,128)(2,1)} %raw.3) | copy-start | bytes 786436
  17.4 0.9 %copy-start.2 = (bf16[128,1024]{1,0:T(8,128)(2,1)S(1)}, bf16[128,1024]{1,0:T(8,128)(2,1)}, u32[]{:S(2)}) copy-start(bf16[128,1024]{1,0:T(8,128)(2,1)} %raw.2) | copy-start | bytes 786436
  20.2 0.7 %copy-start.4 = (s32[1,128]{1,0:T(1,128)S(1)}, s32[1,128]{1,0:T(1,128)}, u32[]{:S(2)}) copy-start(s32[1,128]{1,0:T(1,128)} %positive.5) | copy-start | bytes 1540
  25.9 1.5 %collective-permute-start.7 = (f32[8,128]{1,0:T(8,128)S(1)}, f32[8,128]{1,0:T(8,128)S(1)}, u32[]{:S(2)}, u32[]{:S(2)}) collective-permute-start(f32[8,128]{1,0:T(8,128)S(1)} %get-tuple-element.37.refs_0_), channel_id=1, source_target_pairs={{4,0},{0,4},{12,8},{8,12},{20,16},{16,20},{28,24},{24,28},{5,1},{1... | collective-permute-start | bytes 12296 | tf_op jit(solution)/shard_map/ppermute | solution.py:32
  26.0 3.7 %collective-permute-start.10 = (f32[16,128]{1,0:T(8,128)S(1)}, f32[16,128]{1,0:T(8,128)S(1)}, u32[]{:S(2)}, u32[]{:S(2)}) collective-permute-start(f32[16,128]{1,0:T(8,128)S(1)} %get-tuple-element.38.refs_4_), channel_id=1, source_target_pairs={{1,0},{0,1},{3,2},{2,3},{5,4},{4,5},{7,6},{6,7},{9,8},{8,9},{11,10... | collective-permute-start | bytes 24584 | tf_op jit(solution)/shard_map/ppermute | solution.py:32
  27.4 4.6 %collective-permute-start.8 = (f32[16,128]{1,0:T(8,128)S(1)}, f32[16,128]{1,0:T(8,128)S(1)}, u32[]{:S(2)}, u32[]{:S(2)}) collective-permute-start(f32[16,128]{1,0:T(8,128)S(1)} %pad_maximum_fusion.2), channel_id=1, source_target_pairs={{8,0},{12,4},{0,8},{4,12},{24,16},{28,20},{16,24},{20,28},{9,1},{1... | collective-permute-start | bytes 24584 | tf_op jit(solution)/shard_map/ppermute | solution.py:32
  29.7 4.6 %collective-permute-start.11 = (f32[32,128]{1,0:T(8,128)S(1)}, f32[32,128]{1,0:T(8,128)S(1)}, u32[]{:S(2)}, u32[]{:S(2)}) collective-permute-start(f32[32,128]{1,0:T(8,128)S(1)} %pad_maximum_fusion.1), channel_id=1, source_target_pairs={{2,0},{3,1},{0,2},{1,3},{6,4},{7,5},{4,6},{5,7},{10,8},{11,9},{8,1... | collective-permute-start | bytes 49160 | tf_op jit(solution)/shard_map/ppermute | solution.py:32
  31.9 3.7 %collective-permute-start.9 = (f32[32,128]{1,0:T(8,128)S(1)}, f32[32,128]{1,0:T(8,128)S(1)}, u32[]{:S(2)}, u32[]{:S(2)}) collective-permute-start(f32[32,128]{1,0:T(8,128)S(1)} %pad_maximum_fusion), channel_id=1, source_target_pairs={{16,0},{20,4},{24,8},{28,12},{0,16},{4,20},{8,24},{12,28},{17,1},{... | collective-permute-start | bytes 49160 | tf_op jit(solution)/shard_map/ppermute | solution.py:32
  36.8 2.1 %collective-permute-start.12 = (bf16[128,1024]{1,0:T(8,128)(2,1)S(1)}, bf16[128,1024]{1,0:T(8,128)(2,1)S(1)}, u32[]{:S(2)}, u32[]{:S(2)}) collective-permute-start(bf16[128,1024]{1,0:T(8,128)(2,1)S(1)} %get-tuple-element.45), channel_id=1, source_target_pairs={{0,4},{4,0},{8,12},{12,8},{16,20},{20,16},{24,28},{28,24},{1,5},{5... | collective-permute-start | bytes 786440 | tf_op jit(solution)/shard_map/ppermute | solution.py:57
  36.9 9.2 %collective-permute-start.15 = (bf16[128,1024]{1,0:T(8,128)(2,1)S(1)}, bf16[128,1024]{1,0:T(8,128)(2,1)S(1)}, u32[]{:S(2)}, u32[]{:S(2)}) collective-permute-start(bf16[128,1024]{1,0:T(8,128)(2,1)S(1)} %get-tuple-element.50), channel_id=1, source_target_pairs={{0,1},{3,2},{1,0},{2,3},{4,5},{7,6},{5,4},{6,7},{8,9},{11,10},{9,8... | collective-permute-start | bytes 786440 | tf_op jit(solution)/shard_map/ppermute | solution.py:389
  38.6 13.4 %collective-permute-start.17 = (bf16[128,1024]{1,0:T(8,128)(2,1)S(1)}, bf16[128,1024]{1,0:T(8,128)(2,1)S(1)}, u32[]{:S(2)}, u32[]{:S(2)}) collective-permute-start(bf16[128,1024]{1,0:T(8,128)(2,1)S(1)} %get-tuple-element.51), channel_id=1, source_target_pairs={{0,4},{1,2},{2,1},{3,7},{4,0},{5,6},{6,5},{7,3},{8,12},{9,10},{10,... | collective-permute-start | bytes 786440 | tf_op jit(solution)/shard_map/ppermute | solution.py:52
  39.4 11.5 %collective-permute-start.13 = (bf16[128,1024]{1,0:T(8,128)(2,1)S(1)}, bf16[128,1024]{1,0:T(8,128)(2,1)S(1)}, u32[]{:S(2)}, u32[]{:S(2)}) collective-permute-start(bf16[128,1024]{1,0:T(8,128)(2,1)S(1)} %get-tuple-element.46), channel_id=1, source_target_pairs={{0,4},{4,16},{8,12},{12,24},{16,20},{20,0},{24,28},{28,8},{1,5},{5... | collective-permute-start | bytes 786440 | tf_op jit(solution)/shard_map/ppermute | solution.py:503
  39.8 11.1 %collective-permute-start.14 = (bf16[128,1024]{1,0:T(8,128)(2,1)S(1)}, bf16[128,1024]{1,0:T(8,128)(2,1)S(1)}, u32[]{:S(2)}, u32[]{:S(2)}) collective-permute-start(bf16[128,1024]{1,0:T(8,128)(2,1)S(1)} %get-tuple-element.47), channel_id=1, source_target_pairs={{0,8},{4,12},{8,16},{12,20},{16,24},{20,28},{24,0},{28,4},{1,9},{5... | collective-permute-start | bytes 786440 | tf_op jit(solution)/shard_map/ppermute | solution.py:42
  39.8 12.1 %collective-permute-start.18 = (bf16[128,1024]{1,0:T(8,128)(2,1)S(1)}, bf16[128,1024]{1,0:T(8,128)(2,1)S(1)}, u32[]{:S(2)}, u32[]{:S(2)}) collective-permute-start(bf16[128,1024]{1,0:T(8,128)(2,1)S(1)} %get-tuple-element.51), channel_id=1, source_target_pairs={{0,2},{3,1},{1,0},{2,3},{4,6},{7,5},{5,4},{6,7},{8,10},{11,9},{9,8... | collective-permute-start | bytes 786440 | tf_op jit(solution)/shard_map/ppermute | solution.py:391
  46.1 4.8 %copy-start.3 = (bf16[128,1024]{1,0:T(8,128)(2,1)S(1)}, bf16[128,1024]{1,0:T(8,128)(2,1)}, u32[]{:S(2)}) copy-start(bf16[128,1024]{1,0:T(8,128)(2,1)} %raw.2) | copy-start | bytes 786436
  46.2 12.6 %collective-permute-start.16 = (bf16[128,1024]{1,0:T(8,128)(2,1)S(1)}, bf16[128,1024]{1,0:T(8,128)(2,1)S(1)}, u32[]{:S(2)}, u32[]{:S(2)}) collective-permute-start(bf16[128,1024]{1,0:T(8,128)(2,1)S(1)} %shard_map.82), channel_id=1, source_target_pairs={{0,1},{3,2},{1,3},{2,0},{4,5},{7,6},{5,7},{6,4},{8,9},{11,10},{9,1... | collective-permute-start | bytes 786440 | tf_op jit(solution)/shard_map/ppermute | solution.py:398
  50.9 7.8 %copy-start.1 = (bf16[128,1024]{1,0:T(8,128)(2,1)S(1)}, bf16[128,1024]{1,0:T(8,128)(2,1)}, u32[]{:S(2)}) copy-start(bf16[128,1024]{1,0:T(8,128)(2,1)} %raw.3) | copy-start | bytes 786436

commit v8 on v7

--- a/solution.py
+++ b/solution.py
@@ -132,7 +132,10 @@
     wanted = to_column(positive.astype(F32), eye)
     lane = lax.broadcasted_iota(jnp.int32, (rows, rows), 1)
     quarter = lax.axis_index("rep")
-    return [wanted == (lane + place(quarter, s, parts) * rows).astype(F32) for s in range(parts)]
+    return [
+        wanted == (lane + place(quarter, slot_at_position(s, parts), parts) * rows).astype(F32)
+        for s in range(parts)
+    ]
 
 
 def scores_kernel(parts, slots, factor, positive, images, scores, txt_out, row_out, col_out):
@@ -157,7 +160,8 @@
         peak = jnp.max(tile, axis=0, keepdims=True)
         col_peaks.append(peak)
         col_sums.append(jnp.sum(jnp.exp(tile - peak), axis=0, keepdims=True))
-        match = wanted == (lane + place(quarter, s, parts) * rows).astype(F32)
+        column = lane + place(quarter, slot_at_position(s, parts), parts) * rows
+        match = wanted == column.astype(F32)
         chosen = jnp.where(match, tile[:rows, :], 0.0)
         picked.append(jnp.sum(chosen, axis=0, keepdims=True))
         found = found + jnp.sum(chosen, axis=1, keepdims=True)
@@ -176,8 +180,8 @@
     store_units(second, img_out, 2 * rows)
     store_units(other, img_out, (STEPS - step) * rows)
     txt_out[:rows, :] = own_text[...]
-    for slot, text in zip(near_slots(parts), texts):
-        store_units(text, txt_out, slot * rows)
+    for n, text in enumerate(texts, 1):
+        store_units(text, txt_out, n * rows)
     slots = range(parts - 1)
     scores_kernel(parts, slots, scale[0], positive[...], img_out, scores, txt_out, *stats)
 
@@ -202,8 +206,9 @@
     row_pos[...] = row_first[2 * STEPS :, :] + row_last[2 * STEPS :, :]
     tables = []
     for which in range(3):
-        tables += [col_first[which * (parts - 1) : (which + 1) * (parts - 1), :]]
-        tables += [col_last[which : which + 1, :]]
+        at = which * (parts - 1)
+        near = [col_first[at + n : at + n + 1, :] for n in range(parts - 1)]
+        tables += reordered([*near, col_last[which : which + 1, :]], parts)
     blank = jnp.zeros((col_stats.shape[0] - 3 * parts, col_last.shape[1]), F32)
     col_stats[...] = jnp.concatenate(tables + [blank] * (blank.shape[0] > 0), axis=0)
 
@@ -265,7 +270,9 @@
             col_out[...] = lse
             col_picked[...] = sum(c[2 * parts + q : 2 * parts + q + 1, :] for c, q in at)
         col_lse.append(lse)
-    for s in range(parts):
+    col_lse = reordered(col_lse, parts)
+
+    def weigh(s):
         source, base = (first, s * rows) if s < parts - 1 else (last, 0)
         for k in range(STEPS):
             tile = source[k * rows : (k + 1) * rows, base : base + rows]
@@ -273,18 +280,31 @@
             if k == 0:
                 weight = weight - onehot[s].astype(F32)
             weights[k * rows : (k + 1) * rows, s * rows : (s + 1) * rows] = weight.astype(BF16)
-    for slot, out in zip(sent_slots(parts)[0], narrow):
-        text_part(weights, images, slot, out)
+
+    if is_line(parts):
+        early, late = narrow
+        weigh(2)
+        weigh(3)
+        end = at_end(parts)
+        part = text_parts(weights, images, 2, 4, rows)
+        one, other_one = part[:rows], part[rows:]
+        early[...] = jnp.where(end, other_one, one).astype(BF16)
+        late[...] = jnp.where(end, one, other_one).astype(BF16)
+        weigh(0)
+        weigh(1)
+    else:
+        for s in range(parts):
+            weigh(s)
+        for s, out in enumerate(narrow, 1):
+            out[...] = text_parts(weights, images, s, s + 1, rows).astype(BF16)
     other[...] = image_part(weights, txt_first, txt_last, STEPS - direct_step(), rows).astype(BF16)
 
 
-def text_part(weights, images, slot, out):
-    rows = out.shape[0]
-    strip = pl.ds(pl.multiple_of(slot * rows, rows), rows)
-    part = lax.dot_general(
+def text_parts(weights, images, begin, stop, rows):
+    strip = slice(begin * rows, stop * rows)
+    return lax.dot_general(
         weights[:, strip], images[...], (((0,), (0,)), ((), ())), preferred_element_type=F32
     )
-    out[...] = part.astype(out.dtype)
 
 
 def image_part(weights, first, last, k, rows):
@@ -301,9 +321,11 @@
     direct[...] = image_part(weights, first, last, direct_step(), rows).astype(BF16)
 
 
-def rest_kernel(parts, weights, images, first, last, own, *kept):
-    for slot, out in reversed(list(zip(sent_slots(parts)[1], kept))):
-        text_part(weights, images, slot, out)
+def rest_kernel(weights, images, first, last, own, *kept):
+    rows = own.shape[0]
+    part = text_parts(weights, images, 0, len(kept), rows)
+    for n, out in enumerate(kept):
+        out[...] = part[n * rows : (n + 1) * rows]
     own[...] = image_part(weights, first, last, 0, own.shape[0])
 
 
@@ -354,18 +376,17 @@
     return (quarter == 0) | (quarter == parts - 1)
 
 
-def near_slots(parts):
+def slot_at_position(position, parts):
+    if is_line(parts) and position in (1, 2):
+        return jnp.where(at_end(parts), position, 3 - position)
+    return position
+
+
+def reordered(rows, parts):
     if not is_line(parts):
-        return list(range(1, parts - 1))
-    first = jnp.where(at_end(parts), 1, 2)
-    return [first, 3 - first]
-
-
-def sent_slots(parts):
-    if not is_line(parts):
-        return list(range(1, parts)), [0]
+        return rows
     end = at_end(parts)
-    return [jnp.where(end, 3, 1), jnp.where(end, 2, 3)], [0, jnp.where(end, 1, 2)]
+    return [rows[0], jnp.where(end, rows[1], rows[2]), jnp.where(end, rows[2], rows[1]), rows[3]]
 
 
 def gathered_texts(text):
@@ -466,13 +487,13 @@
         sent = jnp.concatenate(col_tables, axis=0)[: count * height]
         col_tables.append(fetched(sent, "rep", 2**n))
     row_tables = known_row_tables(row_stats)
-    narrow_slots, kept_slots = sent_slots(parts)
+    n_kept = 2 if is_line(parts) else 1
     row_lse, col_lse, col_pos, weights, other, *narrow = call(
         functools.partial(weights_kernel, parts, len(row_tables)),
         (
             *[shape((1, rows), F32)] * 3,
             shape((STEPS * rows, parts * rows), BF16),
-            *[shape((rows, width), BF16) for _ in range(1 + len(narrow_slots))],
+            *[shape((rows, width), BF16) for _ in range(1 + parts - n_kept)],
         ),
         [VMEM] * (6 + len(row_tables) + len(col_tables)),
         (
@@ -495,8 +516,8 @@
         (weights, txt_first, txt_last, swapped),
     )
     own, *kept = call(
-        functools.partial(rest_kernel, parts),
-        [shape((rows, width), F32) for _ in range(1 + len(kept_slots))],
+        rest_kernel,
+        [shape((rows, width), F32) for _ in range(1 + n_kept)],
         [VMEM] * 4,
         (weights, img_tiles, txt_first, txt_last),
     )

time: 60.1 us -> 60.1 us (level)
  no operation moved by 1% of the time
where the time goes in v8:
time: 60.1 us; the launch traced here: 59.9 us
  waiting for transfers between devices  30.1 us (50%)
  starting transfers between devices  18.4 us (31%)
  Pallas kernels  6.97 us (12%)
  local copies, waits for them, and re-layouts  2.56 us (4%)
  between operations  1.37 us (2%)
    pallas_call x9, Pallas kernels, call(): pl.pallas_call(kernel, out_shape=outs, in_specs=[pl.BlockSpec(memory_spac...  6.97 us
    ppermute x1, waiting for transfers between devices, returned_texts(): joined = lax.ppermute(joined, 'rep', [(0, 1), (3, 2), (1, 3), (2, 0)])  6.77 us
    ppermute x5, waiting for transfers between devices, fetched(): lax.ppermute(array, axis, [(place(i, slot, count), i) for i in range(coun...  5.57 us
    ppermute x1, waiting for transfers between devices, returned_texts(): one = lax.ppermute(early, 'rep', [(0, 1), (3, 2), (1, 0), (2, 3)])  4.17 us
    ppermute x5, starting transfers between devices, fetched(): lax.ppermute(array, axis, [(place(i, slot, count), i) for i in range(coun...  4.16 us
    ppermute x2, starting transfers between devices, passed_along(): lax.ppermute(array, axis, [(i, (i + by) % count) for i in range(count)])  3.98 us
    ppermute x2, waiting for transfers between devices, passed_along(): lax.ppermute(array, axis, [(i, (i + by) % count) for i in range(count)])  3.33 us
    ppermute x1, waiting for transfers between devices, gathered_texts(): one = lax.ppermute(text, 'rep', [(0, 2), (3, 1), (1, 0), (2, 3)])  3.21 us
  transfers between devices with their start and end apart: 19, of which 10 were waited for; matrix products, arithmetic and copies ran while one was open for 1% of the time, Pallas kernels for 7%

profile of v8, /device:TPU:0, one launch (start us, length us, event | category | flops | bytes accessed | tf_op | source)
XLA Modules:
  0.0 59.9 jit_solution(9469251183723058409)
XLA Ops:
  0.6 4.0 %collective-permute-start.1 = (bf16[128,1024]{1,0:T(8,128)(2,1)}, bf16[128,1024]{1,0:T(8,128)(2,1)S(1)}, u32[]{:S(2)}, u32[]{:S(2)}) collective-permute-start(bf16[128,1024]{1,0:T(8,128)(2,1)} %raw.2), channel_id=1, source_target_pairs={{0,24},{4,28},{8,0},{12,4},{16,8},{20,12},{24,16},{28,20},{1,25},{... | collective-permute-start | bytes 786440 | tf_op jit(solution)/shard_map/ppermute | solution.py:42
  4.6 2.6 %collective-permute-start.3 = (bf16[128,1024]{1,0:T(8,128)(2,1)}, bf16[128,1024]{1,0:T(8,128)(2,1)S(1)}, u32[]{:S(2)}, u32[]{:S(2)}) collective-permute-start(bf16[128,1024]{1,0:T(8,128)(2,1)} %raw.3), channel_id=1, source_target_pairs={{0,2},{3,1},{1,0},{2,3},{4,6},{7,5},{5,4},{6,7},{8,10},{11,9},{9,8... | collective-permute-start | bytes 786440 | tf_op jit(solution)/shard_map/ppermute | solution.py:397
  7.2 3.3 %collective-permute-done.1.refs_2_ = bf16[128,1024]{1,0:T(8,128)(2,1)S(1)} collective-permute-done((bf16[128,1024]{1,0:T(8,128)(2,1)}, bf16[128,1024]{1,0:T(8,128)(2,1)S(1)}, u32[]{:S(2)}, u32[]{:S(2)}) %collective-permute-start.1) | collective-permute-done | bytes 262176 | tf_op jit(solution)/shard_map/ppermute | solution.py:42
  10.5 0.5 collective-permute-start.6
  11.0 3.2 %collective-permute-done.3.refs_5_ = bf16[128,1024]{1,0:T(8,128)(2,1)S(1)} collective-permute-done((bf16[128,1024]{1,0:T(8,128)(2,1)}, bf16[128,1024]{1,0:T(8,128)(2,1)S(1)}, u32[]{:S(2)}, u32[]{:S(2)}) %collective-permute-start.3) | collective-permute-done | bytes 262176 | tf_op jit(solution)/shard_map/ppermute | solution.py:397
  14.2 2.2 %collective-permute-start.5 = (bf16[128,1024]{1,0:T(8,128)(2,1)S(1)}, bf16[128,1024]{1,0:T(8,128)(2,1)S(1)}, u32[]{:S(2)}, u32[]{:S(2)}) collective-permute-start(bf16[128,1024]{1,0:T(8,128)(2,1)S(1)} %collective-permute-done.3.refs_5_), channel_id=1, source_target_pairs={{1,0},{2,3},{0,1},{3,2},{5,4},{6,7},{4,5},{7,6},{9,8},{10,11},{8,9... | collective-permute-start | bytes 786440 | tf_op jit(solution)/shard_map/ppermute | solution.py:400
  16.5 0.9 %copy-done = bf16[128,1024]{1,0:T(8,128)(2,1)S(1)} copy-done((bf16[128,1024]{1,0:T(8,128)(2,1)S(1)}, bf16[128,1024]{1,0:T(8,128)(2,1)}, u32[]{:S(2)}) %copy-start) | copy-done | bytes 262168
  17.4 0.9 %copy-done.2 = bf16[128,1024]{1,0:T(8,128)(2,1)S(1)} copy-done((bf16[128,1024]{1,0:T(8,128)(2,1)S(1)}, bf16[128,1024]{1,0:T(8,128)(2,1)}, u32[]{:S(2)}) %copy-start.2) | copy-done | bytes 262168
  19.2 1.0 %collective-permute-done.4.refs_6_ = bf16[128,1024]{1,0:T(8,128)(2,1)S(1)} collective-permute-done((bf16[128,1024]{1,0:T(8,128)(2,1)}, bf16[128,1024]{1,0:T(8,128)(2,1)S(1)}, u32[]{:S(2)}, u32[]{:S(2)}) %collective-permute-start.4) | collective-permute-done | bytes 262176 | tf_op jit(solution)/shard_map/ppermute | solution.py:398
  20.2 0.7 %copy-done.4 = s32[1,128]{1,0:T(1,128)S(1)} copy-done((s32[1,128]{1,0:T(1,128)S(1)}, s32[1,128]{1,0:T(1,128)}, u32[]{:S(2)}) %copy-start.4) | copy-done | bytes 536
  20.9 1.4 %shard_map.76 = (bf16[512,1024]{1,0:T(8,128)(2,1)S(1)}, f32[512,384]{1,0:T(8,128)S(1)}, bf16[384,1024]{1,0:T(8,128)(2,1)S(1)}, f32[9,128]{1,0:T(8,128)S(1)}, f32[9,128]{1,0:T(8,128)S(1)}) custom-call(f32[1]{0:T(128)S(6)} %copy.8.scale, s32[1,128]{1,0:T(1,128)S(1)} %copy-done.4, bf16[128,1024]{1,0:T(8,128)(2,1)S(1)} %get-tuple-element.28.refs_0_, ...), custom_call_target="tpu_custom_call" | custom-call | tf_op jit(solution)/shard_map/pallas_call | solution.py:360
  22.2 2.9 %collective-permute-done.5.refs_0_ = bf16[128,1024]{1,0:T(8,128)(2,1)S(1)} collective-permute-done((bf16[128,1024]{1,0:T(8,128)(2,1)S(1)}, bf16[128,1024]{1,0:T(8,128)(2,1)S(1)}, u32[]{:S(2)}, u32[]{:S(2)}) %collective-permute-start.5) | collective-permute-done | bytes 262176 | tf_op jit(solution)/shard_map/ppermute | solution.py:400
  25.1 0.8 %shard_map.77 = (f32[512,128]{1,0:T(8,128)S(1)}, bf16[128,1024]{1,0:T(8,128)(2,1)S(1)}, f32[8,128]{1,0:T(8,128)S(1)}, f32[16,128]{1,0:T(8,128)S(1)}, f32[1,128]{1,0:T(1,128)S(1)}) custom-call(f32[1]{0:T(128)S(6)} %copy.8.scale, s32[1,128]{1,0:T(1,128)S(1)} %copy-done.4, bf16[512,1024]{1,0:T(8,128)(2,1)S(1)} %get-tuple-element.31.images, ...), custom_call_target="tpu_custom_call" | custom-call | tf_op jit(solution)/shard_map/pallas_call | solution.py:360
  26.0 1.4 %collective-permute-start.10 = (f32[16,128]{1,0:T(8,128)S(1)}, f32[16,128]{1,0:T(8,128)S(1)}, u32[]{:S(2)}, u32[]{:S(2)}) collective-permute-start(f32[16,128]{1,0:T(8,128)S(1)} %get-tuple-element.38.refs_4_), channel_id=1, source_target_pairs={{1,0},{0,1},{3,2},{2,3},{5,4},{4,5},{7,6},{6,7},{9,8},{8,9},{11,10... | collective-permute-start | bytes 24584 | tf_op jit(solution)/shard_map/ppermute | solution.py:32
  27.4 2.3 %collective-permute-done.10.refs_5_ = f32[16,128]{1,0:T(8,128)S(1)} collective-permute-done((f32[16,128]{1,0:T(8,128)S(1)}, f32[16,128]{1,0:T(8,128)S(1)}, u32[]{:S(2)}, u32[]{:S(2)}) %collective-permute-start.10) | collective-permute-done | bytes 8224 | tf_op jit(solution)/shard_map/ppermute | solution.py:32
  29.7 2.2 %collective-permute-start.11 = (f32[32,128]{1,0:T(8,128)S(1)}, f32[32,128]{1,0:T(8,128)S(1)}, u32[]{:S(2)}, u32[]{:S(2)}) collective-permute-start(f32[32,128]{1,0:T(8,128)S(1)} %pad_maximum_fusion.1), channel_id=1, source_target_pairs={{2,0},{3,1},{0,2},{1,3},{6,4},{7,5},{4,6},{5,7},{10,8},{11,9},{8,1... | collective-permute-start | bytes 49160 | tf_op jit(solution)/shard_map/ppermute | solution.py:32
  31.9 0.5 collective-permute-start.9
  32.4 1.9 %collective-permute-done.11.refs_6_ = f32[32,128]{1,0:T(8,128)S(1)} collective-permute-done((f32[32,128]{1,0:T(8,128)S(1)}, f32[32,128]{1,0:T(8,128)S(1)}, u32[]{:S(2)}, u32[]{:S(2)}) %collective-permute-start.11) | collective-permute-done | bytes 16416 | tf_op jit(solution)/shard_map/ppermute | solution.py:32
  34.4 1.3 %collective-permute-done.9.refs_3_ = f32[32,128]{1,0:T(8,128)S(1)} collective-permute-done((f32[32,128]{1,0:T(8,128)S(1)}, f32[32,128]{1,0:T(8,128)S(1)}, u32[]{:S(2)}, u32[]{:S(2)}) %collective-permute-start.9) | collective-permute-done | bytes 16416 | tf_op jit(solution)/shard_map/ppermute | solution.py:32
  35.7 1.1 %shard_map.78 = (f32[1,128]{1,0:T(1,128)S(1)}, f32[1,128]{1,0:T(1,128)S(1)}, f32[1,128]{1,0:T(1,128)S(1)}, bf16[512,512]{1,0:T(8,128)(2,1)S(1)}, bf16[128,1024]{...) custom-call(s32[1,128]{1,0:T(1,128)S(1)} %copy-done.4, ...), custom_call_target="tpu_custom_call" | custom-call | tf_op jit(solution)/shard_map/pallas_call | solution.py:360
  36.9 1.1 %collective-permute-start.15 = (bf16[128,1024]{1,0:T(8,128)(2,1)S(1)}, bf16[128,1024]{1,0:T(8,128)(2,1)S(1)}, u32[]{:S(2)}, u32[]{:S(2)}) collective-permute-start(bf16[128,1024]{1,0:T(8,128)(2,1)S(1)} %get-tuple-element.50), channel_id=1, source_target_pairs={{0,1},{3,2},{1,0},{2,3},{4,5},{7,6},{5,4},{6,7},{8,9},{11,10},{9,8... | collective-permute-start | bytes 786440 | tf_op jit(solution)/shard_map/ppermute | solution.py:410
  37.9 0.7 %shard_map.79 = (f32[128,1024]{1,0:T(8,128)S(1)}, f32[128,1024]{1,0:T(8,128)S(1)}, f32[128,1024]{1,0:T(8,128)S(1)}) custom-call(bf16[512,512]{1,0:T(8,128)(2,1)S(1)} %get-tuple-element.43.weights, bf16[512,1024]{1,0:T(8,128)(2,1)S(1)} %get-tuple-element.31.images, bf16[384,1024]{1,0:T(8,128)(2,1)S(1)} %get-tuple-element.35.txt_first.first, ...), custom_call_target="tpu_custom_call" | custom-call | tf_op jit(solution)/shard_map/pallas_call | solution.py:360
  38.8 0.6 shard_map.80
  39.4 0.4 collective-permute-start.13
  39.8 2.1 %collective-permute-start.18 = (bf16[128,1024]{1,0:T(8,128)(2,1)S(1)}, bf16[128,1024]{1,0:T(8,128)(2,1)S(1)}, u32[]{:S(2)}, u32[]{:S(2)}) collective-permute-start(bf16[128,1024]{1,0:T(8,128)(2,1)S(1)} %get-tuple-element.51), channel_id=1, source_target_pairs={{0,2},{3,1},{1,0},{2,3},{4,6},{7,5},{5,4},{6,7},{8,10},{11,9},{9,8... | collective-permute-start | bytes 786440 | tf_op jit(solution)/shard_map/ppermute | solution.py:412
  42.0 4.2 %collective-permute-done.15.arrived.refs_2_ = bf16[128,1024]{1,0:T(8,128)(2,1)S(1)} collective-permute-done((bf16[128,1024]{1,0:T(8,128)(2,1)S(1)}, bf16[128,1024]{1,0:T(8,128)(2,1)S(1)}, u32[]{:S(2)}, u32[]{:S(2)}) %collective-permute-start.15) | collective-permute-done | bytes 262176 | tf_op jit(solution)/shard_map/ppermute | solution.py:410
  46.2 1.0 %collective-permute-start.16 = (bf16[128,1024]{1,0:T(8,128)(2,1)S(1)}, bf16[128,1024]{1,0:T(8,128)(2,1)S(1)}, u32[]{:S(2)}, u32[]{:S(2)}) collective-permute-start(bf16[128,1024]{1,0:T(8,128)(2,1)S(1)} %shard_map.82), channel_id=1, source_target_pairs={{0,1},{3,2},{1,3},{2,0},{4,5},{7,6},{5,7},{6,4},{8,9},{11,10},{9,1... | collective-permute-start | bytes 786440 | tf_op jit(solution)/shard_map/ppermute | solution.py:419
  47.2 0.5 subtract_bitcast_fusion
  47.8 3.1 %collective-permute-done.13.refs_1_ = bf16[128,1024]{1,0:T(8,128)(2,1)S(1)} collective-permute-done((bf16[128,1024]{1,0:T(8,128)(2,1)S(1)}, bf16[128,1024]{1,0:T(8,128)(2,1)S(1)}, u32[]{:S(2)}, u32[]{:S(2)}) %collective-permute-start.13) | collective-permute-done | bytes 262176 | tf_op jit(solution)/shard_map/ppermute | solution.py:524
  50.9 1.1 %shard_map.81 = f32[128,1024]{1,0:T(8,128)} custom-call(f32[1]{0:T(128)S(6)} %copy.8.scale, bf16[128,1024]{1,0:T(8,128)(2,1)S(1)} %copy-done.3, f32[128,1024]{1,0:T(8,128)S(1)} %get-tuple-element.44.refs_0_, bf16[128,1024]{1,0:T(8,128)(2,1)S(1)} %collective-permute-done.13.refs_1_, bf16[128,1024]{1,0:T(8,128)(2,1)S(1)} %collective-permute-done.14.refs_2_), custom_call_target="tpu_custom_call" | custom-call | tf_op jit(solution)/shard_map/pallas_call | solution.py:360
  52.0 6.8 %collective-permute-done.16.refs_1_ = bf16[128,1024]{1,0:T(8,128)(2,1)S(1)} collective-permute-done((bf16[128,1024]{1,0:T(8,128)(2,1)S(1)}, bf16[128,1024]{1,0:T(8,128)(2,1)S(1)}, u32[]{:S(2)}, u32[]{:S(2)}) %collective-permute-start.16) | collective-permute-done | bytes 262176 | tf_op jit(solution)/shard_map/ppermute | solution.py:419
  58.8 1.1 %shard_map.83 = f32[128,1024]{1,0:T(8,128)} custom-call(f32[1]{0:T(128)S(6)} %copy.8.scale, bf16[128,1024]{1,0:T(8,128)(2,1)S(1)} %copy-done.1, f32[128,1024]{1,0:T(8,128)S(1)} %get-tuple-element.48.refs_0_, bf16[128,1024]{1,0:T(8,128)(2,1)S(1)} %collective-permute-done.16.refs_1_, bf16[128,1024]{1,0:T(8,128)(2,1)S(1)} %collective-permute-done.15.arrived.refs_2_, ...), custom_call_target="tpu_custom_call" | custom-call | tf_op jit(solution)/shard_map/pallas_call | solution.py:360
  (29 shorter events, 0.7 us)
Async XLA Ops:
  0.6 9.9 %collective-permute-start.1 = (bf16[128,1024]{1,0:T(8,128)(2,1)}, bf16[128,1024]{1,0:T(8,128)(2,1)S(1)}, u32[]{:S(2)}, u32[]{:S(2)}) collective-permute-start(bf16[128,1024]{1,0:T(8,128)(2,1)} %raw.2), channel_id=1, source_target_pairs={{0,24},{4,28},{8,0},{12,4},{16,8},{20,12},{24,16},{28,20},{1,25},{... | collective-permute-start | bytes 786440 | tf_op jit(solution)/shard_map/ppermute | solution.py:42
  4.6 9.6 %collective-permute-start.3 = (bf16[128,1024]{1,0:T(8,128)(2,1)}, bf16[128,1024]{1,0:T(8,128)(2,1)S(1)}, u32[]{:S(2)}, u32[]{:S(2)}) collective-permute-start(bf16[128,1024]{1,0:T(8,128)(2,1)} %raw.3), channel_id=1, source_target_pairs={{0,2},{3,1},{1,0},{2,3},{4,6},{7,5},{5,4},{6,7},{8,10},{11,9},{9,8... | collective-permute-start | bytes 786440 | tf_op jit(solution)/shard_map/ppermute | solution.py:397
  7.2 12.0 %collective-permute-start = (bf16[128,1024]{1,0:T(8,128)(2,1)}, bf16[128,1024]{1,0:T(8,128)(2,1)S(1)}, u32[]{:S(2)}, u32[]{:S(2)}) collective-permute-start(bf16[128,1024]{1,0:T(8,128)(2,1)} %raw.2), channel_id=1, source_target_pairs={{4,0},{16,4},{12,8},{24,12},{20,16},{0,20},{28,24},{8,28},{5,1},{1... | collective-permute-start | bytes 786440 | tf_op jit(solution)/shard_map/ppermute | solution.py:424
  7.2 13.0 %collective-permute-start.4 = (bf16[128,1024]{1,0:T(8,128)(2,1)}, bf16[128,1024]{1,0:T(8,128)(2,1)S(1)}, u32[]{:S(2)}, u32[]{:S(2)}) collective-permute-start(bf16[128,1024]{1,0:T(8,128)(2,1)} %raw.3), channel_id=1, source_target_pairs={{0,1},{3,2},{1,3},{2,0},{4,5},{7,6},{5,7},{6,4},{8,9},{11,10},{9,1... | collective-permute-start | bytes 786440 | tf_op jit(solution)/shard_map/ppermute | solution.py:398
  10.5 9.7 %collective-permute-start.2 = (bf16[128,1024]{1,0:T(8,128)(2,1)S(1)}, bf16[128,1024]{1,0:T(8,128)(2,1)S(1)}, u32[]{:S(2)}, u32[]{:S(2)}) collective-permute-start(bf16[128,1024]{1,0:T(8,128)(2,1)S(1)} %collective-permute-done.1.refs_2_), channel_id=1, source_target_pairs={{0,4},{4,0},{8,12},{12,8},{16,20},{20,16},{24,28},{28,24},{1,5},{5... | collective-permute-start | bytes 786440 | tf_op jit(solution)/shard_map/ppermute | solution.py:57
  10.5 11.7 %collective-permute-start.6 = (bf16[128,1024]{1,0:T(8,128)(2,1)}, bf16[128,1024]{1,0:T(8,128)(2,1)S(1)}, u32[]{:S(2)}, u32[]{:S(2)}) collective-permute-start(bf16[128,1024]{1,0:T(8,128)(2,1)} %raw.3), channel_id=1, source_target_pairs={{0,4},{1,2},{2,1},{3,7},{4,0},{5,6},{6,5},{7,3},{8,12},{9,10},{10,... | collective-permute-start | bytes 786440 | tf_op jit(solution)/shard_map/ppermute | solution.py:52
  14.2 10.9 %collective-permute-start.5 = (bf16[128,1024]{1,0:T(8,128)(2,1)S(1)}, bf16[128,1024]{1,0:T(8,128)(2,1)S(1)}, u32[]{:S(2)}, u32[]{:S(2)}) collective-permute-start(bf16[128,1024]{1,0:T(8,128)(2,1)S(1)} %collective-permute-done.3.refs_5_), channel_id=1, source_target_pairs={{1,0},{2,3},{0,1},{3,2},{5,4},{6,7},{4,5},{7,6},{9,8},{10,11},{8,9... | collective-permute-start | bytes 786440 | tf_op jit(solution)/shard_map/ppermute | solution.py:400
  16.5 0.9 %copy-start = (bf16[128,1024]{1,0:T(8,128)(2,1)S(1)}, bf16[128,1024]{1,0:T(8,128)(2,1)}, u32[]{:S(2)}) copy-start(bf16[128,1024]{1,0:T(8,128)(2,1)} %raw.3) | copy-start | bytes 786436
  17.4 0.9 %copy-start.2 = (bf16[128,1024]{1,0:T(8,128)(2,1)S(1)}, bf16[128,1024]{1,0:T(8,128)(2,1)}, u32[]{:S(2)}) copy-start(bf16[128,1024]{1,0:T(8,128)(2,1)} %raw.2) | copy-start | bytes 786436
  20.2 0.7 %copy-start.4 = (s32[1,128]{1,0:T(1,128)S(1)}, s32[1,128]{1,0:T(1,128)}, u32[]{:S(2)}) copy-start(s32[1,128]{1,0:T(1,128)} %positive.5) | copy-start | bytes 1540
  25.9 1.5 %collective-permute-start.7 = (f32[8,128]{1,0:T(8,128)S(1)}, f32[8,128]{1,0:T(8,128)S(1)}, u32[]{:S(2)}, u32[]{:S(2)}) collective-permute-start(f32[8,128]{1,0:T(8,128)S(1)} %get-tuple-element.37.refs_0_), channel_id=1, source_target_pairs={{4,0},{0,4},{12,8},{8,12},{20,16},{16,20},{28,24},{24,28},{5,1},{1... | collective-permute-start | bytes 12296 | tf_op jit(solution)/shard_map/ppermute | solution.py:32
  26.0 3.7 %collective-permute-start.10 = (f32[16,128]{1,0:T(8,128)S(1)}, f32[16,128]{1,0:T(8,128)S(1)}, u32[]{:S(2)}, u32[]{:S(2)}) collective-permute-start(f32[16,128]{1,0:T(8,128)S(1)} %get-tuple-element.38.refs_4_), channel_id=1, source_target_pairs={{1,0},{0,1},{3,2},{2,3},{5,4},{4,5},{7,6},{6,7},{9,8},{8,9},{11,10... | collective-permute-start | bytes 24584 | tf_op jit(solution)/shard_map/ppermute | solution.py:32
  27.4 4.6 %collective-permute-start.8 = (f32[16,128]{1,0:T(8,128)S(1)}, f32[16,128]{1,0:T(8,128)S(1)}, u32[]{:S(2)}, u32[]{:S(2)}) collective-permute-start(f32[16,128]{1,0:T(8,128)S(1)} %pad_maximum_fusion.2), channel_id=1, source_target_pairs={{8,0},{12,4},{0,8},{4,12},{24,16},{28,20},{16,24},{20,28},{9,1},{1... | collective-permute-start | bytes 24584 | tf_op jit(solution)/shard_map/ppermute | solution.py:32
  29.7 4.6 %collective-permute-start.11 = (f32[32,128]{1,0:T(8,128)S(1)}, f32[32,128]{1,0:T(8,128)S(1)}, u32[]{:S(2)}, u32[]{:S(2)}) collective-permute-start(f32[32,128]{1,0:T(8,128)S(1)} %pad_maximum_fusion.1), channel_id=1, source_target_pairs={{2,0},{3,1},{0,2},{1,3},{6,4},{7,5},{4,6},{5,7},{10,8},{11,9},{8,1... | collective-permute-start | bytes 49160 | tf_op jit(solution)/shard_map/ppermute | solution.py:32
  31.9 3.7 %collective-permute-start.9 = (f32[32,128]{1,0:T(8,128)S(1)}, f32[32,128]{1,0:T(8,128)S(1)}, u32[]{:S(2)}, u32[]{:S(2)}) collective-permute-start(f32[32,128]{1,0:T(8,128)S(1)} %pad_maximum_fusion), channel_id=1, source_target_pairs={{16,0},{20,4},{24,8},{28,12},{0,16},{4,20},{8,24},{12,28},{17,1},{... | collective-permute-start | bytes 49160 | tf_op jit(solution)/shard_map/ppermute | solution.py:32
  36.8 2.0 %collective-permute-start.12 = (bf16[128,1024]{1,0:T(8,128)(2,1)S(1)}, bf16[128,1024]{1,0:T(8,128)(2,1)S(1)}, u32[]{:S(2)}, u32[]{:S(2)}) collective-permute-start(bf16[128,1024]{1,0:T(8,128)(2,1)S(1)} %get-tuple-element.45), channel_id=1, source_target_pairs={{0,4},{4,0},{8,12},{12,8},{16,20},{20,16},{24,28},{28,24},{1,5},{5... | collective-permute-start | bytes 786440 | tf_op jit(solution)/shard_map/ppermute | solution.py:57
  36.9 9.2 %collective-permute-start.15 = (bf16[128,1024]{1,0:T(8,128)(2,1)S(1)}, bf16[128,1024]{1,0:T(8,128)(2,1)S(1)}, u32[]{:S(2)}, u32[]{:S(2)}) collective-permute-start(bf16[128,1024]{1,0:T(8,128)(2,1)S(1)} %get-tuple-element.50), channel_id=1, source_target_pairs={{0,1},{3,2},{1,0},{2,3},{4,5},{7,6},{5,4},{6,7},{8,9},{11,10},{9,8... | collective-permute-start | bytes 786440 | tf_op jit(solution)/shard_map/ppermute | solution.py:410
  38.6 13.4 %collective-permute-start.17 = (bf16[128,1024]{1,0:T(8,128)(2,1)S(1)}, bf16[128,1024]{1,0:T(8,128)(2,1)S(1)}, u32[]{:S(2)}, u32[]{:S(2)}) collective-permute-start(bf16[128,1024]{1,0:T(8,128)(2,1)S(1)} %get-tuple-element.51), channel_id=1, source_target_pairs={{0,4},{1,2},{2,1},{3,7},{4,0},{5,6},{6,5},{7,3},{8,12},{9,10},{10,... | collective-permute-start | bytes 786440 | tf_op jit(solution)/shard_map/ppermute | solution.py:52
  39.4 11.5 %collective-permute-start.13 = (bf16[128,1024]{1,0:T(8,128)(2,1)S(1)}, bf16[128,1024]{1,0:T(8,128)(2,1)S(1)}, u32[]{:S(2)}, u32[]{:S(2)}) collective-permute-start(bf16[128,1024]{1,0:T(8,128)(2,1)S(1)} %get-tuple-element.46), channel_id=1, source_target_pairs={{0,4},{4,16},{8,12},{12,24},{16,20},{20,0},{24,28},{28,8},{1,5},{5... | collective-permute-start | bytes 786440 | tf_op jit(solution)/shard_map/ppermute | solution.py:524
  39.8 11.1 %collective-permute-start.14 = (bf16[128,1024]{1,0:T(8,128)(2,1)S(1)}, bf16[128,1024]{1,0:T(8,128)(2,1)S(1)}, u32[]{:S(2)}, u32[]{:S(2)}) collective-permute-start(bf16[128,1024]{1,0:T(8,128)(2,1)S(1)} %get-tuple-element.47), channel_id=1, source_target_pairs={{0,8},{4,12},{8,16},{12,20},{16,24},{20,28},{24,0},{28,4},{1,9},{5... | collective-permute-start | bytes 786440 | tf_op jit(solution)/shard_map/ppermute | solution.py:42
  39.8 12.1 %collective-permute-start.18 = (bf16[128,1024]{1,0:T(8,128)(2,1)S(1)}, bf16[128,1024]{1,0:T(8,128)(2,1)S(1)}, u32[]{:S(2)}, u32[]{:S(2)}) collective-permute-start(bf16[128,1024]{1,0:T(8,128)(2,1)S(1)} %get-tuple-element.51), channel_id=1, source_target_pairs={{0,2},{3,1},{1,0},{2,3},{4,6},{7,5},{5,4},{6,7},{8,10},{11,9},{9,8... | collective-permute-start | bytes 786440 | tf_op jit(solution)/shard_map/ppermute | solution.py:412
  46.1 4.8 %copy-start.3 = (bf16[128,1024]{1,0:T(8,128)(2,1)S(1)}, bf16[128,1024]{1,0:T(8,128)(2,1)}, u32[]{:S(2)}) copy-start(bf16[128,1024]{1,0:T(8,128)(2,1)} %raw.2) | copy-start | bytes 786436
  46.2 12.6 %collective-permute-start.16 = (bf16[128,1024]{1,0:T(8,128)(2,1)S(1)}, bf16[128,1024]{1,0:T(8,128)(2,1)S(1)}, u32[]{:S(2)}, u32[]{:S(2)}) collective-permute-start(bf16[128,1024]{1,0:T(8,128)(2,1)S(1)} %shard_map.82), channel_id=1, source_target_pairs={{0,1},{3,2},{1,3},{2,0},{4,5},{7,6},{5,7},{6,4},{8,9},{11,10},{9,1... | collective-permute-start | bytes 786440 | tf_op jit(solution)/shard_map/ppermute | solution.py:419
  50.9 7.9 %copy-start.1 = (bf16[128,1024]{1,0:T(8,128)(2,1)S(1)}, bf16[128,1024]{1,0:T(8,128)(2,1)}, u32[]{:S(2)}) copy-start(bf16[128,1024]{1,0:T(8,128)(2,1)} %raw.3) | copy-start | bytes 786436
